TPU v7x, 32 devices: a whole 2x2x4 slice. The times are simulated.
32 devices in a mesh: dp: 16 (over z, y, x), tensor: 2 (over core).
Axes of the slice: x: 2, y: 2, z: 4, core: 2. Of those that a mesh axis runs over, the one named last changes fastest.
Arguments:
- tokens: bfloat16 [4096, 2048], P(('dp', 'tensor')), may hold values from -6 to 6
- cotangent: bfloat16 [4096, 2048], P(('dp', 'tensor')), may hold values from -6 to 6
- expert_ids: int32 [4096, 8], P('dp'), may hold values from 0 to 15, all different within a row; in each aligned block of 256 rows (0 to 255, 256 to 511, ...) at most 144 rows name the same one
- gate_values: float32 [4096, 8], P('dp'), may hold values from 0.1 to 0.4
- w_query: bfloat16 [2048, 4096], P('dp', 'tensor'), may hold values from -0.125 to 0.125
- w_key: bfloat16 [2048, 512], P('dp', 'tensor'), may hold values from -0.125 to 0.125
- w_value: bfloat16 [2048, 512], P('dp', 'tensor'), may hold values from -0.125 to 0.125
- w_out: bfloat16 [4096, 2048], P('tensor', 'dp'), may hold values from -0.75 to 0.75
- w_gate: bfloat16 [16, 2048, 768], P(None, 'dp', 'tensor'), may hold values from -0.125 to 0.125
- w_up: bfloat16 [16, 2048, 768], P(None, 'dp', 'tensor'), may hold values from -0.125 to 0.125
- w_down: bfloat16 [16, 768, 2048], P(None, 'tensor', 'dp'), may hold values from -0.625 to 0.625
- attn_gain: float32 [2048], replicated, may hold values from 0.25 to 1.75
- ffn_gain: float32 [2048], replicated, may hold values from 0.25 to 1.75
- query_gain: float32 [128], replicated, may hold values from 0.25 to 1.75
- key_gain: float32 [128], replicated, may hold values from 0.25 to 1.75
Outputs:
- output: bfloat16 [4096, 2048], P(('dp', 'tensor'))
- grad_tokens: bfloat16 [4096, 2048], P(('dp', 'tensor'))
- grad_w_query: float32 [2048, 4096], P('dp', 'tensor')
- grad_w_key: float32 [2048, 512], P('dp', 'tensor')
- grad_w_value: float32 [2048, 512], P('dp', 'tensor')
- grad_w_out: float32 [4096, 2048], P('tensor', 'dp')
- grad_w_gate: float32 [16, 2048, 768], P(None, 'dp', 'tensor')
- grad_w_up: float32 [16, 2048, 768], P(None, 'dp', 'tensor')
- grad_w_down: float32 [16, 768, 2048], P(None, 'tensor', 'dp')
- grad_attn_gain: float32 [2048], replicated
- grad_ffn_gain: float32 [2048], replicated
- grad_query_gain: float32 [128], replicated
- grad_key_gain: float32 [128], replicated
Inputs may be any that keep to these rules, and one draw needn't show every extreme that they name: `expert_ids`: each row names 8 different experts. Within each sequence (aligned blocks of 256 rows) no expert is named by more than 144 rows, a bound that some block reaches.
All inputs are finite; a program needn't handle non-finite values.
Results may differ from a plain program's by a relative error of at most 0.02.
Values may be sent and summed in bfloat16 or wider, within the bound.
A program may use at most 256 MiB of HBM per device.

v0:
```python
import jax
import jax.numpy as jnp
from jax import lax
from jax.sharding import PartitionSpec as P

epsilon = 1e-06
theta_base = 1000000.0


def rms_inverse(values):
    return lax.rsqrt(jnp.mean(values * values, axis=-1, keepdims=True) + epsilon)


def norm_backward(grad_in, values, inverse, gain_vec):
    scaled = grad_in * gain_vec
    inner_mean = jnp.mean(scaled * values, axis=-1, keepdims=True)
    return inverse * scaled - values * inverse**3 * inner_mean


def rotary_tables(seq_len, head_dim):
    half_dim = head_dim // 2
    frequency = theta_base ** (-jnp.arange(half_dim, dtype=jnp.float32) * 2.0 / head_dim)
    angles = jnp.arange(seq_len, dtype=jnp.float32)[:, None] * frequency[None, :]
    return (jnp.cos(angles)[:, None, :], jnp.sin(angles)[:, None, :])


def rotate(values, cosine, sine_table):
    half_dim = values.shape[-1] // 2
    first_part = values[..., :half_dim]
    second = values[..., half_dim:]
    return jnp.concatenate(
        [first_part * cosine - second * sine_table, second * cosine + first_part * sine_table],
        axis=-1,
    )


def rotate_back(grad_in, cosine, sine_table):
    half_dim = grad_in.shape[-1] // 2
    first_part = grad_in[..., :half_dim]
    second = grad_in[..., half_dim:]
    return jnp.concatenate(
        [first_part * cosine + second * sine_table, second * cosine - first_part * sine_table],
        axis=-1,
    )


def dispatch(expert_ids, gate_values, experts, capacity):
    seq_len = expert_ids.shape[0]
    is_match = expert_ids[:, :, None] == jnp.arange(experts, dtype=jnp.int32)[None, None, :]
    expert_hits = jnp.sum(is_match.astype(jnp.int32), axis=1)
    before = jnp.cumsum(expert_hits, axis=0) - expert_hits
    slot_ids = jnp.sum(jnp.where(is_match, before[:, None, :], 0), axis=2)
    token_index = jnp.broadcast_to(jnp.arange(seq_len, dtype=jnp.int32)[:, None], expert_ids.shape)
    slot_table = (
        jnp.full((experts, capacity), seq_len, jnp.int32).at[expert_ids, slot_ids].set(token_index)
    )
    gate_table = (
        jnp.zeros((experts, capacity), jnp.float32).at[expert_ids, slot_ids].set(gate_values)
    )
    return (slot_table, gate_table)


def head_forward(head_inputs):
    query_vals, key_vals, value_vals = head_inputs
    seq_len = key_vals.shape[0]
    block_rows = min(512, seq_len)
    key_positions = jnp.arange(seq_len)

    def one_block(row_start):
        scores = jnp.einsum("qgd,sd->gqs", query_vals, key_vals, preferred_element_type=jnp.float32)
        causal = (row_start + jnp.arange(block_rows))[:, None] >= key_positions[None, :]
        exp_scores = jnp.where(causal, jnp.exp(scores), 0.0)
        denominator = jnp.sum(exp_scores, axis=-1, keepdims=True)
        softmax_low = (exp_scores / denominator).astype(jnp.bfloat16)
        mixed_out = jnp.einsum(
            "gqs,sd->qgd", softmax_low, value_vals, preferred_element_type=jnp.float32
        )
        return (mixed_out.astype(jnp.bfloat16), jnp.log(denominator[..., 0]))

    block_starts = jnp.arange(seq_len // block_rows, dtype=jnp.int32) * block_rows
    mixed_out, logsum = lax.map(one_block, block_starts)
    return (mixed_out.reshape(seq_len, query_vals.shape[1], query_vals.shape[2]), logsum)


def head_backward(head_inputs):
    query_vals, key_vals, value_vals, logsum, grad_mixed = head_inputs
    seq_len = key_vals.shape[0]
    block_rows = min(512, seq_len)
    key_positions = jnp.arange(seq_len)

    def one_block(state_in, block_in):
        grad_key, grad_value = state_in
        row_start, block_logsum = block_in
        scores = jnp.einsum("qgd,sd->gqs", query_vals, key_vals, preferred_element_type=jnp.float32)
        causal = (row_start + jnp.arange(block_rows))[:, None] >= key_positions[None, :]
        softmax_vals = jnp.where(causal, jnp.exp(scores - block_logsum[..., None]), 0.0)
        grad_probs = jnp.einsum(
            "qgd,sd->gqs", grad_mixed, value_vals, preferred_element_type=jnp.float32
        )
        delta_sum = jnp.sum(grad_probs * softmax_vals, axis=-1, keepdims=True)
        grad_scores = (softmax_vals * (grad_probs - delta_sum)).astype(jnp.bfloat16)
        grad_query = jnp.einsum(
            "gqs,sd->qgd", grad_scores, key_vals, preferred_element_type=jnp.float32
        )
        grad_key = grad_key + jnp.einsum(
            "gqs,qgd->sd", grad_scores, query_vals, preferred_element_type=jnp.float32
        )
        grad_value = grad_value + jnp.einsum(
            "gqs,qgd->sd",
            softmax_vals.astype(jnp.bfloat16),
            grad_mixed,
            preferred_element_type=jnp.float32,
        )
        return ((grad_key, grad_value), grad_query)

    block_starts = jnp.arange(seq_len // block_rows, dtype=jnp.int32) * block_rows
    zero_rows = jnp.zeros(key_vals.shape, jnp.float32)
    (grad_key, grad_value), grad_query = lax.scan(
        one_block, (zero_rows, zero_rows), (block_starts, logsum)
    )
    return (grad_query.reshape(query_vals.shape), grad_key, grad_value)


def gather_rows(values):
    return lax.all_gather(values, "tensor", axis=0, tiled=True)


def scatter_rows(values):
    return lax.psum_scatter(
        values.astype(jnp.bfloat16), "tensor", scatter_dimension=0, tiled=True
    ).astype(jnp.float32)


def widen(stacked, group):
    experts = stacked.shape[0]
    spread = jnp.broadcast_to(stacked[:, None], (experts, group) + stacked.shape[1:])
    return spread.reshape((experts * group,) + stacked.shape[1:])


def per_device(
    tokens,
    cotangent,
    expert_ids,
    gate_values,
    w_query,
    w_key,
    w_value,
    w_out,
    w_gate,
    w_up,
    w_down,
    attn_gain,
    ffn_gain,
    query_gain,
    key_gain,
):
    contract = (((1,), (1,)), ((), ()))
    contract_rows = (((0,), (0,)), ((), ()))
    residual = tokens.astype(jnp.float32)
    model_width = residual.shape[1]
    inverse_one = rms_inverse(residual)
    seq_normed = gather_rows((residual * inverse_one * attn_gain).astype(jnp.bfloat16))
    full_query, full_key, full_value, full_out = (
        lax.all_gather(w_query, "dp", axis=0, tiled=True),
        lax.all_gather(w_key, "dp", axis=0, tiled=True),
        lax.all_gather(w_value, "dp", axis=0, tiled=True),
        lax.all_gather(w_out, "dp", axis=1, tiled=True),
    )
    seq_len = seq_normed.shape[0]
    head_dim = query_gain.shape[0]
    local_heads = full_query.shape[1] // head_dim
    local_kv = full_key.shape[1] // head_dim
    group_size = local_heads // local_kv
    attn_scale = head_dim ** (-0.5)
    cosine, sine_table = rotary_tables(seq_len, head_dim)
    query_raw = jnp.dot(seq_normed, full_query, preferred_element_type=jnp.float32).reshape(
        seq_len, local_heads, head_dim
    )
    key_raw = jnp.dot(seq_normed, full_key, preferred_element_type=jnp.float32).reshape(
        seq_len, local_kv, head_dim
    )
    value_low = (
        jnp.dot(seq_normed, full_value, preferred_element_type=jnp.float32)
        .astype(jnp.bfloat16)
        .reshape(seq_len, local_kv, head_dim)
    )
    query_inverse = rms_inverse(query_raw)
    key_inverse = rms_inverse(key_raw)
    query_low = (
        rotate(query_raw * query_inverse * query_gain, cosine, sine_table) * attn_scale
    ).astype(jnp.bfloat16)
    key_low = rotate(key_raw * key_inverse * key_gain, cosine, sine_table).astype(jnp.bfloat16)
    query_heads = query_low.reshape(seq_len, local_kv, group_size, head_dim).transpose(1, 0, 2, 3)
    key_heads = key_low.transpose(1, 0, 2)
    value_heads = value_low.transpose(1, 0, 2)
    mixed_heads, logsum = lax.map(head_forward, (query_heads, key_heads, value_heads))
    mixed_flat = mixed_heads.transpose(1, 0, 2, 3).reshape(seq_len, local_heads * head_dim)
    hidden = residual + scatter_rows(
        jnp.dot(mixed_flat, full_out, preferred_element_type=jnp.float32)
    )
    inverse_two = rms_inverse(hidden)
    seq_two = gather_rows((hidden * inverse_two * ffn_gain).astype(jnp.bfloat16))
    seq_grad = gather_rows(cotangent)
    experts = w_gate.shape[0]
    dp_rows = w_gate.shape[1]
    hidden_units = w_gate.shape[2]
    dp_count = lax.axis_size("dp")
    group = dp_count // experts
    routed_rows = seq_len * expert_ids.shape[1] * 9 // 8
    capacity = (routed_rows + experts * group - 1) // (experts * group) * group
    slot_table, gate_table = dispatch(expert_ids, gate_values, experts, capacity)
    blank_row = jnp.zeros((1, model_width), jnp.bfloat16)
    padded_in = jnp.concatenate([seq_two, blank_row], axis=0)
    padded_grad = jnp.concatenate([seq_grad, blank_row], axis=0)
    empty_rows = jnp.zeros((seq_len + 1, model_width), jnp.float32)
    piece_rows = capacity // group
    down_rows = jnp.transpose(w_down, (0, 2, 1))
    gate_mine, up_mine, down_mine = (
        lax.all_to_all(widen(w_gate, group), "dp", split_axis=0, concat_axis=1, tiled=True),
        lax.all_to_all(widen(w_up, group), "dp", split_axis=0, concat_axis=1, tiled=True),
        lax.all_to_all(widen(down_rows, group), "dp", split_axis=0, concat_axis=1, tiled=True),
    )
    gate_mine = gate_mine[0]
    up_mine = up_mine[0]
    down_mine = down_mine[0]
    blocks_in = padded_in[slot_table]
    grad_blocks = (padded_grad[slot_table].astype(jnp.float32) * gate_table[:, :, None]).astype(
        jnp.bfloat16
    )
    recv_in, recv_grad = (
        lax.all_to_all(
            blocks_in.reshape(dp_count, piece_rows, model_width),
            "dp",
            split_axis=0,
            concat_axis=0,
            tiled=True,
        ),
        lax.all_to_all(
            grad_blocks.reshape(dp_count, piece_rows, model_width),
            "dp",
            split_axis=0,
            concat_axis=0,
            tiled=True,
        ),
    )
    rows_in = recv_in.reshape(-1, model_width)
    rows_grad = recv_grad.reshape(-1, model_width)
    gate_pre = jnp.dot(rows_in, gate_mine, preferred_element_type=jnp.float32)
    up_pre = jnp.dot(rows_in, up_mine, preferred_element_type=jnp.float32)
    act_low = (jax.nn.silu(gate_pre) * up_pre).astype(jnp.bfloat16)
    expert_out = lax.dot_general(act_low, down_mine, contract, preferred_element_type=jnp.float32)
    grad_act = jnp.dot(rows_grad, down_mine, preferred_element_type=jnp.float32)
    sigmoid_gate = jax.nn.sigmoid(gate_pre)
    grad_gate = (grad_act * up_pre * sigmoid_gate * (1.0 + gate_pre * (1.0 - sigmoid_gate))).astype(
        jnp.bfloat16
    )
    grad_up = (grad_act * gate_pre * sigmoid_gate).astype(jnp.bfloat16)
    grad_input = lax.dot_general(
        grad_gate, gate_mine, contract, preferred_element_type=jnp.float32
    ) + lax.dot_general(grad_up, up_mine, contract, preferred_element_type=jnp.float32)
    back_out, back_grad = (
        lax.all_to_all(
            expert_out.reshape(dp_count, piece_rows, model_width).astype(jnp.bfloat16),
            "dp",
            split_axis=0,
            concat_axis=0,
            tiled=True,
        ).astype(jnp.float32),
        lax.all_to_all(
            grad_input.reshape(dp_count, piece_rows, model_width).astype(jnp.bfloat16),
            "dp",
            split_axis=0,
            concat_axis=0,
            tiled=True,
        ).astype(jnp.float32),
    )
    back_out = back_out.reshape(experts, capacity, model_width)
    back_grad = back_grad.reshape(experts * capacity, model_width)
    flat_slots = slot_table.reshape(-1)
    combined = empty_rows.at[flat_slots].add(
        (back_out * gate_table[:, :, None]).reshape(-1, model_width)
    )
    grad_acc = empty_rows.at[flat_slots].add(back_grad)
    grad_both = jnp.concatenate([grad_gate, grad_up], axis=1)
    grad_cols = jnp.concatenate(
        [
            lax.dot_general(rows_in, grad_both, contract_rows, preferred_element_type=jnp.float32),
            lax.dot_general(rows_grad, act_low, contract_rows, preferred_element_type=jnp.float32),
        ],
        axis=1,
    )
    returned = lax.all_to_all(
        grad_cols[None].astype(jnp.bfloat16), "dp", split_axis=1, concat_axis=0, tiled=True
    ).astype(jnp.float32)
    summed = jnp.sum(returned.reshape(experts, group, dp_rows, 3 * hidden_units), axis=1)
    grad_w_gate = summed[:, :, :hidden_units]
    grad_w_up = summed[:, :, hidden_units : 2 * hidden_units]
    grad_w_down = jnp.transpose(summed[:, :, 2 * hidden_units :], (0, 2, 1))
    output = (hidden + scatter_rows(combined[:seq_len])).astype(jnp.bfloat16)
    grad_two = scatter_rows(grad_acc[:seq_len])
    ffn_gain_part = jnp.sum(grad_two * hidden * inverse_two, axis=0)
    grad_hidden = cotangent.astype(jnp.float32) + norm_backward(
        grad_two, hidden, inverse_two, ffn_gain
    )
    grad_attn = gather_rows(grad_hidden.astype(jnp.bfloat16))
    grad_mixed = lax.dot_general(
        grad_attn, full_out, contract, preferred_element_type=jnp.float32
    ).astype(jnp.bfloat16)
    grad_mixed_heads = grad_mixed.reshape(seq_len, local_kv, group_size, head_dim).transpose(
        1, 0, 2, 3
    )
    grad_query_heads, grad_key_heads, grad_value_heads = lax.map(
        head_backward, (query_heads, key_heads, value_heads, logsum, grad_mixed_heads)
    )
    grad_query_rot = (
        grad_query_heads.transpose(1, 0, 2, 3).reshape(seq_len, local_heads, head_dim) * attn_scale
    )
    grad_query_norm = rotate_back(grad_query_rot, cosine, sine_table)
    query_gain_part = jnp.sum(grad_query_norm * query_raw * query_inverse, axis=(0, 1))
    grad_query_low = (
        norm_backward(grad_query_norm, query_raw, query_inverse, query_gain)
        .astype(jnp.bfloat16)
        .reshape(seq_len, local_heads * head_dim)
    )
    grad_key_norm = rotate_back(grad_key_heads.transpose(1, 0, 2), cosine, sine_table)
    key_gain_part = jnp.sum(grad_key_norm * key_raw * key_inverse, axis=(0, 1))
    grad_key_low = (
        norm_backward(grad_key_norm, key_raw, key_inverse, key_gain)
        .astype(jnp.bfloat16)
        .reshape(seq_len, local_kv * head_dim)
    )
    grad_value_low = (
        grad_value_heads.transpose(1, 0, 2)
        .reshape(seq_len, local_kv * head_dim)
        .astype(jnp.bfloat16)
    )
    grad_proj = jnp.concatenate([grad_query_low, grad_key_low, grad_value_low], axis=1)
    full_proj = jnp.concatenate([full_query, full_key, full_value], axis=1)
    grad_one = scatter_rows(
        lax.dot_general(grad_proj, full_proj, contract, preferred_element_type=jnp.float32)
    )
    first_part = jnp.einsum("sd,sf->df", seq_normed, grad_proj, preferred_element_type=jnp.float32)
    second = jnp.einsum("sd,sf->df", grad_attn, mixed_flat, preferred_element_type=jnp.float32)
    shares = lax.psum_scatter(
        jnp.concatenate([first_part, second], axis=1), "dp", scatter_dimension=0, tiled=True
    )
    query_cols = w_query.shape[1]
    key_cols = w_key.shape[1]
    grad_w_query = shares[:, :query_cols]
    grad_w_key = shares[:, query_cols : query_cols + key_cols]
    grad_w_value = shares[:, query_cols + key_cols : query_cols + 2 * key_cols]
    grad_w_out = jnp.transpose(shares[:, query_cols + 2 * key_cols :])
    attn_gain_part = jnp.sum(grad_one * residual * inverse_one, axis=0)
    grad_tokens = (grad_hidden + norm_backward(grad_one, residual, inverse_one, attn_gain)).astype(
        jnp.bfloat16
    )
    total_gains = lax.psum(
        (attn_gain_part, ffn_gain_part, query_gain_part, key_gain_part), ("dp", "tensor")
    )
    return (
        output,
        grad_tokens,
        grad_w_query,
        grad_w_key,
        grad_w_value,
        grad_w_out,
        grad_w_gate,
        grad_w_up,
        grad_w_down,
        total_gains[0],
        total_gains[1],
        total_gains[2],
        total_gains[3],
    )


def solution(mesh):
    return jax.shard_map(
        per_device,
        mesh=mesh,
        in_specs=(
            P(("dp", "tensor"), None),
            P(("dp", "tensor"), None),
            P("dp", None),
            P("dp", None),
            P("dp", "tensor"),
            P("dp", "tensor"),
            P("dp", "tensor"),
            P("tensor", "dp"),
            P(None, "dp", "tensor"),
            P(None, "dp", "tensor"),
            P(None, "tensor", "dp"),
            P(),
            P(),
            P(),
            P(),
        ),
        out_specs=(
            P(("dp", "tensor"), None),
            P(("dp", "tensor"), None),
            P("dp", "tensor"),
            P("dp", "tensor"),
            P("dp", "tensor"),
            P("tensor", "dp"),
            P(None, "dp", "tensor"),
            P(None, "dp", "tensor"),
            P(None, "tensor", "dp"),
            P(),
            P(),
            P(),
            P(),
        ),
        check_vma=False,
    )
```

profile of v0, /device:TPU:0, one launch (start us, length us, event | category | flops | bytes accessed | tf_op | source)
XLA Modules:
  0.0 2095.2 jit_solution(8136161525801134340)
XLA Ops:
  23.5 64.7 %all-gather.13.cloned.1.call-done = bf16[2048,256]{1,0:T(8,128)(2,1)} async-done(((bf16[128,256]{1,0:T(8,128)(2,1)}), bf16[2048,256]{1,0:T(8,128)(2,1)}) %all-gather.13.cloned.1.call-update) | async-done | bytes 1048592 | tf_op jit(solution)/shard_map/all_gather | solution.py:165
  91.7 53.3 %all-gather.11.cloned.1.call-done = bf16[2048,256]{1,0:T(8,128)(2,1)} async-done(((bf16[128,256]{1,0:T(8,128)(2,1)}), bf16[2048,256]{1,0:T(8,128)(2,1)}) %all-gather.11.cloned.1.call-update) | async-done | bytes 1048592 | tf_op jit(solution)/shard_map/all_gather | solution.py:166
  146.8 112.0 %all-gather.15.cloned.1.call-done = bf16[2048,2048]{1,0:T(8,128)(2,1)} async-done(((bf16[128,2048]{1,0:T(8,128)(2,1)}), bf16[2048,2048]{1,0:T(8,128)(2,1)}) %all-gather.15.cloned.1.call-update) | async-done | bytes 8388624 | tf_op jit(solution)/shard_map/all_gather | solution.py:164
  278.6 145.2 %all-gather.17.cloned.1.call-done = bf16[2048,2048]{1,0:T(8,128)(2,1)} async-done(((bf16[2048,128]{1,0:T(8,128)(2,1)}), bf16[2048,2048]{1,0:T(8,128)(2,1)}) %all-gather.17.cloned.1.call-update) | async-done | bytes 8388624 | tf_op jit(solution)/shard_map/all_gather | solution.py:167
  509.3 142.6 %all-to-all-done = bf16[16,144,2048]{2,1,0:T(8,128)(2,1)} async-done(((bf16[16,144,2048]{2,1,0:T(8,128)(2,1)}), bf16[16,144,2048]{2,1,0:T(8,128)(2,1)}, u32[]{:S(2)}, u32[]{:S(2)}) %all-to-all-start) | async-done | bytes 9437216 | tf_op jit(solution)/shard_map/all_to_all | solution.py:231
  651.8 43.6 %all-to-all-start.5 = ((bf16[16,144,2048]{2,1,0:T(8,128)(2,1)}), bf16[16,144,2048]{2,1,0:T(8,128)(2,1)}, u32[]{:S(2)}, u32[]{:S(2)}) async-start(bf16[16,144,2048]{2,1,0:T(8,128)(2,1)} %fusion.45), calls=%async_computation.7 | async-start | bytes 18874368 | tf_op jit(solution)/shard_map/all_to_all | solution.py:238
  715.7 150.9 %all-to-all-done.5 = bf16[16,144,2048]{2,1,0:T(8,128)(2,1)} async-done(((bf16[16,144,2048]{2,1,0:T(8,128)(2,1)}), bf16[16,144,2048]{2,1,0:T(8,128)(2,1)}, u32[]{:S(2)}, u32[]{:S(2)}) %all-to-all-start.5) | async-done | bytes 9437216 | tf_op jit(solution)/shard_map/all_to_all | solution.py:238
  866.6 13.3 multiply_convert_fusion
  879.9 11.7 fusion.118
  891.6 11.6 add_convert_fusion
  903.2 43.5 %all-to-all-start.6 = ((bf16[16,144,2048]{2,1,0:T(8,128)(2,1)}), bf16[16,144,2048]{2,1,0:T(8,128)(2,1)}, u32[]{:S(2)}, u32[]{:S(2)}) async-start(bf16[16,144,2048]{2,1,0:T(8,128)(2,1)} %bitcast.309), calls=%async_computation.8 | async-start | bytes 18874368 | tf_op jit(solution)/shard_map/all_to_all | solution.py:269
  955.8 159.3 %all-to-all-done.6 = bf16[16,144,2048]{2,1,0:T(8,128)(2,1)} async-done(((bf16[16,144,2048]{2,1,0:T(8,128)(2,1)}), bf16[16,144,2048]{2,1,0:T(8,128)(2,1)}, u32[]{:S(2)}, u32[]{:S(2)}) %all-to-all-start.6) | async-done | bytes 9437216 | tf_op jit(solution)/shard_map/all_to_all | solution.py:269
  1115.1 41.3 %all-to-all-start.4 = ((bf16[16,144,2048]{2,1,0:T(8,128)(2,1)}), bf16[16,144,2048]{2,1,0:T(8,128)(2,1)}, u32[]{:S(2)}, u32[]{:S(2)}) async-start(bf16[16,144,2048]{2,1,0:T(8,128)(2,1)} %convolution_convert_fusion.1), calls=%async_computation.5 | async-start | bytes 18874368 | tf_op jit(solution)/shard_map/all_to_all | solution.py:262
  1156.5 35.5 %scatter_custom_fusion.1 = f32[257,2048]{1,0:T(8,128)} fusion(s32[2304]{0:T(1024)S(1)} %fusion.102, bf16[2304,2048]{1,0:T(8,128)(2,1)} %bitcast.77, f32[]{:T(128)} %constant.68.clone.1), kind=kCustom, calls=%fused_computation.63 | custom fusion | flops 9437184 | bytes 11542532 | tf_op jit(solution)/shard_map/scatter-add | solution.py:283
  1262.8 66.2 %all-to-all-done.4 = bf16[16,144,2048]{2,1,0:T(8,128)(2,1)} async-done(((bf16[16,144,2048]{2,1,0:T(8,128)(2,1)}), bf16[16,144,2048]{2,1,0:T(8,128)(2,1)}, u32[]{:S(2)}, u32[]{:S(2)}) %all-to-all-start.4) | async-done | bytes 9437216 | tf_op jit(solution)/shard_map/all_to_all | solution.py:262
  1329.0 11.4 convert_multiply_fusion.1
  1340.5 34.8 %scatter_custom_fusion = f32[257,2048]{1,0:T(8,128)} fusion(s32[2304]{0:T(1024)} %copy-done.53, f32[2304,2048]{1,0:T(8,128)} %bitcast.318, f32[]{:T(128)} %constant.68.clone.1), kind=kCustom, calls=%fused_computation.129 | custom fusion | flops 4718592 | bytes 2105856 | tf_op jit(solution)/shard_map/scatter-add | solution.py:280
  1396.7 24.7 %pad_maximum_fusion = f32[2048,4608]{1,0:T(8,128)} fusion(f32[2048,2048]{1,0:T(8,128)} %fusion.119, f32[2048,2560]{1,0:T(8,128)} %fusion.95), kind=kLoop, calls=%fused_computation.62 | loop fusion | flops 9437184 | bytes 75497472 | tf_op jit(solution)/shard_map/concatenate | solution.py:345
  1443.4 21.3 %copy.135 = bf16[1,2048,1152]{2,0,1:T(2,128)(2,1)} copy(bf16[1,2048,1152]{1,2,0:T(8,128)(2,1)} %pad_maximum_fusion.1) | data formatting | bytes 9437184 | tf_op jit(solution)/shard_map/concatenate | solution.py:285
  1465.3 102.1 %reduce.14 = bf16[2048,1152]{1,0:T(8,128)(2,1)} reduce(bf16[2048,1,1152]{2,1,0:T(2,128)(2,1)} %bitcast.312, bf16[]{:T(256)} %broadcast.318), dimensions={1}, to_apply=%bitcast.217.reduce_sub_computation | reduce | bytes 9437186
  1578.2 196.7 %all_to_all.56 = bf16[16,2,73728]{2,1,0:T(2,128)(2,1)} all-to-all(bf16[16,2,73728]{2,1,0:T(2,128)(2,1)} %reshape.422), channel_id=1, replica_groups=mesh['dp'=16,'tensor'=2] {'dp'}, dimensions={0} | all-to-all | bytes 9437184 | tf_op jit(solution)/shard_map/all_to_all | solution.py:292
  1774.9 12.9 reshape.423
  1801.6 40.7 %all-reduce.2 = (f32[2048]{0:T(1024)}, f32[2048]{0:T(1024)}, f32[128]{0:T(128)}, f32[128]{0:T(128)}) all-reduce(f32[2048]{0:T(1024)S(1)} %get-tuple-element.229, f32[2048]{0:T(1024)S(1)} %copy-done.49, f32[128]{0:T(128)S(1)} %bitcast_reduce_fusion, f32[128]{0:T(128)S(1)} %bitcast_reduce_fusion.1), channel_id=1, replica_groups=mesh['dp'=16,'tensor'=2] {'dp','tensor'}, use_global_device_ids=true, to_apply=%region_28.29 | all-reduce | flops 4352 | bytes 34816 | tf_op jit(solution)/shard_map/psum | solution.py:357
  1845.4 237.2 %reduce-scatter.14.cloned.1.call-done = f32[128,4608]{1,0:T(8,128)} async-done(((f32[2048,4608]{1,0:T(8,128)}), f32[128,4608]{1,0:T(8,128)}) %reduce-scatter.14.cloned.1.call-update) | async-done | bytes 2359312 | tf_op jit(solution)/shard_map/reduce_scatter | solution.py:344
  (333 shorter events, 315.0 us)
Async XLA Ops:
  7.2 16.4 all-gather.9.cloned.1.call-start
  11.6 76.6 %all-gather.13.cloned.1.call-start = ((), (), s32[]{:S(2)}) async-start(), calls=%async_computation.15 | async-start | bytes 1114112 | tf_op jit(solution)/shard_map/all_gather | solution.py:165
  12.4 132.6 %all-gather.11.cloned.1.call-start = ((), (), s32[]{:S(2)}) async-start(), calls=%async_computation.14 | async-start | bytes 1114112 | tf_op jit(solution)/shard_map/all_gather | solution.py:166
  13.1 245.7 %all-gather.15.cloned.1.call-start = ((), (), s32[]{:S(2)}) async-start(), calls=%async_computation.16 | async-start | bytes 8912896 | tf_op jit(solution)/shard_map/all_gather | solution.py:164
  13.7 410.1 %all-gather.17.cloned.1.call-start = ((), (), s32[]{:S(2)}) async-start(), calls=%async_computation.17 | async-start | bytes 8912896 | tf_op jit(solution)/shard_map/all_gather | solution.py:167
  14.3 257.1 %all-to-all-start.1 = ((bf16[16,128,384]{2,1,0:T(8,128)(2,1)}), bf16[16,128,384]{2,1,0:T(8,128)(2,1)}, u32[]{:S(2)}, u32[]{:S(2)}) async-start(bf16[16,128,384]{2,1,0:T(8,128)(2,1)} %param.27), calls=%async_computation.2 | async-start | bytes 3145728 | tf_op jit(solution)/shard_map/all_to_all | solution.py:219
  23.2 245.4 %copy-start.21 = (f32[256,64]{1,0:T(8,128)}, f32[256,64]{1,0:T(8,128)S(1)}, u32[]{:S(2)}) copy-start(f32[256,64]{1,0:T(8,128)S(1)} %get-tuple-element.307) | copy-start | bytes 196612
  23.3 245.4 %copy-start.23 = (f32[256,64]{1,0:T(8,128)}, f32[256,64]{1,0:T(8,128)S(1)}, u32[]{:S(2)}) copy-start(f32[256,64]{1,0:T(8,128)S(1)} %get-tuple-element.308) | copy-start | bytes 196612
  271.4 159.1 %all-to-all-start.2 = ((bf16[16,128,384]{2,1,0:T(8,128)(2,1)}), bf16[16,128,384]{2,1,0:T(8,128)(2,1)}, u32[]{:S(2)}, u32[]{:S(2)}) async-start(bf16[16,128,384]{2,1,0:T(8,128)(2,1)} %param.28), calls=%async_computation.3 | async-start | bytes 3145728 | tf_op jit(solution)/shard_map/all_to_all | solution.py:220
  275.9 161.5 %reduce-scatter.6.cloned.1.call-start = ((), (), s32[]{:S(2)}) async-start(), calls=%async_computation.18 | async-start | bytes 1572864 | tf_op jit(solution)/shard_map/reduce_scatter | solution.py:129
  430.5 38.1 %all-to-all-start.3 = ((bf16[16,128,384]{1,2,0:T(8,128)(2,1)}), bf16[16,128,384]{1,2,0:T(8,128)(2,1)S(1)}, u32[]{:S(2)}, u32[]{:S(2)}) async-start(bf16[16,128,384]{1,2,0:T(8,128)(2,1)} %bitcast.333), calls=%async_computation.4 | async-start | bytes 3145728 | tf_op jit(solution)/shard_map/all_to_all | solution.py:221
  434.5 16.5 all-gather.19.cloned.1.call-start
  438.6 768.0 %copy-start.56 = (f32[128]{0:T(128)}, f32[128]{0:T(128)S(1)}, u32[]{:S(2)}) copy-start(f32[128]{0:T(128)S(1)} %get-tuple-element.306) | copy-start | bytes 1540
  438.6 768.0 %copy-start.65 = (f32[128]{0:T(128)}, f32[128]{0:T(128)S(1)}, u32[]{:S(2)}) copy-start(f32[128]{0:T(128)S(1)} %get-tuple-element.305) | copy-start | bytes 1540
  468.6 183.2 %all-to-all-start = ((bf16[16,144,2048]{2,1,0:T(8,128)(2,1)}), bf16[16,144,2048]{2,1,0:T(8,128)(2,1)}, u32[]{:S(2)}, u32[]{:S(2)}) async-start(bf16[16,144,2048]{2,1,0:T(8,128)(2,1)} %bitcast.314), calls=%async_computation.1 | async-start | bytes 18874368 | tf_op jit(solution)/shard_map/all_to_all | solution.py:231
  476.6 12.7 all-gather.21.cloned.1.call-start
  651.8 214.8 %all-to-all-start.5 = ((bf16[16,144,2048]{2,1,0:T(8,128)(2,1)}), bf16[16,144,2048]{2,1,0:T(8,128)(2,1)}, u32[]{:S(2)}, u32[]{:S(2)}) async-start(bf16[16,144,2048]{2,1,0:T(8,128)(2,1)} %fusion.45), calls=%async_computation.7 | async-start | bytes 18874368 | tf_op jit(solution)/shard_map/all_to_all | solution.py:238
  903.2 211.9 %all-to-all-start.6 = ((bf16[16,144,2048]{2,1,0:T(8,128)(2,1)}), bf16[16,144,2048]{2,1,0:T(8,128)(2,1)}, u32[]{:S(2)}, u32[]{:S(2)}) async-start(bf16[16,144,2048]{2,1,0:T(8,128)(2,1)} %bitcast.309), calls=%async_computation.8 | async-start | bytes 18874368 | tf_op jit(solution)/shard_map/all_to_all | solution.py:269
  1115.1 213.9 %all-to-all-start.4 = ((bf16[16,144,2048]{2,1,0:T(8,128)(2,1)}), bf16[16,144,2048]{2,1,0:T(8,128)(2,1)}, u32[]{:S(2)}, u32[]{:S(2)}) async-start(bf16[16,144,2048]{2,1,0:T(8,128)(2,1)} %convolution_convert_fusion.1), calls=%async_computation.5 | async-start | bytes 18874368 | tf_op jit(solution)/shard_map/all_to_all | solution.py:262
  1156.4 48.3 %reduce-scatter.10.cloned.1.call-start = ((), (), s32[]{:S(2)}) async-start(), calls=%async_computation.22 | async-start | bytes 1572864 | tf_op jit(solution)/shard_map/reduce_scatter | solution.py:129
  1194.9 24.5 %all-gather.23.cloned.1.call-start = ((), (), s32[]{:S(2)}) async-start(), calls=%async_computation.23 | async-start | bytes 1572864 | tf_op jit(solution)/shard_map/all_gather | solution.py:125
  1209.0 591.2 %reduce-scatter.12.cloned.1.call-start = ((), (), s32[]{:S(2)}) async-start(), calls=%async_computation.24 | async-start | bytes 1572864 | tf_op jit(solution)/shard_map/reduce_scatter | solution.py:129
  1262.6 579.7 %reduce-scatter.8.cloned.1.call-start = ((), (), s32[]{:S(2)}) async-start(), calls=%async_computation.20 | async-start | bytes 1572864 | tf_op jit(solution)/shard_map/reduce_scatter | solution.py:129
  1378.1 704.4 %reduce-scatter.14.cloned.1.call-start = ((), (), s32[]{:S(2)}) async-start(), calls=%async_computation.25 | async-start | bytes 40108032 | tf_op jit(solution)/shard_map/reduce_scatter | solution.py:344
  (72 other events, 1754.8 us)
Sparse Core Ops, SparseCore 0:
  11.8 11.7 all-gather.8
  26.3 61.9 all-gather.12
  91.0 53.9 all-gather.10
  147.6 111.1 all-gather.14
  261.3 162.3 all-gather.16
  430.6 6.6 reduce-scatter.5
  440.8 10.1 all-gather.18
  479.0 10.2 all-gather.20
  1195.0 9.6 reduce-scatter.9
  1209.1 10.2 all-gather.22
  1262.7 9.5 reduce-scatter.11
  1378.2 47.0 reduce-scatter.7
  1431.4 651.1 reduce-scatter.13
where the time goes:
time: 2100 us
  waiting for transfers between devices  1170 us (56%)
  other arithmetic  252 us (12%)
  blocking collectives  237 us (11%)
  starting transfers between devices  154 us (7%)
  matrix products  136 us (6%)
  local copies, waits for them, and re-layouts  132 us (6%)
    reduce_scatter x1, waiting for transfers between devices, per_device(): lax.psum_scatter(jnp.concatenate([first_part, second], axis=1), 'dp', sca...  237 us
    all_to_all x1, blocking collectives, per_device(): lax.all_to_all(grad_cols[None].astype(jnp.bfloat16), 'dp', split_axis=1,...  197 us
    all_to_all x1, waiting for transfers between devices, per_device(): lax.all_to_all(grad_input.reshape(dp_count, piece_rows, model_width).asty...  159 us
    all_to_all x1, waiting for transfers between devices, per_device(): lax.all_to_all(grad_blocks.reshape(dp_count, piece_rows, model_width), 'd...  151 us
    all_gather x1, waiting for transfers between devices, per_device(): lax.all_gather(w_out, 'dp', axis=1, tiled=True)  145 us
    all_to_all x1, waiting for transfers between devices, per_device(): lax.all_to_all(blocks_in.reshape(dp_count, piece_rows, model_width), 'dp'...  143 us
    all_gather x1, waiting for transfers between devices, per_device(): lax.all_gather(w_query, 'dp', axis=0, tiled=True)  112 us
    unnamed x4, other arithmetic  102 us
  transfers between devices with their start and end apart: 20, of which 16 were waited for; matrix products, arithmetic and copies ran while one was open for 22% of the time, Pallas kernels for 0%

commit v1 on v0

--- a/solution.py
+++ b/solution.py
@@ -1,6 +1,10 @@
+import functools
+
 import jax
 import jax.numpy as jnp
 from jax import lax
+from jax.experimental import pallas as pl
+from jax.experimental.pallas import tpu as pltpu
 from jax.sharding import PartitionSpec as P
 
 epsilon = 1e-06
@@ -137,7 +141,647 @@
     return spread.reshape((experts * group,) + stacked.shape[1:])
 
 
-def per_device(
+MESH = pl.DeviceIdType.MESH
+LIMIT = 66_000_000
+
+
+class Place:
+    def __init__(self):
+        self.dp = lax.axis_index("dp")
+        self.core = lax.axis_index("tensor")
+        x, y = self.dp % 2, (self.dp // 2) % 2
+        self.z = self.dp // 4
+        step_x, step_y = 1 - 2 * x, 2 * (1 - 2 * y)
+        self.da = (1 - self.core) * step_x + self.core * step_y
+        self.db = (1 - self.core) * step_y + self.core * step_x
+        self.half = self.z % 2
+        self.pair = 4 * (1 - 2 * self.half)
+        self.far = 8 * (1 - 2 * (self.z // 2))
+
+    def copy(self, src, dst, send_sem, recv_sem, to, core=None):
+        return pltpu.make_async_remote_copy(
+            src_ref=src,
+            dst_ref=dst,
+            send_sem=send_sem,
+            recv_sem=recv_sem,
+            device_id=(to, self.core if core is None else core),
+            device_id_type=MESH,
+        )
+
+    def greet(self, line=False, near=False, chain=False, everyone=False, partner=False):
+        barrier = pltpu.get_barrier_semaphore()
+        count = 0
+
+        def signal(to, core):
+            pl.semaphore_signal(barrier, inc=1, device_id=(to, core), device_id_type=MESH)
+
+        if everyone:
+            for r in range(1, 16):
+                signal((self.dp + r) % 16, self.core)
+            count = count + 15
+        else:
+            if near:
+                signal(self.dp + self.da, self.core)
+                signal(self.dp + self.db, self.core)
+                count = count + 2
+            if chain:
+                signal(self.dp + self.pair, self.core)
+                count = count + 1
+                if near:
+                    signal(self.dp + self.far, self.core)
+                    count = count + 1
+            if line:
+                pl.when(self.z > 0)(lambda: signal(self.dp - 4, self.core))
+                pl.when(self.z < 3)(lambda: signal(self.dp + 4, self.core))
+                count = count + jnp.where(self.z > 0, 1, 0) + jnp.where(self.z < 3, 1, 0)
+        if partner:
+            signal(self.dp, 1 - self.core)
+            count = count + 1
+        pl.semaphore_wait(barrier, count)
+
+
+def add_rows(target, terms, rows, block=16):
+    def body(i, _):
+        at = pl.ds(pl.multiple_of(i * block, block), block)
+        total = terms[0][at, :].astype(jnp.float32)
+        for term in terms[1:]:
+            total = total + term[at, :].astype(jnp.float32)
+        target[at, :] = total.astype(target.dtype)
+        return 0
+
+    lax.fori_loop(0, rows // block, body, 0)
+
+
+def gather_line_kernel(chunks, x_ref, out_ref, own, send_sem, recv_sem, copy_sem):
+    me = Place()
+    rows = x_ref.shape[0] // chunks
+    load = pltpu.make_async_copy(x_ref, own, copy_sem.at[0])
+    load.start()
+    me.greet(line=True, near=True)
+
+    def part(k, source, to, slot):
+        at = pl.ds(k * rows, rows)
+        src = x_ref.at[at] if source is None else out_ref.at[source, at]
+        where = me.dp if source is None else source
+        return me.copy(src, out_ref.at[where, at], send_sem.at[k, slot], recv_sem.at[k, where], to)
+
+    sides = ((-1, me.z > 0, me.z < 3, 4), (1, me.z < 3, me.z > 0, -4))
+
+    def exists(d, side):
+        return (me.z - d >= 0) if side == 0 else (me.z + d <= 3)
+
+    def slot_z(d, side, j):
+        return 4 + ((d - 1) * 2 + side) * 3 + j
+
+    def slot_a(off):
+        return 22 + 3 + off
+
+    def pass_a(k, off):
+        source = me.dp + me.da + 4 * off
+        part(k, source, me.dp + me.da, slot_a(off)).wait_recv()
+        part(k, source, me.dp + me.db, slot_a(off)).start()
+
+    for k in range(chunks):
+        pl.when(me.z < 3)(lambda: part(k, None, me.dp + 4, 0).start())
+        pl.when(me.z > 0)(lambda: part(k, None, me.dp - 4, 1).start())
+        part(k, None, me.dp + me.db, 3).start()
+        part(k, None, me.dp + me.da, 2).start()
+    load.wait()
+    keep = pltpu.make_async_copy(own, out_ref.at[me.dp], copy_sem.at[1])
+    keep.start()
+    for d in range(1, 5):
+        for k in range(chunks):
+            for side, (sign, _, forward, step) in enumerate(sides):
+                if d == 4:
+                    continue
+                source = me.dp + 4 * sign * d
+
+                def arrive():
+                    part(k, source, me.dp, slot_z(d, side, 0)).wait_recv()
+                    pl.when(forward)(lambda: part(k, source, me.dp + step, slot_z(d, side, 0)).start())
+                    part(k, source, me.dp + me.db, slot_z(d, side, 2)).start()
+                    part(k, source, me.dp + me.da, slot_z(d, side, 1)).start()
+
+                pl.when(exists(d, side))(arrive)
+            if d == 1:
+                pass_a(k, 0)
+            else:
+                for side, (sign, *_) in enumerate(sides):
+                    pl.when(exists(d - 1, side))(lambda: pass_a(k, sign * (d - 1)))
+    for z in range(4):
+        for k in range(chunks):
+            for g in (0, 1):
+                part(k, me.dp + me.db + g * me.da + 4 * (z - me.z), me.dp, 0).wait_recv()
+    keep.wait()
+    for k in range(chunks):
+
+        def sent(slot):
+            part(k, me.dp, me.dp, slot).wait_send()
+
+        pl.when(me.z < 3)(lambda: sent(0))
+        pl.when(me.z > 0)(lambda: sent(1))
+        sent(2)
+        sent(3)
+        sent(slot_a(0))
+        for d in range(1, 4):
+            for side, (sign, _, forward, _) in enumerate(sides):
+
+                def finish():
+                    pl.when(forward)(lambda: sent(slot_z(d, side, 0)))
+                    sent(slot_z(d, side, 1))
+                    sent(slot_z(d, side, 2))
+                    sent(slot_a(sign * d))
+
+                pl.when(exists(d, side))(finish)
+
+
+def gather_line(x, cid, chunks=2):
+    rows, columns = x.shape
+    return pl.pallas_call(
+        functools.partial(gather_line_kernel, chunks),
+        out_shape=jax.ShapeDtypeStruct((16, rows, columns), x.dtype),
+        in_specs=[pl.BlockSpec(memory_space=pl.ANY)],
+        out_specs=pl.BlockSpec(memory_space=pl.ANY),
+        scratch_shapes=[
+            pltpu.VMEM((rows, columns), x.dtype),
+            pltpu.SemaphoreType.DMA((chunks, 29)),
+            pltpu.SemaphoreType.DMA((chunks, 16)),
+            pltpu.SemaphoreType.DMA((2,)),
+        ],
+        compiler_params=pltpu.CompilerParams(collective_id=cid, has_side_effects=True),
+        name="gather_line",
+    )(x)
+
+
+def gather_pairs_kernel(x_ref, out_ref, own, send_sem, recv_sem, copy_sem):
+    me = Place()
+    load = pltpu.make_async_copy(x_ref.at[me.half], own, copy_sem.at[0])
+    load.start()
+    me.greet(near=True, chain=True)
+    mine, other = me.dp, me.dp + me.pair
+
+    def part(src, where, to, slot):
+        return me.copy(src, out_ref.at[where], send_sem.at[slot], recv_sem.at[where], to)
+
+    def relay(where, to, slot):
+        part(out_ref.at[where], where, to, slot).start()
+
+    def arrived(where):
+        part(out_ref.at[where], where, me.dp, 0).wait_recv()
+
+    part(x_ref.at[1 - me.half], mine, other, 0).start()
+    part(x_ref.at[me.half], mine, me.dp + me.far, 1).start()
+    part(x_ref.at[me.half], mine, me.dp + me.db, 2).start()
+    part(x_ref.at[me.half], mine, me.dp + me.da, 3).start()
+    load.wait()
+    keep = pltpu.make_async_copy(own, out_ref.at[mine], copy_sem.at[1])
+    keep.start()
+    arrived(other)
+    relay(other, me.dp + me.far, 4)
+    relay(other, me.dp + me.db, 5)
+    relay(other, me.dp + me.da, 6)
+    arrived(mine + me.da)
+    relay(mine + me.da, me.dp + me.db, 7)
+    arrived(mine + me.far)
+    relay(mine + me.far, me.dp + me.db, 8)
+    relay(mine + me.far, me.dp + me.da, 9)
+    arrived(other + me.da)
+    relay(other + me.da, me.dp + me.db, 10)
+    arrived(other + me.far)
+    relay(other + me.far, me.dp + me.db, 11)
+    relay(other + me.far, me.dp + me.da, 12)
+    arrived(mine + me.far + me.da)
+    relay(mine + me.far + me.da, me.dp + me.db, 13)
+    arrived(other + me.far + me.da)
+    relay(other + me.far + me.da, me.dp + me.db, 14)
+    for base in (mine, other, mine + me.far, other + me.far):
+        arrived(base + me.db)
+        arrived(base + me.da + me.db)
+    keep.wait()
+    for slot in range(15):
+        part(out_ref.at[mine], mine, me.dp, slot).wait_send()
+
+
+def gather_pairs(x, cid):
+    _, rows, columns = x.shape
+    return pl.pallas_call(
+        gather_pairs_kernel,
+        out_shape=jax.ShapeDtypeStruct((16, rows, columns), x.dtype),
+        in_specs=[pl.BlockSpec(memory_space=pl.ANY)],
+        out_specs=pl.BlockSpec(memory_space=pl.ANY),
+        scratch_shapes=[
+            pltpu.VMEM((rows, columns), x.dtype),
+            pltpu.SemaphoreType.DMA((15,)),
+            pltpu.SemaphoreType.DMA((16,)),
+            pltpu.SemaphoreType.DMA((2,)),
+        ],
+        compiler_params=pltpu.CompilerParams(collective_id=cid, has_side_effects=True),
+        name="gather_pairs",
+    )(x)
+
+
+def scatter_pairs_kernel(p_ref, out_ref, from_b, from_a, from_far, send_sem, recv_sem):
+    me = Place()
+    rows = p_ref.shape[1]
+    me.greet(near=True, chain=True)
+    mine, other = me.dp, me.dp + me.pair
+    bases = (mine, other, mine + me.far, other + me.far)
+    order = (2, 3, 1, 0)
+
+    def send_b(g, j, slot):
+        return me.copy(p_ref.at[bases[j] + me.db + g * me.da], from_b.at[g, j], send_sem.at[slot], recv_sem.at[slot], me.dp + me.db)
+
+    def send_a(j):
+        return me.copy(from_b.at[1, j], from_a.at[j], send_sem.at[8 + j], recv_sem.at[8 + j], me.dp + me.da)
+
+    def send_far(j):
+        return me.copy(from_b.at[0, 2 + j], from_far.at[j], send_sem.at[12 + j], recv_sem.at[12 + j], me.dp + me.far)
+
+    def swap():
+        return me.copy(from_b.at[0, 1], out_ref.at[me.half], send_sem.at[14], recv_sem.at[14], other)
+
+    for g in (1, 0):
+        for j in order:
+            send_b(g, j, g * 4 + j).start()
+    for j in order:
+        send_b(1, j, 4 + j).wait_recv()
+        add_rows(from_b.at[1, j], (p_ref.at[bases[j] + me.da], from_b.at[1, j]), rows)
+        send_a(j).start()
+    for j in order:
+        send_b(0, j, j).wait_recv()
+        send_a(j).wait_recv()
+        terms = (p_ref.at[bases[j]], from_b.at[0, j], from_a.at[j])
+        if j >= 2:
+            add_rows(from_b.at[0, j], terms, rows)
+            send_far(j - 2).start()
+        else:
+            send_far(j).wait_recv()
+            add_rows(from_b.at[0, 1] if j else out_ref.at[me.half], terms + (from_far.at[j],), rows)
+            if j:
+                swap().start()
+    swap().wait_send()
+    me.copy(out_ref.at[1 - me.half], out_ref.at[1 - me.half], send_sem.at[14], recv_sem.at[14], other).wait_recv()
+    for g in (0, 1):
+        for j in range(4):
+            send_b(g, j, g * 4 + j).wait_send()
+    for j in range(4):
+        send_a(j).wait_send()
+    send_far(0).wait_send()
+    send_far(1).wait_send()
+
+
+def scatter_pairs(p, cid):
+    _, rows, columns = p.shape
+    return pl.pallas_call(
+        scatter_pairs_kernel,
+        out_shape=jax.ShapeDtypeStruct((2, rows, columns), p.dtype),
+        in_specs=[pl.BlockSpec(memory_space=pltpu.VMEM)],
+        out_specs=pl.BlockSpec(memory_space=pltpu.VMEM),
+        scratch_shapes=[
+            pltpu.VMEM((2, 4, rows, columns), p.dtype),
+            pltpu.VMEM((4, rows, columns), p.dtype),
+            pltpu.VMEM((2, rows, columns), p.dtype),
+            pltpu.SemaphoreType.DMA((15,)),
+            pltpu.SemaphoreType.DMA((15,)),
+        ],
+        compiler_params=pltpu.CompilerParams(collective_id=cid, has_side_effects=True, vmem_limit_bytes=LIMIT),
+        name="scatter_pairs",
+    )(p)
+
+
+def scatter_line_kernel(number, *refs):
+    p_refs, out_refs = refs[:number], refs[number : 2 * number]
+    from_b, from_a, from_z, send_sem, recv_sem = refs[2 * number :]
+    me = Place()
+    rows = p_refs[0].shape[1]
+    me.greet(line=True, near=True)
+
+    def at_z(z):
+        return me.dp + 4 * (z - me.z)
+
+    def send_b(i, g, z):
+        slot = g * 4 + z
+        return me.copy(p_refs[i].at[at_z(z) + me.db + g * me.da], from_b.at[i, g, z], send_sem.at[i, slot], recv_sem.at[i, slot], me.dp + me.db)
+
+    def send_a(i, z):
+        return me.copy(from_b.at[i, 1, z], from_a.at[i, z], send_sem.at[i, 8 + z], recv_sem.at[i, 8 + z], me.dp + me.da)
+
+    def send_z(i, z, up):
+        slot = 12 + 4 * up + z
+        return me.copy(from_b.at[i, 0, z], from_z.at[i, up, z], send_sem.at[i, slot], recv_sem.at[i, slot], me.dp - 4 + 8 * up)
+
+    order = (0, 3, 1, 2)
+    for g in (1, 0):
+        for z in order:
+            for i in range(number):
+                send_b(i, g, z).start()
+    for z in order:
+        for i in range(number):
+            send_b(i, 1, z).wait_recv()
+            add_rows(from_b.at[i, 1, z], (p_refs[i].at[at_z(z) + me.da], from_b.at[i, 1, z]), rows)
+            send_a(i, z).start()
+    for z in order:
+        for i in range(number):
+            send_b(i, 0, z).wait_recv()
+            send_a(i, z).wait_recv()
+            add_rows(from_b.at[i, 0, z], (p_refs[i].at[at_z(z)], from_b.at[i, 0, z], from_a.at[i, z]), rows)
+    low = me.z < 2
+    depth = jnp.where(low, me.z, 3 - me.z)
+    away = jnp.where(low, 1, 0)
+    for t in (3, 2, 1, 0):
+        z = jnp.where(low, t, 3 - t)
+        up = away if t else 1 - away
+        for i in range(number):
+
+            def join():
+                send_z(i, z, up).wait_recv()
+                add_rows(from_b.at[i, 0, z], (from_b.at[i, 0, z], from_z.at[i, up, z]), rows)
+
+            def move():
+                pl.when(depth != 0)(join)
+                send_z(i, z, up).start()
+
+            pl.when((depth < t) if t else (depth == 1))(move)
+    for i in range(number):
+        here = from_b.at[i, 0, me.z]
+
+        def below():
+            send_z(i, me.z, 1).wait_recv()
+
+        def above():
+            send_z(i, me.z, 0).wait_recv()
+
+        pl.when(me.z > 0)(below)
+        pl.when(me.z < 3)(above)
+        pl.when(me.z == 0)(lambda: add_rows(out_refs[i], (here, from_z.at[i, 0, me.z]), rows))
+        pl.when(me.z == 3)(lambda: add_rows(out_refs[i], (here, from_z.at[i, 1, me.z]), rows))
+        pl.when((me.z != 0) & (me.z != 3))(
+            lambda: add_rows(out_refs[i], (here, from_z.at[i, 0, me.z], from_z.at[i, 1, me.z]), rows)
+        )
+    for i in range(number):
+        for z in range(4):
+            send_b(i, 0, z).wait_send()
+            send_b(i, 1, z).wait_send()
+            send_a(i, z).wait_send()
+            pl.when(me.z < z)(lambda: send_z(i, z, 1).wait_send())
+            pl.when(me.z > z)(lambda: send_z(i, z, 0).wait_send())
+
+
+def scatter_line(arrays, cid):
+    number = len(arrays)
+    _, rows, columns = arrays[0].shape
+    dtype = arrays[0].dtype
+    vmem = pl.BlockSpec(memory_space=pltpu.VMEM)
+    return pl.pallas_call(
+        functools.partial(scatter_line_kernel, number),
+        out_shape=[jax.ShapeDtypeStruct((rows, columns), jnp.float32)] * number,
+        in_specs=[vmem] * number,
+        out_specs=[vmem] * number,
+        scratch_shapes=[
+            pltpu.VMEM((number, 2, 4, rows, columns), dtype),
+            pltpu.VMEM((number, 4, rows, columns), dtype),
+            pltpu.VMEM((number, 2, 4, rows, columns), dtype),
+            pltpu.SemaphoreType.DMA((number, 20)),
+            pltpu.SemaphoreType.DMA((number, 20)),
+        ],
+        compiler_params=pltpu.CompilerParams(collective_id=cid, has_side_effects=True, vmem_limit_bytes=LIMIT),
+        name="scatter_line",
+    )(*arrays)
+
+
+def gather_four_kernel(x_ref, out_ref, send_sem, recv_sem):
+    me = Place()
+    me.greet(chain=True, partner=True)
+    mine, theirs = out_ref.at[me.half, me.core], out_ref.at[1 - me.half, me.core]
+    across = me.copy(x_ref, mine, send_sem.at[0], recv_sem.at[0], me.dp + me.pair)
+    across.start()
+    beside = me.copy(x_ref, mine, send_sem.at[1], recv_sem.at[1], me.dp, 1 - me.core)
+    beside.start()
+    mine[...] = x_ref[...]
+    across.wait_recv()
+    relay = me.copy(theirs, theirs, send_sem.at[2], recv_sem.at[2], me.dp, 1 - me.core)
+    relay.start()
+    across.wait_send()
+    beside.wait()
+    relay.wait()
+
+
+def gather_four(x, cid):
+    rows, columns = x.shape
+    vmem = pl.BlockSpec(memory_space=pltpu.VMEM)
+    return pl.pallas_call(
+        gather_four_kernel,
+        out_shape=jax.ShapeDtypeStruct((2, 2, rows, columns), x.dtype),
+        in_specs=[vmem],
+        out_specs=vmem,
+        scratch_shapes=[pltpu.SemaphoreType.DMA((3,)), pltpu.SemaphoreType.DMA((3,))],
+        compiler_params=pltpu.CompilerParams(collective_id=cid, has_side_effects=True),
+        name="gather_four",
+    )(x)
+
+
+def scatter_four_kernel(p_ref, out_ref, from_core, from_pair, send_sem, recv_sem):
+    me = Place()
+    rows = p_ref.shape[2]
+    me.greet(chain=True, partner=True)
+
+    def beside(h, slot):
+        return me.copy(p_ref.at[h, 1 - me.core], from_core.at[slot], send_sem.at[slot], recv_sem.at[slot], me.dp, 1 - me.core)
+
+    first, second = beside(1 - me.half, 0), beside(me.half, 1)
+    first.start()
+    second.start()
+    first.wait_recv()
+    add_rows(from_core.at[0], (p_ref.at[1 - me.half, me.core], from_core.at[0]), rows)
+    across = me.copy(from_core.at[0], from_pair, send_sem.at[2], recv_sem.at[2], me.dp + me.pair)
+    across.start()
+    second.wait_recv()
+    add_rows(from_core.at[1], (p_ref.at[me.half, me.core], from_core.at[1]), rows)
+    across.wait_recv()
+    add_rows(out_ref, (from_core.at[1], from_pair), rows)
+    across.wait_send()
+    first.wait_send()
+    second.wait_send()
+
+
+def scatter_four(p, cid):
+    _, _, rows, columns = p.shape
+    vmem = pl.BlockSpec(memory_space=pltpu.VMEM)
+    return pl.pallas_call(
+        scatter_four_kernel,
+        out_shape=jax.ShapeDtypeStruct((rows, columns), jnp.float32),
+        in_specs=[vmem],
+        out_specs=vmem,
+        scratch_shapes=[
+            pltpu.VMEM((2, rows, columns), p.dtype),
+            pltpu.VMEM((rows, columns), p.dtype),
+            pltpu.SemaphoreType.DMA((3,)),
+            pltpu.SemaphoreType.DMA((3,)),
+        ],
+        compiler_params=pltpu.CompilerParams(collective_id=cid, has_side_effects=True),
+        name="scatter_four",
+    )(p)
+
+
+def expert_weights_kernel(gate_ref, up_ref, down_ref, gate_out, up_out, down_out, send_sem, recv_sem, copy_sem):
+    me = Place()
+    me.greet(everyone=True, partner=True)
+    depth, hidden = gate_ref.shape[1], gate_ref.shape[2]
+    cols = pl.ds(pl.multiple_of(me.core * hidden, 128), hidden)
+
+    def views(s):
+        rows = pl.ds(pl.multiple_of(s * depth, depth), depth)
+        return gate_out.at[rows, cols], up_out.at[rows, cols], down_out.at[cols, rows]
+
+    def locals_of(e):
+        return gate_ref.at[e], up_ref.at[e], down_ref.at[e]
+
+    def send(r):
+        to = (me.dp + r) % 16
+        return [
+            me.copy(src, dst, send_sem.at[0, r, j], recv_sem.at[0, r, j], to)
+            for j, (src, dst) in enumerate(zip(locals_of(to), views(me.dp)))
+        ]
+
+    def receive(r):
+        s = (me.dp + 16 - r) % 16
+        return [me.copy(v, v, send_sem.at[0, r, j], recv_sem.at[0, r, j], me.dp) for j, v in enumerate(views(s))]
+
+    def share(r):
+        s = (me.dp + 16 - r) % 16
+        sources = locals_of(me.dp) if r == 0 else views(s)
+        return [
+            me.copy(src, dst, send_sem.at[1, r, j], recv_sem.at[1, r, j], me.dp, 1 - me.core)
+            for j, (src, dst) in enumerate(zip(sources, views(s)))
+        ]
+
+    for r in range(1, 16):
+        for c in send(r):
+            c.start()
+    keep = [pltpu.make_async_copy(src, dst, copy_sem.at[j]) for j, (src, dst) in enumerate(zip(locals_of(me.dp), views(me.dp)))]
+    for c in keep + share(0):
+        c.start()
+    for r in range(1, 16):
+        for c in receive(r):
+            c.wait_recv()
+        for c in share(r):
+            c.start()
+    for c in keep:
+        c.wait()
+    for r in range(16):
+        other = pl.ds(pl.multiple_of((1 - me.core) * hidden, 128), hidden)
+        s = (me.dp + 16 - r) % 16
+        rows = pl.ds(pl.multiple_of(s * depth, depth), depth)
+        for j, v in enumerate((gate_out.at[rows, other], up_out.at[rows, other], down_out.at[other, rows])):
+            me.copy(v, v, send_sem.at[1, r, j], recv_sem.at[1, r, j], me.dp, 1 - me.core).wait_recv()
+    for r in range(16):
+        if r:
+            for c in send(r):
+                c.wait_send()
+        for c in share(r):
+            c.wait_send()
+
+
+def expert_weights(w_gate, w_up, w_down, cid):
+    _, depth, hidden = w_gate.shape
+    hbm = pl.BlockSpec(memory_space=pl.ANY)
+    wide = jax.ShapeDtypeStruct((16 * depth, 2 * hidden), w_gate.dtype)
+    return pl.pallas_call(
+        expert_weights_kernel,
+        out_shape=[wide, wide, jax.ShapeDtypeStruct((2 * hidden, 16 * depth), w_gate.dtype)],
+        in_specs=[hbm] * 3,
+        out_specs=[hbm] * 3,
+        scratch_shapes=[
+            pltpu.SemaphoreType.DMA((2, 16, 3)),
+            pltpu.SemaphoreType.DMA((2, 16, 3)),
+            pltpu.SemaphoreType.DMA((3,)),
+        ],
+        compiler_params=pltpu.CompilerParams(collective_id=cid, has_side_effects=True),
+        name="expert_weights",
+    )(w_gate, w_up, w_down)
+
+
+def expert_grads_kernel(gate_ref, up_ref, down_ref, gate_out, up_out, down_out, tall, flat, send_sem, recv_sem, copy_sem):
+    me = Place()
+    me.greet(everyone=True, partner=True)
+    depth, hidden = gate_out.shape[1], gate_out.shape[2]
+
+    def views(s, core):
+        cols = pl.ds(pl.multiple_of(core * hidden, 128), hidden)
+        rows = pl.ds(pl.multiple_of(s * depth, depth), depth)
+        return gate_ref.at[rows, cols], up_ref.at[rows, cols], down_ref.at[cols, rows]
+
+    def beside(r):
+        to = (me.dp + r) % 16
+        sources = views(to, 1 - me.core)
+        slots = (tall.at[0, r], tall.at[1, r], flat.at[r])
+        return [
+            me.copy(src, dst, send_sem.at[0, r, j], recv_sem.at[0, r, j], me.dp, 1 - me.core)
+            for j, (src, dst) in enumerate(zip(sources, slots))
+        ]
+
+    def sums(r):
+        return tall.at[0, r], tall.at[1, r], flat.at[r]
+
+    def outs(s):
+        return gate_out.at[s], up_out.at[s], down_out.at[s]
+
+    def send(r):
+        to = (me.dp + r) % 16
+        return [
+            me.copy(src, dst, send_sem.at[1, r, j], recv_sem.at[1, r, j], to)
+            for j, (src, dst) in enumerate(zip(sums(r), outs(me.dp)))
+        ]
+
+    order = tuple(range(1, 16)) + (0,)
+    for r in order:
+        for c in beside(r):
+            c.start()
+    keep = [pltpu.make_async_copy(src, dst, copy_sem.at[j]) for j, (src, dst) in enumerate(zip(sums(0), outs(me.dp)))]
+    for r in order:
+        for c in beside(r):
+            c.wait_recv()
+        for v, slot in zip(views((me.dp + r) % 16, me.core), sums(r)):
+            add_rows(slot, (v, slot), slot.shape[0], 64)
+        for c in send(r) if r else keep:
+            c.start()
+    for r in range(1, 16):
+        s = (me.dp + 16 - r) % 16
+        for j, v in enumerate(outs(s)):
+            me.copy(v, v, send_sem.at[1, r, j], recv_sem.at[1, r, j], me.dp).wait_recv()
+    for c in keep:
+        c.wait()
+    for r in range(16):
+        for c in beside(r):
+            c.wait_send()
+        if r:
+            for c in send(r):
+                c.wait_send()
+
+
+def expert_grads(gate, up, down, cid):
+    depth, hidden = gate.shape[0] // 16, gate.shape[1] // 2
+    hbm = pl.BlockSpec(memory_space=pl.ANY)
+    vmem = pl.BlockSpec(memory_space=pltpu.VMEM)
+    tall = jax.ShapeDtypeStruct((16, depth, hidden), gate.dtype)
+    return pl.pallas_call(
+        expert_grads_kernel,
+        out_shape=[tall, tall, jax.ShapeDtypeStruct((16, hidden, depth), gate.dtype)],
+        in_specs=[vmem] * 3,
+        out_specs=[hbm] * 3,
+        scratch_shapes=[
+            pltpu.VMEM((2, 16, depth, hidden), gate.dtype),
+            pltpu.VMEM((16, hidden, depth), gate.dtype),
+            pltpu.SemaphoreType.DMA((2, 16, 3)),
+            pltpu.SemaphoreType.DMA((2, 16, 3)),
+            pltpu.SemaphoreType.DMA((3,)),
+        ],
+        compiler_params=pltpu.CompilerParams(collective_id=cid, has_side_effects=True, vmem_limit_bytes=LIMIT),
+        name="expert_grads",
+    )(gate, up, down)
+
+
+def per_device_any(
     tokens,
     cotangent,
     expert_ids,
@@ -374,9 +1018,124 @@
     )
 
 
+def per_device_relay(
+    tokens,
+    cotangent,
+    expert_ids,
+    gate_values,
+    w_query,
+    w_key,
+    w_value,
+    w_out,
+    w_gate,
+    w_up,
+    w_down,
+    attn_gain,
+    ffn_gain,
+    query_gain,
+    key_gain,
+):
+    dot = functools.partial(jnp.dot, preferred_element_type=jnp.float32)
+    dot_t = functools.partial(lax.dot_general, dimension_numbers=(((1,), (1,)), ((), ())), preferred_element_type=jnp.float32)
+    t_dot = functools.partial(lax.dot_general, dimension_numbers=(((0,), (0,)), ((), ())), preferred_element_type=jnp.float32)
+    low = jnp.bfloat16
+    rows, width = tokens.shape
+    head_dim = query_gain.shape[0]
+    experts = w_gate.shape[0]
+    me, core = lax.axis_index("dp"), lax.axis_index("tensor")
+    mine = lax.dynamic_slice_in_dim(expert_ids, core * rows, rows, 0)
+    values = lax.dynamic_slice_in_dim(gate_values, core * rows, rows, 0)
+    match = mine[None] == jnp.arange(experts, dtype=jnp.int32)[:, None, None]
+    gates = jnp.sum(jnp.where(match, values[None], 0.0), axis=2)
+    gates = lax.dynamic_index_in_dim(lax.all_gather(gates, "dp", axis=1, tiled=True), me, 0, keepdims=False)[:, None]
+
+    q_cols, kv_cols = w_query.shape[1] // 2, w_key.shape[1] // 2
+    w_out_rows = jnp.transpose(w_out)
+    halves = jnp.stack(
+        [
+            jnp.concatenate([w[:, h * (w.shape[1] // 2) : (h + 1) * (w.shape[1] // 2)] for w in (w_query, w_key, w_value, w_out_rows)], axis=1)
+            for h in range(2)
+        ]
+    )
+    weights = gather_pairs(halves, 1)
+    weights = weights.reshape(-1, weights.shape[2])
+    proj_cols = q_cols + 2 * kv_cols
+    w_proj, w_back = weights[:, :proj_cols], weights[:, proj_cols:]
+    gate_full, up_full, down_full = expert_weights(w_gate, w_up, w_down, 2)
+    rows_grad = gather_line(cotangent, 3).reshape(-1, width)
+
+    residual = tokens.astype(jnp.float32)
+    inverse_one = rms_inverse(residual)
+    seq_normed = gather_four((residual * inverse_one * attn_gain).astype(low), 4).reshape(-1, width)
+    seq_len = 2 * rows
+    group = q_cols // head_dim
+    scale = head_dim ** (-0.5)
+    cosine, sine_table = rotary_tables(seq_len, head_dim)
+    proj = dot(seq_normed, w_proj)
+    query_raw = proj[:, :q_cols].reshape(2, seq_len, group, head_dim)
+    key_raw = proj[:, q_cols : q_cols + kv_cols].reshape(2, seq_len, 1, head_dim)
+    value_low = proj[:, q_cols + kv_cols :].astype(low).reshape(2, seq_len, head_dim)
+    query_inverse, key_inverse = rms_inverse(query_raw), rms_inverse(key_raw)
+    query_low = (rotate(query_raw * query_inverse * query_gain, cosine, sine_table) * scale).astype(low)
+    key_low = rotate(key_raw * key_inverse * key_gain, cosine, sine_table).astype(low)[:, :, 0]
+    causal = jnp.arange(seq_len)[:, None] >= jnp.arange(seq_len)[None, :]
+    scores = jnp.einsum("bqgd,bsd->bgqs", query_low, key_low, preferred_element_type=jnp.float32)
+    exp_scores = jnp.where(causal, jnp.exp(scores), 0.0)
+    probs = exp_scores / jnp.sum(exp_scores, axis=-1, keepdims=True)
+    probs_low = probs.astype(low)
+    mixed = jnp.einsum("bgqs,bsd->bqgd", probs_low, value_low, preferred_element_type=jnp.float32).astype(low).reshape(2 * seq_len, q_cols)
+    hidden = residual + scatter_four(dot_t(mixed, w_back).astype(low).reshape(2, 2, rows, width), 5)
+    inverse_two = rms_inverse(hidden)
+    rows_in = gather_line((hidden * inverse_two * ffn_gain).astype(low), 6).reshape(-1, width)
+
+    gate_pre = dot(rows_in, gate_full)
+    up_pre = dot(rows_in, up_full)
+    sigmoid_gate = jax.nn.sigmoid(gate_pre)
+    act = (gate_pre * sigmoid_gate * up_pre).astype(low)
+    expert_out = (dot(act, down_full) * gates).astype(low)
+    grad_out = (rows_grad.astype(jnp.float32) * gates).astype(low)
+    grad_act = dot_t(grad_out, down_full)
+    grad_gate = (grad_act * up_pre * sigmoid_gate * (1.0 + gate_pre * (1.0 - sigmoid_gate))).astype(low)
+    grad_up = (grad_act * gate_pre * sigmoid_gate).astype(low)
+    grad_in = (dot_t(grad_gate, gate_full) + dot_t(grad_up, up_full)).astype(low)
+    moe, grad_two = scatter_line([v.reshape(-1, rows, width) for v in (expert_out, grad_in)], 7)
+    w_gate_part = t_dot(rows_in, grad_gate).astype(low)
+    w_up_part = t_dot(rows_in, grad_up).astype(low)
+    w_down_part = t_dot(act, grad_out).astype(low)
+    grad_w_gate, grad_w_up, grad_w_down = [v.astype(jnp.float32) for v in expert_grads(w_gate_part, w_up_part, w_down_part, 8)]
+
+    output = (hidden + moe).astype(low)
+    ffn_gain_part = jnp.sum(grad_two * hidden * inverse_two, axis=0)
+    grad_hidden = cotangent.astype(jnp.float32) + norm_backward(grad_two, hidden, inverse_two, ffn_gain)
+    grad_attn = gather_four(grad_hidden.astype(low), 9).reshape(-1, width)
+    grad_mixed = dot(grad_attn, w_back).astype(low).reshape(2, seq_len, group, head_dim)
+    grad_probs = jnp.einsum("bqgd,bsd->bgqs", grad_mixed, value_low, preferred_element_type=jnp.float32)
+    delta_sum = jnp.sum(grad_probs * probs, axis=-1, keepdims=True)
+    grad_scores = (probs * (grad_probs - delta_sum)).astype(low)
+    grad_query = jnp.einsum("bgqs,bsd->bqgd", grad_scores, key_low, preferred_element_type=jnp.float32)
+    grad_key = jnp.einsum("bgqs,bqgd->bsd", grad_scores, query_low, preferred_element_type=jnp.float32)
+    grad_value = jnp.einsum("bgqs,bqgd->bsd", probs_low, grad_mixed, preferred_element_type=jnp.float32)
+    grad_query_norm = rotate_back(grad_query * scale, cosine, sine_table)
+    query_gain_part = jnp.sum(grad_query_norm * query_raw * query_inverse, axis=(0, 1, 2))
+    grad_query_low = norm_backward(grad_query_norm, query_raw, query_inverse, query_gain).astype(low)
+    grad_key_norm = rotate_back(grad_key[:, :, None], cosine, sine_table)
+    key_gain_part = jnp.sum(grad_key_norm * key_raw * key_inverse, axis=(0, 1, 2))
+    grad_key_low = norm_backward(grad_key_norm, key_raw, key_inverse, key_gain).astype(low)
+    grad_proj = jnp.concatenate([v.astype(low).reshape(2 * seq_len, -1) for v in (grad_query_low, grad_key_low, grad_value)], axis=1)
+    grad_one = scatter_four(dot_t(grad_proj, w_proj).astype(low).reshape(2, 2, rows, width), 10)
+    w_parts = jnp.concatenate([t_dot(seq_normed, grad_proj), t_dot(grad_attn, mixed)], axis=1).astype(low)
+    shares = scatter_pairs(w_parts.reshape(-1, rows, w_parts.shape[1]), 11).astype(jnp.float32)
+    stops = (0, q_cols, q_cols + kv_cols, proj_cols, proj_cols + q_cols)
+    grads = [jnp.concatenate([shares[0, :, a:b], shares[1, :, a:b]], axis=1) for a, b in zip(stops, stops[1:])]
+    attn_gain_part = jnp.sum(grad_one * residual * inverse_one, axis=0)
+    grad_tokens = (grad_hidden + norm_backward(grad_one, residual, inverse_one, attn_gain)).astype(low)
+    totals = lax.psum((attn_gain_part, ffn_gain_part, query_gain_part, key_gain_part), ("dp", "tensor"))
+    return (output, grad_tokens, grads[0], grads[1], grads[2], jnp.transpose(grads[3]), grad_w_gate, grad_w_up, grad_w_down, *totals)
+
+
 def solution(mesh):
     return jax.shard_map(
-        per_device,
+        per_device_relay if tuple(mesh.shape.values()) == (16, 2) else per_device_any,
         mesh=mesh,
         in_specs=(
             P(("dp", "tensor"), None),

time: 2100 us -> 1230 us (0.59)
  waiting for transfers between devices: 1170 us -> 0 us
  Pallas kernels: 0 us -> 897 us
  other arithmetic: 252 us -> 55 us
  starting transfers between devices: 154 us -> 0 us
  blocking collectives: 237 us -> 90.2 us
  local copies, waits for them, and re-layouts: 132 us -> 32.1 us
    pallas_call x0 -> x11, Pallas kernels: none -> 897 us  [the longest x1 237 us: scatter_line(): pl.pallas_call(functools.partial(scatter_line_kernel, number), out_shape=...]
    all_to_all x7 -> x0, waiting for transfers between devices: 525 us -> none  [the longest x1 159 us: per_device(): lax.all_to_all(grad_input.reshape(dp_count, piece_rows, model_width).asty...]
    all_gather x8 -> x0, waiting for transfers between devices: 390 us -> none  [the longest x1 145 us: per_device(): lax.all_gather(w_out, 'dp', axis=1, tiled=True)]
    reduce_scatter x5 -> x0, waiting for transfers between devices: 249 us -> none  [the longest x1 237 us: per_device(): lax.psum_scatter(jnp.concatenate([first_part, second], axis=1), 'dp', sca...]
    all_to_all x1 -> x0, blocking collectives: 197 us -> none  [per_device(): lax.all_to_all(grad_cols[None].astype(jnp.bfloat16), 'dp', split_axis=1,...]
    all_to_all x7 -> x0, starting transfers between devices: 153 us -> none  [the longest x1 43.6 us: per_device(): lax.all_to_all(grad_blocks.reshape(dp_count, piece_rows, model_width), 'd...]
    unnamed x4 -> x2, other arithmetic: 102 us -> 0.01 us
    scatter-add x2 -> x0, other arithmetic: 70.4 us -> none  [the longest x1 35.5 us: per_device(): grad_acc = empty_rows.at[flat_slots].add(back_grad)]
  transfers between devices with their start and end apart: 20 -> 0, of which waited for: 16 -> 0; matrix products, arithmetic and copies ran while one was open for 22% -> 0% of each run, Pallas kernels for 0% -> 0%
where the time goes in v1:
time: 1230 us; the launch traced here: 1210 us
  Pallas kernels  897 us (73%)
  matrix products  137 us (11%)
  blocking collectives  90.2 us (7%)
  other arithmetic  55 us (4%)
  local copies, waits for them, and re-layouts  32.1 us (3%)
    pallas_call x1, Pallas kernels, scatter_line(): pl.pallas_call(functools.partial(scatter_line_kernel, number), out_shape=...  237 us
    pallas_call x2, Pallas kernels, gather_line(): pl.pallas_call(functools.partial(gather_line_kernel, chunks), out_shape=j...  143 us
    pallas_call x1, Pallas kernels, expert_grads(): pl.pallas_call(expert_grads_kernel, out_shape=[tall, tall, jax.ShapeDtype...  135 us
    pallas_call x1, Pallas kernels, scatter_pairs(): pl.pallas_call(scatter_pairs_kernel, out_shape=jax.ShapeDtypeStruct((2, r...  124 us
    pallas_call x1, Pallas kernels, gather_pairs(): pl.pallas_call(gather_pairs_kernel, out_shape=jax.ShapeDtypeStruct((16, r...  94.8 us
    pallas_call x1, Pallas kernels, expert_weights(): pl.pallas_call(expert_weights_kernel, out_shape=[wide, wide, jax.ShapeDty...  92.1 us
    psum x1, blocking collectives, per_device_relay(): lax.psum((attn_gain_part, ffn_gain_part, query_gain_part, key_gain_part),...  47.1 us
    all_gather x1, blocking collectives, per_device_relay(): lax.all_gather(gates, 'dp', axis=1, tiled=True)  43.2 us

profile of v1, /device:TPU:0, one launch (start us, length us, event | category | flops | bytes accessed | tf_op | source)
XLA Modules:
  0.0 1213.3 jit_solution(13529294387736679821)
XLA Ops:
  6.2 43.2 %all_gather.3 = f32[16,2048]{1,0:T(8,128)S(1)} all-gather(f32[16,128]{1,0:T(8,128)S(1)} %select_reduce_fusion), channel_id=1, replica_groups=mesh['dp'=16,'tensor'=2] {'dp'}, dimensions={1}, use_global_device_ids=true | all-gather | bytes 139264 | tf_op jit(solution)/shard_map/all_gather | solution.py:1050
  54.6 14.6 %gather_four.2 = bf16[2,2,128,2048]{3,2,1,0:T(8,128)(2,1)} custom-call(bf16[128,2048]{1,0:T(8,128)(2,1)} %fusion.37.x_ref), custom_call_target="tpu_custom_call" | custom-call | tf_op jit(solution)/shard_map/gather_four/pallas_call | solution.py:572
  73.1 94.8 %gather_pairs.1 = bf16[16,128,2304]{2,1,0:T(8,128)(2,1)} custom-call(bf16[2,128,2304]{2,1,0:T(8,128)(2,1)} %pad_maximum_fusion.3.x_ref), custom_call_target="tpu_custom_call" | custom-call | tf_op jit(solution)/shard_map/gather_pairs/pallas_call | solution.py:367
  196.3 19.0 %scatter_four.2 = f32[128,2048]{1,0:T(8,128)} custom-call(bf16[2,2,128,2048]{3,2,1,0:T(8,128)(2,1)} %bitcast.221), custom_call_target="tpu_custom_call" | custom-call | tf_op jit(solution)/shard_map/scatter_four/pallas_call | solution.py:610
  218.8 71.5 %gather_line.2 = bf16[16,128,2048]{2,1,0:T(8,128)(2,1)} custom-call(bf16[128,2048]{1,0:T(8,128)(2,1)} %multiply_convert_fusion.4.x_ref), custom_call_target="tpu_custom_call" | custom-call | tf_op jit(solution)/shard_map/gather_line/pallas_call | solution.py:300
  290.3 71.4 %gather_line.3 = bf16[16,128,2048]{2,1,0:T(8,128)(2,1)} custom-call(bf16[128,2048]{1,0:T(8,128)(2,1)} %x_ref.1), custom_call_target="tpu_custom_call" | custom-call | tf_op jit(solution)/shard_map/gather_line/pallas_call | solution.py:300
  361.7 8.1 fusion
  369.8 92.1 %expert_weights.1 = (bf16[2048,768]{1,0:T(8,128)(2,1)}, bf16[2048,768]{1,0:T(8,128)(2,1)}, bf16[768,2048]{1,0:T(8,128)(2,1)}) custom-call(bf16[16,128,384]{2,1,0:T(8,128)(2,1)} %gate_ref.1, bf16[16,128,384]{2,1,0:T(8,128)(2,1)} %up_ref.1, bf16[16,384,128]{2,1,0:T(8,128)(2,1)} %down_ref.1), custom_call_target="tpu_custom_call" | custom-call | tf_op jit(solution)/shard_map/expert_weights/pallas_call | solution.py:689
  461.9 11.8 fusion.68
  473.7 10.9 fusion.69
  484.6 16.5 %multiply_convert_fusion.1 = (bf16[2048,768]{1,0:T(8,128)(2,1)}, bf16[2048,768]{1,0:T(8,128)(2,1)}, bf16[2048,768]{1,0:T(8,128)(2,1)}) fusion(f32[2048,768]{1,0:T(8,128)} %fusion.68, f32[2048,768]{1,0:T(8,128)} %fusion.69, bf16[2048,2048]{1,0:T(8,128)(2,1)} %fusion, bf16[768,2048]{1,0:T(8,128)(2,1)S(1)} %copy-done.62), kind=kOutput, calls=%fused_computation.5 | convolution fusion | flops 6467616768 | bytes 33554432 | tf_op jit(solution)/shard_map/dot_general | solution.py:1097
  501.1 12.1 convolution_convert_fusion.1.down_ref
  513.2 8.7 convolution_convert_fusion.2.up_ref
  521.9 8.6 convolution_convert_fusion.3.gate_ref
  530.5 134.7 %expert_grads.1 = (bf16[16,128,384]{2,1,0:T(8,128)(2,1)}, bf16[16,128,384]{2,1,0:T(8,128)(2,1)}, bf16[16,384,128]{2,1,0:T(8,128)(2,1)}) custom-call(bf16[2048,768]{1,0:T(8,128)(2,1)} %convolution_convert_fusion.3.gate_ref, bf16[2048,768]{1,0:T(8,128)(2,1)} %convolution_convert_fusion.2.up_ref, bf16[768,2048]{1,0:T(8,128)(2,1)} %convolution_convert_fusion.1.down_ref), custom_call_target="tpu_custom_call" | custom-call | tf_op jit(solution)/shard_map/expert_grads/pallas_call | solution.py:767
  674.4 9.3 multiply_convert_fusion
  683.8 9.6 fusion.70
  693.3 12.7 %add_convert_fusion = bf16[2048,2048]{1,0:T(8,128)(2,1)} fusion(f32[2048,2048]{1,0:T(8,128)} %fusion.70, bf16[2048,768]{1,0:T(8,128)(2,1)S(1)} %copy-done.68, bf16[2048,768]{1,0:T(8,128)(2,1)S(1)} %copy-done.60), kind=kOutput, calls=%fused_computation.2 | convolution fusion | flops 6450839552 | bytes 31457280 | tf_op jit(solution)/shard_map/dot_general | solution.py:1100
  706.1 236.6 %scatter_line.1 = (f32[128,2048]{1,0:T(8,128)}, f32[128,2048]{1,0:T(8,128)}) custom-call(bf16[16,128,2048]{2,1,0:T(8,128)(2,1)} %bitcast.213, bf16[16,128,2048]{2,1,0:T(8,128)(2,1)} %bitcast.214), custom_call_target="tpu_custom_call" | custom-call | tf_op jit(solution)/shard_map/scatter_line/pallas_call | solution.py:535
  948.1 19.2 %gather_four.3 = bf16[2,2,128,2048]{3,2,1,0:T(8,128)(2,1)} custom-call(bf16[128,2048]{1,0:T(8,128)(2,1)} %get-tuple-element.119.x_ref), custom_call_target="tpu_custom_call" | custom-call | tf_op jit(solution)/shard_map/gather_four/pallas_call | solution.py:572
  977.8 6.1 convolution_convert_fusion.4
  1005.7 19.0 %scatter_four.3 = f32[128,2048]{1,0:T(8,128)} custom-call(bf16[2,2,128,2048]{3,2,1,0:T(8,128)(2,1)} %bitcast.220), custom_call_target="tpu_custom_call" | custom-call | tf_op jit(solution)/shard_map/scatter_four/pallas_call | solution.py:610
  1026.4 47.1 %all-reduce = (f32[2048]{0:T(1024)}, f32[2048]{0:T(1024)}, f32[128]{0:T(128)}, f32[128]{0:T(128)}) all-reduce(f32[2048]{0:T(1024)S(1)} %get-tuple-element.111, f32[2048]{0:T(1024)S(1)} %get-tuple-element.109, f32[128]{0:T(128)S(1)} %bitcast_reduce_fusion, ...), channel_id=1, replica_groups=mesh['dp'=16,'tensor'=2] {'dp','tensor'}, use_global_device_ids=true, to_apply=%region_12.13 | all-reduce | flops 4352 | bytes 34816 | tf_op jit(solution)/shard_map/psum | solution.py:1132
  1083.3 124.3 %scatter_pairs.1 = bf16[2,128,2304]{2,1,0:T(8,128)(2,1)} custom-call(bf16[16,128,2304]{2,1,0:T(8,128)(2,1)} %pad_maximum_fusion.p_ref), custom_call_target="tpu_custom_call" | custom-call | tf_op jit(solution)/shard_map/scatter_pairs/pallas_call | solution.py:435
  (236 shorter events, 109.6 us)
Async XLA Ops:
  0.7 52.6 %copy-start.37 = (bf16[128,2048]{1,0:T(8,128)(2,1)S(1)}, bf16[128,2048]{1,0:T(8,128)(2,1)}, u32[]{:S(2)}) copy-start(bf16[128,2048]{1,0:T(8,128)(2,1)} %param.19) | copy-start | bytes 1572868
  2.6 50.9 %copy-start.51 = (f32[128]{0:T(128)}, f32[128]{0:T(128)S(1)}, u32[]{:S(2)}) copy-start(f32[128]{0:T(128)S(1)} %get-tuple-element.160) | copy-start | bytes 1540
  4.6 180.7 %copy-start.30 = (pred[256,256]{0,1:T(8,128)(4,1)}, pred[256,256]{0,1:T(8,128)(4,1)S(1)}, u32[]{:S(2)}) copy-start(pred[256,256]{0,1:T(8,128)(4,1)S(1)} %iota_compare_fusion) | copy-start | bytes 196612
  49.9 131.8 %copy-start.18 = (f32[256,64]{1,0:T(8,128)}, f32[256,64]{1,0:T(8,128)S(1)}, u32[]{:S(2)}) copy-start(f32[256,64]{1,0:T(8,128)S(1)} %get-tuple-element.163) | copy-start | bytes 196612
  49.9 131.8 %copy-start.20 = (f32[256,64]{1,0:T(8,128)}, f32[256,64]{1,0:T(8,128)S(1)}, u32[]{:S(2)}) copy-start(f32[256,64]{1,0:T(8,128)S(1)} %get-tuple-element.164) | copy-start | bytes 196612
  173.9 11.4 copy-start.38
  196.3 19.0 %copy-start.8 = (bf16[128,2048]{1,0:T(8,128)(2,1)S(1)}, bf16[128,2048]{1,0:T(8,128)(2,1)}, u32[]{:S(2)}) copy-start(bf16[128,2048]{1,0:T(8,128)(2,1)} %param.15) | copy-start | bytes 1572868
  196.3 21.5 %copy-start.40 = (f32[2048]{0:T(1024)S(1)}, f32[2048]{0:T(1024)}, u32[]{:S(2)}) copy-start(f32[2048]{0:T(1024)} %param.27) | copy-start | bytes 24580
  461.8 11.8 copy-start.59
  473.7 10.9 copy-start.62
  473.7 39.5 %slice-start.3 = ((s8[8388608]{0:T(1024)(128)(4,1)}), s8[4194304]{0:T(1024)(128)(4,1)S(1)}, s32[]{:S(2)}) async-start(s8[8388608]{0:T(1024)(128)(4,1)} %bitcast.209), calls=%async_computation.3 | async-start | bytes 8388608
  484.6 28.6 %slice-start.4 = ((s8[8388608]{0:T(1024)(128)(4,1)}), s8[4194304]{0:T(1024)(128)(4,1)S(1)}, s32[]{:S(2)}) async-start(s8[8388608]{0:T(1024)(128)(4,1)} %bitcast.209), calls=%async_computation.4 | async-start | bytes 8388608
  501.1 12.1 copy-start.67
  683.8 9.6 copy-start.68
  706.0 236.6 %copy-start.41 = (f32[2048]{0:T(1024)S(1)}, f32[2048]{0:T(1024)}, u32[]{:S(2)}) copy-start(f32[2048]{0:T(1024)} %param.27) | copy-start | bytes 24580
  706.0 236.6 %copy-start.56 = (f32[128]{0:T(128)S(1)}, f32[128]{0:T(128)}, u32[]{:S(2)}) copy-start(f32[128]{0:T(128)} %copy-done.55) | copy-start | bytes 1540
  706.0 238.4 %copy-start.22 = (bf16[128,2048]{1,0:T(8,128)(2,1)S(1)}, bf16[128,2048]{1,0:T(8,128)(2,1)}, u32[]{:S(2)}) copy-start(bf16[128,2048]{1,0:T(8,128)(2,1)} %x_ref.1) | copy-start | bytes 1572868
  706.0 238.5 %copy-start.58 = (f32[128]{0:T(128)S(1)}, f32[128]{0:T(128)}, u32[]{:S(2)}) copy-start(f32[128]{0:T(128)} %get-tuple-element.161) | copy-start | bytes 1540
  1005.6 19.1 %copy-start.9 = (bf16[128,2048]{1,0:T(8,128)(2,1)S(1)}, bf16[128,2048]{1,0:T(8,128)(2,1)}, u32[]{:S(2)}) copy-start(bf16[128,2048]{1,0:T(8,128)(2,1)} %param.15) | copy-start | bytes 1572868
  1005.6 19.1 %copy-start.42 = (f32[2048]{0:T(1024)S(1)}, f32[2048]{0:T(1024)}, u32[]{:S(2)}) copy-start(f32[2048]{0:T(1024)} %param.26) | copy-start | bytes 24580
  1005.6 19.1 %copy-start.52 = (f32[128]{0:T(128)S(1)}, f32[128]{0:T(128)}, u32[]{:S(2)}) copy-start(f32[128]{0:T(128)} %copy-done.51) | copy-start | bytes 1540
  1005.7 67.8 %copy-start.16 = (f32[128,2048]{1,0:T(8,128)S(1)}, f32[128,2048]{1,0:T(8,128)}, u32[]{:S(2)}) copy-start(f32[128,2048]{1,0:T(8,128)} %get-tuple-element.120) | copy-start | bytes 3145732
  1005.7 67.8 %copy-start.57 = (f32[128]{0:T(128)S(1)}, f32[128]{0:T(128)}, u32[]{:S(2)}) copy-start(f32[128]{0:T(128)} %get-tuple-element.159) | copy-start | bytes 1540
  1024.8 51.4 %copy-start.33 = (bf16[512,1024]{1,0:T(8,128)(2,1)S(1)}, bf16[512,1024]{1,0:T(8,128)(2,1)}, u32[]{:S(2)}) copy-start(bf16[512,1024]{1,0:T(8,128)(2,1)} %copy-done.32) | copy-start | bytes 3145732
  (50 other events, 195.1 us)

commit v2 on v0

--- a/solution.py
+++ b/solution.py
@@ -1,6 +1,10 @@
+import functools
+
 import jax
 import jax.numpy as jnp
 from jax import lax
+from jax.experimental import pallas as pl
+from jax.experimental.pallas import tpu as pltpu
 from jax.sharding import PartitionSpec as P
 
 epsilon = 1e-06
@@ -137,7 +141,677 @@
     return spread.reshape((experts * group,) + stacked.shape[1:])
 
 
-def per_device(
+MESH = pl.DeviceIdType.MESH
+LIMIT = 66_000_000
+
+
+class Place:
+    def __init__(self):
+        self.dp = lax.axis_index("dp")
+        self.core = lax.axis_index("tensor")
+        x, y = self.dp % 2, (self.dp // 2) % 2
+        self.z = self.dp // 4
+        step_x, step_y = 1 - 2 * x, 2 * (1 - 2 * y)
+        self.da = (1 - self.core) * step_x + self.core * step_y
+        self.db = (1 - self.core) * step_y + self.core * step_x
+        self.half = self.z % 2
+        self.pair = 4 * (1 - 2 * self.half)
+        self.far = 8 * (1 - 2 * (self.z // 2))
+
+    def copy(self, src, dst, send_sem, recv_sem, to, core=None):
+        return pltpu.make_async_remote_copy(
+            src_ref=src,
+            dst_ref=dst,
+            send_sem=send_sem,
+            recv_sem=recv_sem,
+            device_id=(to, self.core if core is None else core),
+            device_id_type=MESH,
+        )
+
+    def at_z(self, z):
+        return self.dp + 4 * (z - self.z)
+
+    def greet(self, line=False, near=False, chain=False, everyone=False, partner=False):
+        barrier = pltpu.get_barrier_semaphore()
+        count = 0
+
+        def signal(to, core):
+            pl.semaphore_signal(barrier, inc=1, device_id=(to, core), device_id_type=MESH)
+
+        if everyone:
+            for r in range(1, 16):
+                signal((self.dp + r) % 16, self.core)
+            count = count + 15
+        else:
+            if near:
+                signal(self.dp + self.da, self.core)
+                signal(self.dp + self.db, self.core)
+                count = count + 2
+            if chain:
+                signal(self.dp + self.pair, self.core)
+                count = count + 1
+                if near:
+                    signal(self.dp + self.far, self.core)
+                    count = count + 1
+            if line:
+                pl.when(self.z > 0)(lambda: signal(self.dp - 4, self.core))
+                pl.when(self.z < 3)(lambda: signal(self.dp + 4, self.core))
+                count = count + jnp.where(self.z > 0, 1, 0) + jnp.where(self.z < 3, 1, 0)
+        if partner:
+            signal(self.dp, 1 - self.core)
+            count = count + 1
+        pl.semaphore_wait(barrier, count)
+
+
+def add_rows(target, terms, rows, block=16):
+    def body(i, _):
+        at = pl.ds(pl.multiple_of(i * block, block), block)
+        total = terms[0][at, :].astype(jnp.float32)
+        for term in terms[1:]:
+            total = total + term[at, :].astype(jnp.float32)
+        target[at, :] = total.astype(target.dtype)
+        return 0
+
+    lax.fori_loop(0, rows // block, body, 0)
+
+
+def gather_four_kernel(x_ref, out_ref, send_sem, recv_sem):
+    me = Place()
+    me.greet(chain=True, partner=True)
+    mine, theirs = out_ref.at[me.half, me.core], out_ref.at[1 - me.half, me.core]
+    across = me.copy(x_ref, mine, send_sem.at[0], recv_sem.at[0], me.dp + me.pair)
+    across.start()
+    beside = me.copy(x_ref, mine, send_sem.at[1], recv_sem.at[1], me.dp, 1 - me.core)
+    beside.start()
+    mine[...] = x_ref[...]
+    across.wait_recv()
+    relay = me.copy(theirs, theirs, send_sem.at[2], recv_sem.at[2], me.dp, 1 - me.core)
+    relay.start()
+    across.wait_send()
+    beside.wait()
+    relay.wait()
+
+
+def gather_four(x, cid):
+    rows, columns = x.shape
+    vmem = pl.BlockSpec(memory_space=pltpu.VMEM)
+    return pl.pallas_call(
+        gather_four_kernel,
+        out_shape=jax.ShapeDtypeStruct((2, 2, rows, columns), x.dtype),
+        in_specs=[vmem],
+        out_specs=vmem,
+        scratch_shapes=[pltpu.SemaphoreType.DMA((3,)), pltpu.SemaphoreType.DMA((3,))],
+        compiler_params=pltpu.CompilerParams(collective_id=cid, has_side_effects=True),
+        name="gather_four",
+    )(x)
+
+
+def scatter_four_kernel(p_ref, out_ref, from_core, from_pair, send_sem, recv_sem):
+    me = Place()
+    rows = p_ref.shape[2]
+    me.greet(chain=True, partner=True)
+
+    def beside(h, slot):
+        return me.copy(p_ref.at[h, 1 - me.core], from_core.at[slot], send_sem.at[slot], recv_sem.at[slot], me.dp, 1 - me.core)
+
+    first, second = beside(1 - me.half, 0), beside(me.half, 1)
+    first.start()
+    second.start()
+    first.wait_recv()
+    add_rows(from_core.at[0], (p_ref.at[1 - me.half, me.core], from_core.at[0]), rows)
+    across = me.copy(from_core.at[0], from_pair, send_sem.at[2], recv_sem.at[2], me.dp + me.pair)
+    across.start()
+    second.wait_recv()
+    add_rows(from_core.at[1], (p_ref.at[me.half, me.core], from_core.at[1]), rows)
+    across.wait_recv()
+    add_rows(out_ref, (from_core.at[1], from_pair), rows)
+    across.wait_send()
+    first.wait_send()
+    second.wait_send()
+
+
+def scatter_four(p, cid):
+    _, _, rows, columns = p.shape
+    vmem = pl.BlockSpec(memory_space=pltpu.VMEM)
+    return pl.pallas_call(
+        scatter_four_kernel,
+        out_shape=jax.ShapeDtypeStruct((rows, columns), jnp.float32),
+        in_specs=[vmem],
+        out_specs=vmem,
+        scratch_shapes=[
+            pltpu.VMEM((2, rows, columns), p.dtype),
+            pltpu.VMEM((rows, columns), p.dtype),
+            pltpu.SemaphoreType.DMA((3,)),
+            pltpu.SemaphoreType.DMA((3,)),
+        ],
+        compiler_params=pltpu.CompilerParams(collective_id=cid, has_side_effects=True),
+        name="scatter_four",
+    )(p)
+
+
+def run(*threads):
+    threads = list(threads)
+    while threads:
+        for thread in list(threads):
+            if next(thread, "end") == "end":
+                threads.remove(thread)
+
+
+def lagged(items, first, second, lag):
+    for n in range(len(items) + lag):
+        if n < len(items):
+            first(items[n])
+            yield
+        if n >= lag:
+            second(items[n - lag])
+            yield
+
+
+def gather_line(me, x_ref, out_ref, send_sem, recv_sem):
+    def part(source, to, slot, own=False):
+        return me.copy(x_ref if own else out_ref.at[source], out_ref.at[source], send_sem.at[slot], recv_sem.at[source], to)
+
+    sides = ((-1, me.z < 3, 4), (1, me.z > 0, -4))
+
+    def exists(d, side):
+        return (me.z - d >= 0) if side == 0 else (me.z + d <= 3)
+
+    def slot_z(d, side, j):
+        return 4 + ((d - 1) * 2 + side) * 3 + j
+
+    def slot_a(off):
+        return 25 + off
+
+    def pass_a(off):
+        source = me.dp + me.da + 4 * off
+        part(source, me.dp, slot_a(off)).wait_recv()
+        part(source, me.dp + me.db, slot_a(off)).start()
+
+    pl.when(me.z < 3)(lambda: part(me.dp, me.dp + 4, 0, True).start())
+    pl.when(me.z > 0)(lambda: part(me.dp, me.dp - 4, 1, True).start())
+    part(me.dp, me.dp + me.db, 3, True).start()
+    part(me.dp, me.dp + me.da, 2, True).start()
+    yield
+    for d in range(1, 5):
+        if d < 4:
+            for side, (sign, forward, step) in enumerate(sides):
+                source = me.dp + 4 * sign * d
+
+                def arrive():
+                    part(source, me.dp, slot_z(d, side, 0)).wait_recv()
+                    pl.when(forward)(lambda: part(source, me.dp + step, slot_z(d, side, 0)).start())
+                    part(source, me.dp + me.db, slot_z(d, side, 2)).start()
+                    part(source, me.dp + me.da, slot_z(d, side, 1)).start()
+
+                pl.when(exists(d, side))(arrive)
+                yield
+        if d == 1:
+            pass_a(0)
+            yield
+        else:
+            for side, (sign, *_) in enumerate(sides):
+                pl.when(exists(d - 1, side))(lambda: pass_a(sign * (d - 1)))
+                yield
+    for z in range(4):
+        for g in (0, 1):
+            part(me.at_z(z) + me.db + g * me.da, me.dp, 0).wait_recv()
+            yield
+
+    def sent(slot):
+        part(me.dp, me.dp, slot).wait_send()
+
+    pl.when(me.z < 3)(lambda: sent(0))
+    pl.when(me.z > 0)(lambda: sent(1))
+    sent(2)
+    sent(3)
+    sent(slot_a(0))
+    for d in range(1, 4):
+        for side, (sign, forward, _) in enumerate(sides):
+
+            def finish():
+                pl.when(forward)(lambda: sent(slot_z(d, side, 0)))
+                sent(slot_z(d, side, 1))
+                sent(slot_z(d, side, 2))
+                sent(slot_a(sign * d))
+
+            pl.when(exists(d, side))(finish)
+
+
+def gather_pairs(me, x_ref, out_ref, send_sem, recv_sem):
+    mine, other = me.dp, me.dp + me.pair
+
+    def part(src, where, to, slot):
+        return me.copy(src, out_ref.at[where], send_sem.at[slot], recv_sem.at[where], to)
+
+    def relay(where, to, slot):
+        part(out_ref.at[where], where, to, slot).start()
+
+    def arrived(where):
+        part(out_ref.at[where], where, me.dp, 0).wait_recv()
+
+    part(x_ref.at[1 - me.half], mine, other, 0).start()
+    part(x_ref.at[me.half], mine, me.dp + me.far, 1).start()
+    part(x_ref.at[me.half], mine, me.dp + me.db, 2).start()
+    part(x_ref.at[me.half], mine, me.dp + me.da, 3).start()
+    yield
+    arrived(other)
+    relay(other, me.dp + me.far, 4)
+    relay(other, me.dp + me.db, 5)
+    relay(other, me.dp + me.da, 6)
+    yield
+    arrived(mine + me.da)
+    relay(mine + me.da, me.dp + me.db, 7)
+    yield
+    arrived(mine + me.far)
+    relay(mine + me.far, me.dp + me.db, 8)
+    relay(mine + me.far, me.dp + me.da, 9)
+    yield
+    arrived(other + me.da)
+    relay(other + me.da, me.dp + me.db, 10)
+    yield
+    arrived(other + me.far)
+    relay(other + me.far, me.dp + me.db, 11)
+    relay(other + me.far, me.dp + me.da, 12)
+    yield
+    arrived(mine + me.far + me.da)
+    relay(mine + me.far + me.da, me.dp + me.db, 13)
+    yield
+    arrived(other + me.far + me.da)
+    relay(other + me.far + me.da, me.dp + me.db, 14)
+    yield
+    for base in (mine, other, mine + me.far, other + me.far):
+        arrived(base + me.db)
+        yield
+        arrived(base + me.da + me.db)
+        yield
+    for slot in range(15):
+        part(out_ref.at[mine], mine, me.dp, slot).wait_send()
+
+
+def swap_rows(me, x_ref, out_ref, send_sem, recv_sem):
+    for r in range(1, 16):
+        to = (me.dp + r) % 16
+        me.copy(x_ref.at[to], out_ref.at[me.dp], send_sem.at[r], recv_sem.at[r], to).start()
+    yield
+    for r in range(1, 16):
+        s = (me.dp + 16 - r) % 16
+        me.copy(x_ref.at[s], out_ref.at[s], send_sem.at[r], recv_sem.at[r], me.dp).wait_recv()
+    for r in range(1, 16):
+        me.copy(x_ref.at[me.dp], out_ref.at[me.dp], send_sem.at[r], recv_sem.at[r], me.dp).wait_send()
+
+
+def keep_own(src, staging, dst, sems):
+    load = pltpu.make_async_copy(src, staging, sems.at[0])
+    store = pltpu.make_async_copy(staging, dst, sems.at[1])
+    load.start()
+
+    def finish():
+        load.wait()
+        store.start()
+        store.wait()
+
+    return finish
+
+
+def gather_first_kernel(w_ref, c_ref, g_ref, w_out, c_out, g_out, w_own, c_own, w_send, w_recv, c_send, c_recv, g_send, g_recv, copy_sem):
+    me = Place()
+    ends = [
+        keep_own(w_ref.at[me.half], w_own, w_out.at[me.dp], copy_sem.at[0]),
+        keep_own(c_ref, c_own, c_out.at[me.dp], copy_sem.at[1]),
+    ]
+    g_out[me.dp] = g_ref[me.dp]
+    me.greet(everyone=True)
+    run(
+        gather_pairs(me, w_ref, w_out, w_send, w_recv),
+        gather_line(me, c_ref, c_out, c_send, c_recv),
+        swap_rows(me, g_ref, g_out, g_send, g_recv),
+    )
+    for end in ends:
+        end()
+
+
+def gather_first(weights, rows, gates, cid):
+    hbm, vmem = pl.BlockSpec(memory_space=pl.ANY), pl.BlockSpec(memory_space=pltpu.VMEM)
+    dma = pltpu.SemaphoreType.DMA
+    return pl.pallas_call(
+        gather_first_kernel,
+        out_shape=[
+            jax.ShapeDtypeStruct((16,) + weights.shape[1:], weights.dtype),
+            jax.ShapeDtypeStruct((16,) + rows.shape, rows.dtype),
+            jax.ShapeDtypeStruct(gates.shape, gates.dtype),
+        ],
+        in_specs=[hbm, hbm, vmem],
+        out_specs=[hbm, hbm, vmem],
+        scratch_shapes=[
+            pltpu.VMEM(weights.shape[1:], weights.dtype),
+            pltpu.VMEM(rows.shape, rows.dtype),
+            dma((15,)),
+            dma((16,)),
+            dma((29,)),
+            dma((16,)),
+            dma((16,)),
+            dma((16,)),
+            dma((2, 2)),
+        ],
+        compiler_params=pltpu.CompilerParams(collective_id=cid, has_side_effects=True),
+        name="gather_first",
+    )(weights, rows, gates)
+
+
+def gather_rows_kernel(x_ref, out_ref, own, send_sem, recv_sem, copy_sem):
+    me = Place()
+    end = keep_own(x_ref, own, out_ref.at[me.dp], copy_sem)
+    me.greet(line=True, near=True)
+    run(gather_line(me, x_ref, out_ref, send_sem, recv_sem))
+    end()
+
+
+def gather_dp(x, cid):
+    hbm = pl.BlockSpec(memory_space=pl.ANY)
+    dma = pltpu.SemaphoreType.DMA
+    return pl.pallas_call(
+        gather_rows_kernel,
+        out_shape=jax.ShapeDtypeStruct((16,) + x.shape, x.dtype),
+        in_specs=[hbm],
+        out_specs=hbm,
+        scratch_shapes=[pltpu.VMEM(x.shape, x.dtype), dma((29,)), dma((16,)), dma((2,))],
+        compiler_params=pltpu.CompilerParams(collective_id=cid, has_side_effects=True),
+        name="gather_dp",
+    )(x)
+
+
+def scatter_pairs(me, chunks, p_ref, out_ref, from_b, from_a, from_far, send_sem, recv_sem):
+    rows = p_ref.shape[1] // chunks
+    other = me.dp + me.pair
+    bases = (me.dp, other, me.dp + me.far, other + me.far)
+    items = [(j, k) for j in (2, 3, 1, 0) for k in range(chunks)]
+
+    def at(k):
+        return pl.ds(k * rows, rows)
+
+    def copy(src, dst, slot, k, to):
+        return me.copy(src, dst, send_sem.at[slot, k], recv_sem.at[slot, k], to)
+
+    def send_b(g, j, k):
+        return copy(p_ref.at[bases[j] + me.db + g * me.da, at(k)], from_b.at[g, j, at(k)], g * 4 + j, k, me.dp + me.db)
+
+    def send_a(j, k):
+        return copy(from_b.at[1, j, at(k)], from_a.at[j, at(k)], 8 + j, k, me.dp + me.da)
+
+    def send_far(j, k):
+        return copy(from_b.at[0, 2 + j, at(k)], from_far.at[j, at(k)], 12 + j, k, me.dp + me.far)
+
+    def swap(k):
+        return copy(from_b.at[0, 1, at(k)], out_ref.at[me.half, at(k)], 14, k, other)
+
+    for j, k in items:
+        send_b(1, j, k).start()
+        send_b(0, j, k).start()
+    yield
+
+    def first(item):
+        j, k = item
+        send_b(1, j, k).wait_recv()
+        add_rows(from_b.at[1, j, at(k)], (p_ref.at[bases[j] + me.da, at(k)], from_b.at[1, j, at(k)]), rows)
+        send_a(j, k).start()
+
+    def second(item):
+        j, k = item
+        send_b(0, j, k).wait_recv()
+        send_a(j, k).wait_recv()
+        terms = (p_ref.at[bases[j], at(k)], from_b.at[0, j, at(k)], from_a.at[j, at(k)])
+        if j >= 2:
+            add_rows(from_b.at[0, j, at(k)], terms, rows)
+            send_far(j - 2, k).start()
+        else:
+            send_far(j, k).wait_recv()
+            target = from_b.at[0, 1, at(k)] if j else out_ref.at[me.half, at(k)]
+            add_rows(target, terms + (from_far.at[j, at(k)],), rows)
+            if j:
+                swap(k).start()
+
+    yield from lagged(items, first, second, 2)
+    for k in range(chunks):
+        swap(k).wait_send()
+        theirs = out_ref.at[1 - me.half, at(k)]
+        copy(theirs, theirs, 14, k, other).wait_recv()
+        for j in range(4):
+            send_b(0, j, k).wait_send()
+            send_b(1, j, k).wait_send()
+            send_a(j, k).wait_send()
+        send_far(0, k).wait_send()
+        send_far(1, k).wait_send()
+
+
+def sum_all(me, x_ref, out_ref, held, send_sem, recv_sem):
+    out_ref[...] = x_ref[...]
+    steps = ((me.dp, 1 - me.core), (me.dp + me.da, me.core), (me.dp + me.db, me.core), (me.dp + me.pair, me.core), (me.dp + me.far, me.core))
+    yield
+    for n, (to, core) in enumerate(steps):
+        send = me.copy(held.at[0, n], held.at[1, n], send_sem.at[n], recv_sem.at[n], to, core)
+        held[0, n] = out_ref[...]
+        send.start()
+        yield
+        send.wait()
+        out_ref[...] = held[0, n] + held[1, n]
+        yield
+
+
+def scatter_last_kernel(chunks, p_ref, x_ref, out_ref, sum_ref, from_b, from_a, from_far, held, send_sem, recv_sem, sum_send, sum_recv):
+    me = Place()
+    me.greet(near=True, chain=True, partner=True)
+    run(
+        scatter_pairs(me, chunks, p_ref, out_ref, from_b, from_a, from_far, send_sem, recv_sem),
+        sum_all(me, x_ref, sum_ref, held, sum_send, sum_recv),
+    )
+
+
+def scatter_last(p, x, cid, chunks=2):
+    _, rows, columns = p.shape
+    vmem = pl.BlockSpec(memory_space=pltpu.VMEM)
+    dma = pltpu.SemaphoreType.DMA
+    return pl.pallas_call(
+        functools.partial(scatter_last_kernel, chunks),
+        out_shape=[jax.ShapeDtypeStruct((2, rows, columns), p.dtype), jax.ShapeDtypeStruct(x.shape, x.dtype)],
+        in_specs=[vmem] * 2,
+        out_specs=[vmem] * 2,
+        scratch_shapes=[
+            pltpu.VMEM((2, 4, rows, columns), p.dtype),
+            pltpu.VMEM((4, rows, columns), p.dtype),
+            pltpu.VMEM((2, rows, columns), p.dtype),
+            pltpu.VMEM((2, 5) + x.shape, x.dtype),
+            dma((15, chunks)),
+            dma((15, chunks)),
+            dma((5,)),
+            dma((5,)),
+        ],
+        compiler_params=pltpu.CompilerParams(collective_id=cid, has_side_effects=True, vmem_limit_bytes=LIMIT),
+        name="scatter_last",
+    )(p, x)
+
+
+def scatter_line(me, p_ref, out_ref, from_b, from_a, from_z, send_sem, recv_sem):
+    rows = p_ref.shape[1]
+    low = me.z < 2
+    depth = jnp.where(low, me.z, 3 - me.z)
+    away = jnp.where(low, 1, 0)
+    items = [(t, jnp.where(low, t, 3 - t)) for t in (3, 2, 1, 0)]
+
+    def copy(src, dst, slot, to):
+        return me.copy(src, dst, send_sem.at[slot], recv_sem.at[slot], to)
+
+    def send_b(g, z):
+        return copy(p_ref.at[me.at_z(z) + me.db + g * me.da], from_b.at[g, z], g * 4 + z, me.dp + me.db)
+
+    def send_a(z):
+        return copy(from_b.at[1, z], from_a.at[z], 8 + z, me.dp + me.da)
+
+    def send_z(z, up):
+        return copy(from_b.at[0, z], from_z.at[up, z], 12 + 4 * up + z, me.dp - 4 + 8 * up)
+
+    for _, z in items:
+        send_b(1, z).start()
+        send_b(0, z).start()
+    yield
+
+    def first(item):
+        _, z = item
+        send_b(1, z).wait_recv()
+        add_rows(from_b.at[1, z], (p_ref.at[me.at_z(z) + me.da], from_b.at[1, z]), rows)
+        send_a(z).start()
+
+    def second(item):
+        t, z = item
+        up = away if t else 1 - away
+        send_b(0, z).wait_recv()
+        send_a(z).wait_recv()
+        terms = (p_ref.at[me.at_z(z)], from_b.at[0, z], from_a.at[z])
+        joins = (depth == 1) & (t != 1) if t < 2 else depth == 1
+
+        def alone():
+            add_rows(from_b.at[0, z], terms, rows)
+
+        def join():
+            send_z(z, up).wait_recv()
+            add_rows(from_b.at[0, z], terms + (from_z.at[up, z],), rows)
+
+        pl.when(joins)(join)
+        pl.when(jnp.logical_not(joins))(alone)
+        pl.when((depth < t) if t else (depth == 1))(lambda: send_z(z, up).start())
+
+    yield from lagged(items, first, second, 1)
+    here = from_b.at[0, me.z]
+    pl.when(me.z > 0)(lambda: send_z(me.z, 1).wait_recv())
+    pl.when(me.z < 3)(lambda: send_z(me.z, 0).wait_recv())
+    pl.when(me.z == 0)(lambda: add_rows(out_ref, (here, from_z.at[0, me.z]), rows))
+    pl.when(me.z == 3)(lambda: add_rows(out_ref, (here, from_z.at[1, me.z]), rows))
+    pl.when(depth == 1)(lambda: add_rows(out_ref, (here, from_z.at[0, me.z], from_z.at[1, me.z]), rows))
+    yield
+    for z in range(4):
+        send_b(0, z).wait_send()
+        send_b(1, z).wait_send()
+        send_a(z).wait_send()
+        pl.when(me.z < z)(lambda: send_z(z, 1).wait_send())
+        pl.when(me.z > z)(lambda: send_z(z, 0).wait_send())
+
+
+def scatter_rows_kernel(number, *refs):
+    p_refs, out_refs = refs[:number], refs[number : 2 * number]
+    from_b, from_a, from_z, send_sem, recv_sem = refs[2 * number :]
+    me = Place()
+    me.greet(line=True, near=True)
+    run(
+        *(
+            scatter_line(me, p_refs[i], out_refs[i], from_b.at[i], from_a.at[i], from_z.at[i], send_sem.at[i], recv_sem.at[i])
+            for i in range(number)
+        )
+    )
+
+
+def scatter_dp(arrays, cid):
+    number = len(arrays)
+    _, rows, columns = arrays[0].shape
+    dtype = arrays[0].dtype
+    vmem = pl.BlockSpec(memory_space=pltpu.VMEM)
+    return pl.pallas_call(
+        functools.partial(scatter_rows_kernel, number),
+        out_shape=[jax.ShapeDtypeStruct((rows, columns), jnp.float32)] * number,
+        in_specs=[vmem] * number,
+        out_specs=[vmem] * number,
+        scratch_shapes=[
+            pltpu.VMEM((number, 2, 4, rows, columns), dtype),
+            pltpu.VMEM((number, 4, rows, columns), dtype),
+            pltpu.VMEM((number, 2, 4, rows, columns), dtype),
+            pltpu.SemaphoreType.DMA((number, 20)),
+            pltpu.SemaphoreType.DMA((number, 20)),
+        ],
+        compiler_params=pltpu.CompilerParams(collective_id=cid, has_side_effects=True, vmem_limit_bytes=LIMIT),
+        name="scatter_dp",
+    )(*arrays)
+
+
+def join_cores_kernel(number, *refs):
+    ins, outs = refs[:number], refs[number : 2 * number]
+    send_sem, recv_sem, copy_sem = refs[2 * number :]
+    me = Place()
+    me.greet(partner=True)
+    columns = ins[0].shape[1]
+    cols = pl.ds(pl.multiple_of(me.core * columns, 128), columns)
+    copies = []
+    for i, (src, dst) in enumerate(zip(ins, outs)):
+        copies.append(me.copy(src, dst.at[:, cols], send_sem.at[i], recv_sem.at[i], me.dp, 1 - me.core))
+        copies.append(pltpu.make_async_copy(src, dst.at[:, cols], copy_sem.at[i]))
+    for c in copies:
+        c.start()
+    for c in copies[1::2]:
+        c.wait()
+    other = pl.ds(pl.multiple_of((1 - me.core) * columns, 128), columns)
+    for i, (src, dst) in enumerate(zip(ins, outs)):
+        me.copy(src, dst.at[:, other], send_sem.at[i], recv_sem.at[i], me.dp, 1 - me.core).wait_recv()
+        copies[2 * i].wait_send()
+
+
+def join_cores(arrays, cid):
+    number = len(arrays)
+    rows, columns = arrays[0].shape
+    hbm, vmem = pl.BlockSpec(memory_space=pl.ANY), pl.BlockSpec(memory_space=pltpu.VMEM)
+    return pl.pallas_call(
+        functools.partial(join_cores_kernel, number),
+        out_shape=[jax.ShapeDtypeStruct((rows, 2 * columns), arrays[0].dtype)] * number,
+        in_specs=[vmem] * number,
+        out_specs=[hbm] * number,
+        scratch_shapes=[pltpu.SemaphoreType.DMA((number,))] * 3,
+        compiler_params=pltpu.CompilerParams(collective_id=cid, has_side_effects=True),
+        name="join_cores",
+    )(*arrays)
+
+
+def sum_cores_kernel(number, *refs):
+    ins, outs = refs[:number], refs[number : 2 * number]
+    held, send_sem, recv_sem = refs[2 * number :]
+    me = Place()
+    me.greet(partner=True)
+    rows, columns = outs[0].shape
+    chunks = send_sem.shape[1]
+    part = rows // chunks
+    cols = pl.ds(pl.multiple_of(me.core * columns, 128), columns)
+    other = pl.ds(pl.multiple_of((1 - me.core) * columns, 128), columns)
+
+    def send(i, k):
+        at = pl.ds(k * part, part)
+        return me.copy(ins[i].at[at, other], held.at[i, at], send_sem.at[i, k], recv_sem.at[i, k], me.dp, 1 - me.core)
+
+    every = [(i, k) for i in range(number) for k in range(chunks)]
+    for i, k in every:
+        send(i, k).start()
+    for i, k in every:
+        send(i, k).wait_recv()
+        at = pl.ds(k * part, part)
+        add_rows(outs[i].at[at], (ins[i].at[at, cols], held.at[i, at]), part, 64)
+    for i, k in every:
+        send(i, k).wait_send()
+
+
+def sum_cores(arrays, cid, chunks=4):
+    number = len(arrays)
+    rows, columns = arrays[0].shape[0], arrays[0].shape[1] // 2
+    vmem = pl.BlockSpec(memory_space=pltpu.VMEM)
+    return pl.pallas_call(
+        functools.partial(sum_cores_kernel, number),
+        out_shape=[jax.ShapeDtypeStruct((rows, columns), arrays[0].dtype)] * number,
+        in_specs=[vmem] * number,
+        out_specs=[vmem] * number,
+        scratch_shapes=[
+            pltpu.VMEM((number, rows, columns), arrays[0].dtype),
+            pltpu.SemaphoreType.DMA((number, chunks)),
+            pltpu.SemaphoreType.DMA((number, chunks)),
+        ],
+        compiler_params=pltpu.CompilerParams(collective_id=cid, has_side_effects=True, vmem_limit_bytes=LIMIT),
+        name="sum_cores",
+    )(*arrays)
+
+
+def per_device_any(
     tokens,
     cotangent,
     expert_ids,
@@ -374,9 +1048,131 @@
     )
 
 
+def per_device_relay(
+    tokens,
+    cotangent,
+    expert_ids,
+    gate_values,
+    w_query,
+    w_key,
+    w_value,
+    w_out,
+    w_gate,
+    w_up,
+    w_down,
+    attn_gain,
+    ffn_gain,
+    query_gain,
+    key_gain,
+):
+    dot = functools.partial(jnp.dot, preferred_element_type=jnp.float32)
+    dot_t = functools.partial(lax.dot_general, dimension_numbers=(((1,), (1,)), ((), ())), preferred_element_type=jnp.float32)
+    t_dot = functools.partial(lax.dot_general, dimension_numbers=(((0,), (0,)), ((), ())), preferred_element_type=jnp.float32)
+    low = jnp.bfloat16
+    rows, width = tokens.shape
+    head_dim = query_gain.shape[0]
+    experts = w_gate.shape[0]
+    core = lax.axis_index("tensor")
+    mine = lax.dynamic_slice_in_dim(expert_ids, core * rows, rows, 0)
+    values = lax.dynamic_slice_in_dim(gate_values, core * rows, rows, 0)
+    match = mine[None] == jnp.arange(experts, dtype=jnp.int32)[:, None, None]
+    gates = jnp.sum(jnp.where(match, values[None], 0.0), axis=2)
+    gates = jnp.broadcast_to(gates[:, None], (experts, 8, rows))
+
+    q_cols, kv_cols = w_query.shape[1] // 2, w_key.shape[1] // 2
+    w_out_rows = jnp.transpose(w_out)
+    halves = jnp.stack(
+        [
+            jnp.concatenate([w[:, h * (w.shape[1] // 2) : (h + 1) * (w.shape[1] // 2)] for w in (w_query, w_key, w_value, w_out_rows)], axis=1)
+            for h in range(2)
+        ]
+    )
+    swap_weights = functools.partial(lax.all_to_all, axis_name="dp", split_axis=0, concat_axis=1, tiled=True)
+    gate_mine, up_mine, down_mine = [swap_weights(w)[0] for w in (w_gate, w_up, jnp.transpose(w_down, (0, 2, 1)))]
+    weights, rows_grad, gates = gather_first(halves, cotangent, gates, 1)
+    weights, rows_grad, gates = weights.reshape(-1, weights.shape[2]), rows_grad.reshape(-1, width), gates[:, 0].reshape(-1, 1)
+    proj_cols = q_cols + 2 * kv_cols
+    w_proj, w_back = weights[:, :proj_cols], weights[:, proj_cols:]
+
+    residual = tokens.astype(jnp.float32)
+    inverse_one = rms_inverse(residual)
+    seq_normed = gather_four((residual * inverse_one * attn_gain).astype(low), 4).reshape(-1, width)
+    seq_len = 2 * rows
+    group = q_cols // head_dim
+    scale = head_dim ** (-0.5)
+    cosine, sine_table = rotary_tables(seq_len, head_dim)
+    proj = dot(seq_normed, w_proj)
+    query_raw = proj[:, :q_cols].reshape(2, seq_len, group, head_dim)
+    key_raw = proj[:, q_cols : q_cols + kv_cols].reshape(2, seq_len, 1, head_dim)
+    value_low = proj[:, q_cols + kv_cols :].astype(low).reshape(2, seq_len, head_dim)
+    query_inverse, key_inverse = rms_inverse(query_raw), rms_inverse(key_raw)
+    query_low = (rotate(query_raw * query_inverse * query_gain, cosine, sine_table) * scale).astype(low)
+    key_low = rotate(key_raw * key_inverse * key_gain, cosine, sine_table).astype(low)[:, :, 0]
+    causal = jnp.arange(seq_len)[:, None] >= jnp.arange(seq_len)[None, :]
+    scores = jnp.einsum("bqgd,bsd->bgqs", query_low, key_low, preferred_element_type=jnp.float32)
+    exp_scores = jnp.where(causal, jnp.exp(scores), 0.0)
+    probs = exp_scores / jnp.sum(exp_scores, axis=-1, keepdims=True)
+    probs_low = probs.astype(low)
+    mixed = jnp.einsum("bgqs,bsd->bqgd", probs_low, value_low, preferred_element_type=jnp.float32).astype(low).reshape(2 * seq_len, q_cols)
+    hidden = residual + scatter_four(dot_t(mixed, w_back).astype(low).reshape(2, 2, rows, width), 5)
+    inverse_two = rms_inverse(hidden)
+    rows_in = gather_dp((hidden * inverse_two * ffn_gain).astype(low), 6).reshape(-1, width)
+    gate_full, up_full, down_full = join_cores((gate_mine, up_mine, down_mine), 2)
+
+    gate_pre = dot(rows_in, gate_full)
+    up_pre = dot(rows_in, up_full)
+    sigmoid_gate = jax.nn.sigmoid(gate_pre)
+    act = (gate_pre * sigmoid_gate * up_pre).astype(low)
+    expert_out = (dot_t(act, down_full) * gates).astype(low)
+    grad_out = (rows_grad.astype(jnp.float32) * gates).astype(low)
+    grad_act = dot(grad_out, down_full)
+    grad_gate = (grad_act * up_pre * sigmoid_gate * (1.0 + gate_pre * (1.0 - sigmoid_gate))).astype(low)
+    grad_up = (grad_act * gate_pre * sigmoid_gate).astype(low)
+    grad_in = (dot_t(grad_gate, gate_full) + dot_t(grad_up, up_full)).astype(low)
+    moe, grad_two = scatter_dp([v.reshape(-1, rows, width) for v in (expert_out, grad_in)], 7)
+    w_gate_part = t_dot(rows_in, grad_gate).astype(low)
+    w_up_part = t_dot(rows_in, grad_up).astype(low)
+    w_down_part = t_dot(grad_out, act).astype(low)
+    owned = sum_cores((w_gate_part, w_up_part, w_down_part), 8)
+    swap_grads = functools.partial(lax.all_to_all, axis_name="dp", split_axis=0, concat_axis=0, tiled=True)
+    grad_w_gate, grad_w_up, grad_w_down = [swap_grads(v.reshape(experts, rows, -1)).astype(jnp.float32) for v in owned]
+    grad_w_down = jnp.transpose(grad_w_down, (0, 2, 1))
+
+    output = (hidden + moe).astype(low)
+    ffn_gain_part = jnp.sum(grad_two * hidden * inverse_two, axis=0)
+    grad_hidden = cotangent.astype(jnp.float32) + norm_backward(grad_two, hidden, inverse_two, ffn_gain)
+    grad_attn = gather_four(grad_hidden.astype(low), 9).reshape(-1, width)
+    grad_mixed = dot(grad_attn, w_back).astype(low).reshape(2, seq_len, group, head_dim)
+    grad_probs = jnp.einsum("bqgd,bsd->bgqs", grad_mixed, value_low, preferred_element_type=jnp.float32)
+    delta_sum = jnp.sum(grad_probs * probs, axis=-1, keepdims=True)
+    grad_scores = (probs * (grad_probs - delta_sum)).astype(low)
+    grad_query = jnp.einsum("bgqs,bsd->bqgd", grad_scores, key_low, preferred_element_type=jnp.float32)
+    grad_key = jnp.einsum("bgqs,bqgd->bsd", grad_scores, query_low, preferred_element_type=jnp.float32)
+    grad_value = jnp.einsum("bgqs,bqgd->bsd", probs_low, grad_mixed, preferred_element_type=jnp.float32)
+    grad_query_norm = rotate_back(grad_query * scale, cosine, sine_table)
+    query_gain_part = jnp.sum(grad_query_norm * query_raw * query_inverse, axis=(0, 1, 2))
+    grad_query_low = norm_backward(grad_query_norm, query_raw, query_inverse, query_gain).astype(low)
+    grad_key_norm = rotate_back(grad_key[:, :, None], cosine, sine_table)
+    key_gain_part = jnp.sum(grad_key_norm * key_raw * key_inverse, axis=(0, 1, 2))
+    grad_key_low = norm_backward(grad_key_norm, key_raw, key_inverse, key_gain).astype(low)
+    grad_proj = jnp.concatenate([v.astype(low).reshape(2 * seq_len, -1) for v in (grad_query_low, grad_key_low, grad_value)], axis=1)
+    grad_one = scatter_four(dot_t(grad_proj, w_proj).astype(low).reshape(2, 2, rows, width), 10)
+    w_parts = jnp.concatenate([t_dot(seq_normed, grad_proj), t_dot(grad_attn, mixed)], axis=1).astype(low)
+    attn_gain_part = jnp.sum(grad_one * residual * inverse_one, axis=0)
+    gains = jnp.concatenate([attn_gain_part, ffn_gain_part, query_gain_part, key_gain_part])
+    gains = jnp.pad(gains, (0, -gains.shape[0] % 1024)).reshape(-1, 128)
+    shares, totals = scatter_last(w_parts.reshape(-1, rows, w_parts.shape[1]), gains, 11)
+    shares, totals = shares.astype(jnp.float32), totals.reshape(-1)
+    stops = (0, q_cols, q_cols + kv_cols, proj_cols, proj_cols + q_cols)
+    grads = [jnp.concatenate([shares[0, :, a:b], shares[1, :, a:b]], axis=1) for a, b in zip(stops, stops[1:])]
+    grad_tokens = (grad_hidden + norm_backward(grad_one, residual, inverse_one, attn_gain)).astype(low)
+    totals = jnp.split(totals, (width, 2 * width, 2 * width + head_dim, 2 * width + 2 * head_dim))[:4]
+    return (output, grad_tokens, grads[0], grads[1], grads[2], jnp.transpose(grads[3]), grad_w_gate, grad_w_up, grad_w_down, *totals)
+
+
 def solution(mesh):
     return jax.shard_map(
-        per_device,
+        per_device_relay if tuple(mesh.shape.values()) == (16, 2) else per_device_any,
         mesh=mesh,
         in_specs=(
             P(("dp", "tensor"), None),

time: 2100 us -> 981 us (0.47)
  waiting for transfers between devices: 1170 us -> 24 us
  Pallas kernels: 0 us -> 678 us
  blocking collectives: 237 us -> 0 us
  other arithmetic: 252 us -> 55.6 us
  starting transfers between devices: 154 us -> 36.5 us
  local copies, waits for them, and re-layouts: 132 us -> 36 us
    pallas_call x0 -> x10, Pallas kernels: none -> 678 us  [the longest x1 173 us: scatter_dp(): pl.pallas_call(functools.partial(scatter_rows_kernel, number), out_shape=...]
    all_to_all x7 -> x6, waiting for transfers between devices: 525 us -> 24 us  [the longest x3 24 us: per_device_relay(): swap_weights(w)[0]]
    all_gather x8 -> x0, waiting for transfers between devices: 390 us -> none  [the longest x1 145 us: per_device(): lax.all_gather(w_out, 'dp', axis=1, tiled=True)]
    reduce_scatter x5 -> x0, waiting for transfers between devices: 249 us -> none  [the longest x1 237 us: per_device(): lax.psum_scatter(jnp.concatenate([first_part, second], axis=1), 'dp', sca...]
    all_to_all x1 -> x0, blocking collectives: 197 us -> none  [per_device(): lax.all_to_all(grad_cols[None].astype(jnp.bfloat16), 'dp', split_axis=1,...]
    all_to_all x7 -> x6, starting transfers between devices: 153 us -> 36.5 us  [the longest x3 21.8 us: per_device_relay(): swap_weights(w)[0]]
    unnamed x4 -> x2, other arithmetic: 102 us -> 0.01 us
    scatter-add x2 -> x0, other arithmetic: 70.4 us -> none  [the longest x1 35.5 us: per_device(): grad_acc = empty_rows.at[flat_slots].add(back_grad)]
  transfers between devices with their start and end apart: 20 -> 6, of which waited for: 16 -> 1; matrix products, arithmetic and copies ran while one was open for 22% -> 14% of each run, Pallas kernels for 0% -> 68%
where the time goes in v2:
time: 981 us; the launch traced here: 967 us
  Pallas kernels  678 us (69%)
  matrix products  135 us (14%)
  other arithmetic  55.6 us (6%)
  starting transfers between devices  36.5 us (4%)
  local copies, waits for them, and re-layouts  36 us (4%)
  waiting for transfers between devices  24 us (2%)
    pallas_call x1, Pallas kernels, scatter_dp(): pl.pallas_call(functools.partial(scatter_rows_kernel, number), out_shape=...  173 us
    pallas_call x1, Pallas kernels, gather_first(): pl.pallas_call(gather_first_kernel, out_shape=[jax.ShapeDtypeStruct((16,)...  158 us
    pallas_call x1, Pallas kernels, scatter_last(): pl.pallas_call(functools.partial(scatter_last_kernel, chunks), out_shape=...  127 us
    pallas_call x1, Pallas kernels, gather_dp(): pl.pallas_call(gather_rows_kernel, out_shape=jax.ShapeDtypeStruct((16,) +...  73 us
    pallas_call x2, Pallas kernels, scatter_four(): pl.pallas_call(scatter_four_kernel, out_shape=jax.ShapeDtypeStruct((rows,...  66.6 us
    pallas_call x2, Pallas kernels, gather_four(): pl.pallas_call(gather_four_kernel, out_shape=jax.ShapeDtypeStruct((2, 2,...  55.9 us
    all_to_all x3, waiting for transfers between devices, per_device_relay(): swap_weights(w)[0]  24 us
    all_to_all x3, starting transfers between devices, per_device_relay(): swap_weights(w)[0]  21.8 us
  transfers between devices with their start and end apart: 6, of which 1 were waited for; matrix products, arithmetic and copies ran while one was open for 14% of the time, Pallas kernels for 68%

profile of v2, /device:TPU:0, one launch (start us, length us, event | category | flops | bytes accessed | tf_op | source)
XLA Modules:
  0.0 966.7 jit_solution(16985422948336216664)
XLA Ops:
  0.7 8.5 all-to-all-start.2
  11.4 39.4 %gather_four.2 = bf16[2,2,128,2048]{3,2,1,0:T(8,128)(2,1)} custom-call(bf16[128,2048]{1,0:T(8,128)(2,1)} %fusion.37.x_ref), custom_call_target="tpu_custom_call" | custom-call | tf_op jit(solution)/shard_map/gather_four/pallas_call | solution.py:238
  52.8 158.1 %gather_first.1 = (bf16[16,128,2304]{2,1,0:T(8,128)(2,1)}, bf16[16,128,2048]{2,1,0:T(8,128)(2,1)}, f32[16,8,128]{2,1,0:T(8,128)}) custom-call(bf16[2,128,2304]{2,1,0:T(8,128)(2,1)} %pad_maximum_fusion.3.w_ref, bf16[128,2048]{1,0:T(8,128)(2,1)} %c_ref.1, f32[16,8,128]{2,1,0:T(8,128)} %broadcast_in_dim.24.g_ref), custom_call_target="tpu_custom_call" | custom-call | tf_op jit(solution)/shard_map/gather_first/pallas_call | solution.py:476
  235.0 24.0 %all-to-all-done = bf16[16,128,384]{2,1,0:T(8,128)(2,1)} async-done(((bf16[16,128,384]{2,1,0:T(8,128)(2,1)}), bf16[16,128,384]{2,1,0:T(8,128)(2,1)}, u32[]{:S(2)}, u32[]{:S(2)}) %all-to-all-start) | async-done | bytes 1572896 | tf_op jit(solution)/shard_map/all_to_all | solution.py:1091
  259.0 8.8 all-to-all-start.1
  273.8 33.6 %scatter_four.2 = f32[128,2048]{1,0:T(8,128)} custom-call(bf16[2,2,128,2048]{3,2,1,0:T(8,128)(2,1)} %bitcast.236), custom_call_target="tpu_custom_call" | custom-call | tf_op jit(solution)/shard_map/scatter_four/pallas_call | solution.py:276
  310.8 73.0 %gather_dp.1 = bf16[16,128,2048]{2,1,0:T(8,128)(2,1)} custom-call(bf16[128,2048]{1,0:T(8,128)(2,1)} %multiply_convert_fusion.4.x_ref), custom_call_target="tpu_custom_call" | custom-call | tf_op jit(solution)/shard_map/gather_dp/pallas_call | solution.py:512
  388.5 8.1 fusion
  399.2 10.5 %join_cores.1 = (bf16[2048,768]{1,0:T(8,128)(2,1)}, bf16[2048,768]{1,0:T(8,128)(2,1)}, bf16[2048,768]{1,0:T(8,128)(2,1)}) custom-call(bf16[2048,384]{1,0:T(8,128)(2,1)} %bitcast.16.refs_0_, bf16[2048,384]{1,0:T(8,128)(2,1)} %bitcast.17.refs_1_, bf16[2048,384]{1,0:T(8,128)(2,1)} %bitcast.230), custom_call_target="tpu_custom_call" | custom-call | tf_op jit(solution)/shard_map/join_cores/pallas_call | solution.py:758
  409.7 11.8 %fusion.69 = f32[2048,768]{1,0:T(8,128)} fusion(bf16[2048,2048]{1,0:T(8,128)(2,1)} %bitcast.220, bf16[2048,768]{1,0:T(8,128)(2,1)} %get-tuple-element.27), kind=kOutput, calls=%fused_computation.163 | convolution fusion | flops 6442450944 | bytes 17825792 | tf_op jit(solution)/shard_map/dot_general | solution.py:1122
  421.5 10.9 %fusion.70 = f32[2048,768]{1,0:T(8,128)} fusion(bf16[2048,2048]{1,0:T(8,128)(2,1)} %bitcast.221, bf16[2048,768]{1,0:T(8,128)(2,1)S(1)} %copy-done.62), kind=kOutput, calls=%fused_computation.164 | convolution fusion | flops 6442450944 | bytes 17825792 | tf_op jit(solution)/shard_map/dot_general | solution.py:1123
  432.4 14.9 %multiply_convert_fusion.1 = (bf16[2048,768]{1,0:T(8,128)(2,1)}, bf16[2048,768]{1,0:T(8,128)(2,1)}, bf16[2048,768]{1,0:T(8,128)(2,1)}) fusion(f32[2048,768]{1,0:T(8,128)} %fusion.69, f32[2048,768]{1,0:T(8,128)} %fusion.70, bf16[2048,2048]{1,0:T(8,128)(2,1)S(1)} %bitcast.229, bf16[2048,768]{1,0:T(8,128)(2,1)} %get-tuple-element.29), kind=kOutput, calls=%fused_computation.5 | convolution fusion | flops 6467616768 | bytes 33554432 | tf_op jit(solution)/shard_map/dot_general | solution.py:1128
  447.2 10.7 %convolution_convert_fusion.3.refs_0_ = bf16[2048,768]{1,0:T(8,128)(2,1)} fusion(bf16[2048,2048]{1,0:T(8,128)(2,1)S(1)} %bitcast.224, bf16[2048,768]{1,0:T(8,128)(2,1)} %get-tuple-element.130), kind=kOutput, calls=%fused_computation.28 | convolution fusion | flops 6444023808 | bytes 14680064 | tf_op jit(solution)/shard_map/dot_general | solution.py:1133
  457.9 9.6 fusion.71
  467.5 8.5 convolution_convert_fusion.1.refs_2_
  476.0 9.2 multiply_convert_fusion
  485.1 8.7 convolution_convert_fusion.2.refs_1_
  493.9 14.2 %sum_cores.1 = (bf16[2048,384]{1,0:T(8,128)(2,1)}, bf16[2048,384]{1,0:T(8,128)(2,1)}, bf16[2048,384]{1,0:T(8,128)(2,1)}) custom-call(bf16[2048,768]{1,0:T(8,128)(2,1)} %convolution_convert_fusion.3.refs_0_, bf16[2048,768]{1,0:T(8,128)(2,1)} %convolution_convert_fusion.2.refs_1_, bf16[2048,768]{1,0:T(8,128)(2,1)} %convolution_convert_fusion.1.refs_2_), custom_call_target="tpu_custom_call" | custom-call | tf_op jit(solution)/shard_map/sum_cores/pallas_call | solution.py:799
  515.1 13.8 %add_convert_fusion = bf16[2048,2048]{1,0:T(8,128)(2,1)} fusion(f32[2048,2048]{1,0:T(8,128)} %fusion.71, bf16[2048,768]{1,0:T(8,128)(2,1)} %get-tuple-element.129, bf16[2048,768]{1,0:T(8,128)(2,1)} %get-tuple-element.28), kind=kOutput, calls=%fused_computation.2 | convolution fusion | flops 6450839552 | bytes 31457280 | tf_op jit(solution)/shard_map/dot_general | solution.py:1131
  528.8 172.8 %scatter_dp.1 = (f32[128,2048]{1,0:T(8,128)}, f32[128,2048]{1,0:T(8,128)}) custom-call(bf16[16,128,2048]{2,1,0:T(8,128)(2,1)} %bitcast.226, bf16[16,128,2048]{2,1,0:T(8,128)(2,1)} %bitcast.227), custom_call_target="tpu_custom_call" | custom-call | tf_op jit(solution)/shard_map/scatter_dp/pallas_call | solution.py:716
  707.1 16.5 %gather_four.3 = bf16[2,2,128,2048]{3,2,1,0:T(8,128)(2,1)} custom-call(bf16[128,2048]{1,0:T(8,128)(2,1)} %get-tuple-element.125.x_ref), custom_call_target="tpu_custom_call" | custom-call | tf_op jit(solution)/shard_map/gather_four/pallas_call | solution.py:238
  753.6 6.6 fusion.17
  760.2 33.0 %scatter_four.3 = f32[128,2048]{1,0:T(8,128)} custom-call(bf16[2,2,128,2048]{3,2,1,0:T(8,128)(2,1)} %bitcast.237), custom_call_target="tpu_custom_call" | custom-call | tf_op jit(solution)/shard_map/scatter_four/pallas_call | solution.py:276
  815.6 126.8 %scatter_last.1 = (bf16[2,128,2304]{2,1,0:T(8,128)(2,1)}, f32[40,128]{1,0:T(8,128)}) custom-call(bf16[16,128,2304]{2,1,0:T(8,128)(2,1)} %pad_maximum_fusion.p_ref, f32[40,128]{1,0:T(8,128)} %fusion.56.x_ref), custom_call_target="tpu_custom_call" | custom-call | tf_op jit(solution)/shard_map/scatter_last/pallas_call | solution.py:613
  (247 shorter events, 132.8 us)
Async XLA Ops:
  0.7 219.6 %all-to-all-start.2 = ((bf16[16,128,384]{1,2,0:T(8,128)(2,1)}), bf16[16,128,384]{1,2,0:T(8,128)(2,1)}, u32[]{:S(2)}, u32[]{:S(2)}) async-start(bf16[16,128,384]{1,2,0:T(8,128)(2,1)} %bitcast.241), calls=%async_computation.2 | async-start | bytes 3145728 | tf_op jit(solution)/shard_map/all_to_all | solution.py:1091
  9.3 41.6 %copy-start.47 = (bf16[128,256]{1,0:T(8,128)(2,1)S(1)}, bf16[128,256]{1,0:T(8,128)(2,1)}, u32[]{:S(2)}) copy-start(bf16[128,256]{1,0:T(8,128)(2,1)} %param.21) | copy-start | bytes 196612
  9.3 41.6 %copy-start.38 = (bf16[128,2048]{1,0:T(8,128)(2,1)S(1)}, bf16[128,2048]{1,0:T(8,128)(2,1)}, u32[]{:S(2)}) copy-start(bf16[128,2048]{1,0:T(8,128)(2,1)} %param.19) | copy-start | bytes 1572868
  51.0 160.0 %copy-start.17 = (bf16[2,2,128,2048]{3,2,1,0:T(8,128)(2,1)S(1)}, bf16[2,2,128,2048]{3,2,1,0:T(8,128)(2,1)}, u32[]{:S(2)}) copy-start(bf16[2,2,128,2048]{3,2,1,0:T(8,128)(2,1)} %gather_four.2) | copy-start | bytes 6291460
  216.4 13.5 %copy-start.39 = (bf16[512,128]{1,0:T(8,128)(2,1)}, bf16[512,128]{1,0:T(8,128)(2,1)S(1)}, u32[]{:S(2)}) copy-start(bf16[512,128]{1,0:T(8,128)(2,1)S(1)} %slice.204) | copy-start | bytes 393220
  220.3 38.7 %all-to-all-start = ((bf16[16,128,384]{2,1,0:T(8,128)(2,1)}), bf16[16,128,384]{2,1,0:T(8,128)(2,1)}, u32[]{:S(2)}, u32[]{:S(2)}) async-start(bf16[16,128,384]{2,1,0:T(8,128)(2,1)} %param.23), calls=%async_computation | async-start | bytes 3145728 | tf_op jit(solution)/shard_map/all_to_all | solution.py:1091
  259.0 140.1 %all-to-all-start.1 = ((bf16[16,128,384]{2,1,0:T(8,128)(2,1)}), bf16[16,128,384]{2,1,0:T(8,128)(2,1)}, u32[]{:S(2)}, u32[]{:S(2)}) async-start(bf16[16,128,384]{2,1,0:T(8,128)(2,1)} %param.24), calls=%async_computation.1 | async-start | bytes 3145728 | tf_op jit(solution)/shard_map/all_to_all | solution.py:1091
  273.8 36.0 %copy-start.41 = (f32[2048]{0:T(1024)S(1)}, f32[2048]{0:T(1024)}, u32[]{:S(2)}) copy-start(f32[2048]{0:T(1024)} %param.27) | copy-start | bytes 24580
  310.7 74.7 %copy-start.18 = (bf16[2,2,128,2048]{3,2,1,0:T(8,128)(2,1)S(1)}, bf16[2,2,128,2048]{3,2,1,0:T(8,128)(2,1)}, u32[]{:S(2)}) copy-start(bf16[2,2,128,2048]{3,2,1,0:T(8,128)(2,1)} %gather_four.2) | copy-start | bytes 6291460
  409.6 11.8 %copy-start.62 = (bf16[2048,768]{1,0:T(8,128)(2,1)S(1)}, bf16[2048,768]{1,0:T(8,128)(2,1)}, u32[]{:S(2)}) copy-start(bf16[2048,768]{1,0:T(8,128)(2,1)} %get-tuple-element.28) | copy-start | bytes 9437188
  409.7 22.7 %slice-start.2 = ((s8[8388608]{0:T(1024)(128)(4,1)}), s8[4194304]{0:T(1024)(128)(4,1)S(1)}, s32[]{:S(2)}) async-start(s8[8388608]{0:T(1024)(128)(4,1)} %bitcast.228), calls=%async_computation.8 | async-start | bytes 8388608
  421.5 10.9 %slice-start.3 = ((s8[8388608]{0:T(1024)(128)(4,1)}), s8[4194304]{0:T(1024)(128)(4,1)S(1)}, s32[]{:S(2)}) async-start(s8[8388608]{0:T(1024)(128)(4,1)} %bitcast.228), calls=%async_computation.9 | async-start | bytes 8388608
  421.5 25.7 %slice-start = ((s8[8388608]{0:T(1024)(128)(4,1)}), s8[4194304]{0:T(1024)(128)(4,1)S(1)}, s32[]{:S(2)}) async-start(s8[8388608]{0:T(1024)(128)(4,1)} %bitcast.222), calls=%async_computation.6 | async-start | bytes 8388608
  432.4 14.9 %slice-start.1 = ((s8[8388608]{0:T(1024)(128)(4,1)}), s8[4194304]{0:T(1024)(128)(4,1)S(1)}, s32[]{:S(2)}) async-start(s8[8388608]{0:T(1024)(128)(4,1)} %bitcast.222), calls=%async_computation.7 | async-start | bytes 8388608
  447.2 10.7 %copy-start.64 = (bf16[2048,768]{1,0:T(8,128)(2,1)S(1)}, bf16[2048,768]{1,0:T(8,128)(2,1)}, u32[]{:S(2)}) copy-start(bf16[2048,768]{1,0:T(8,128)(2,1)} %get-tuple-element.27) | copy-start | bytes 9437188
  447.2 10.7 %copy-start.65 = (bf16[2048,768]{1,0:T(8,128)(2,1)S(1)}, bf16[2048,768]{1,0:T(8,128)(2,1)}, u32[]{:S(2)}) copy-start(bf16[2048,768]{1,0:T(8,128)(2,1)} %get-tuple-element.130) | copy-start | bytes 9437188
  510.6 237.2 %all-to-all-start.5 = ((bf16[16,128,384]{1,2,0:T(8,128)(2,1)}), bf16[16,128,384]{1,2,0:T(8,128)(2,1)}, u32[]{:S(2)}, u32[]{:S(2)}) async-start(bf16[16,128,384]{1,2,0:T(8,128)(2,1)} %copy.173), calls=%async_computation.5 | async-start | bytes 3145728 | tf_op jit(solution)/shard_map/all_to_all | solution.py:1138
  528.8 174.7 %copy-start.24 = (bf16[128,2048]{1,0:T(8,128)(2,1)S(1)}, bf16[128,2048]{1,0:T(8,128)(2,1)}, u32[]{:S(2)}) copy-start(bf16[128,2048]{1,0:T(8,128)(2,1)} %c_ref.1) | copy-start | bytes 1572868
  528.8 174.7 %copy-start.61 = (f32[128]{0:T(128)S(1)}, f32[128]{0:T(128)}, u32[]{:S(2)}) copy-start(f32[128]{0:T(128)} %get-tuple-element.171) | copy-start | bytes 1540
  747.9 61.2 %all-to-all-start.3 = ((bf16[16,128,384]{2,1,0:T(8,128)(2,1)}), bf16[16,128,384]{2,1,0:T(8,128)(2,1)}, u32[]{:S(2)}, u32[]{:S(2)}) async-start(bf16[16,128,384]{2,1,0:T(8,128)(2,1)} %bitcast.55), calls=%async_computation.3 | async-start | bytes 3145728 | tf_op jit(solution)/shard_map/all_to_all | solution.py:1138
  760.2 37.1 %copy-start.9 = (bf16[128,2048]{1,0:T(8,128)(2,1)S(1)}, bf16[128,2048]{1,0:T(8,128)(2,1)}, u32[]{:S(2)}) copy-start(bf16[128,2048]{1,0:T(8,128)(2,1)} %param.15) | copy-start | bytes 1572868
  760.2 37.1 %copy-start.43 = (f32[2048]{0:T(1024)S(1)}, f32[2048]{0:T(1024)}, u32[]{:S(2)}) copy-start(f32[2048]{0:T(1024)} %param.26) | copy-start | bytes 24580
  760.2 37.1 %copy-start.56 = (f32[128]{0:T(128)S(1)}, f32[128]{0:T(128)}, u32[]{:S(2)}) copy-start(f32[128]{0:T(128)} %copy-done.55) | copy-start | bytes 1540
  809.1 154.0 %all-to-all-start.4 = ((bf16[16,128,384]{2,1,0:T(8,128)(2,1)}), bf16[16,128,384]{2,1,0:T(8,128)(2,1)}, u32[]{:S(2)}, u32[]{:S(2)}) async-start(bf16[16,128,384]{2,1,0:T(8,128)(2,1)} %bitcast.56), calls=%async_computation.4 | async-start | bytes 3145728 | tf_op jit(solution)/shard_map/all_to_all | solution.py:1138
  (54 other events, 234.1 us)

commit v3 on v2

--- a/solution.py
+++ b/solution.py
@@ -498,28 +498,6 @@
     )(weights, rows, gates)
 
 
-def gather_rows_kernel(x_ref, out_ref, own, send_sem, recv_sem, copy_sem):
-    me = Place()
-    end = keep_own(x_ref, own, out_ref.at[me.dp], copy_sem)
-    me.greet(line=True, near=True)
-    run(gather_line(me, x_ref, out_ref, send_sem, recv_sem))
-    end()
-
-
-def gather_dp(x, cid):
-    hbm = pl.BlockSpec(memory_space=pl.ANY)
-    dma = pltpu.SemaphoreType.DMA
-    return pl.pallas_call(
-        gather_rows_kernel,
-        out_shape=jax.ShapeDtypeStruct((16,) + x.shape, x.dtype),
-        in_specs=[hbm],
-        out_specs=hbm,
-        scratch_shapes=[pltpu.VMEM(x.shape, x.dtype), dma((29,)), dma((16,)), dma((2,))],
-        compiler_params=pltpu.CompilerParams(collective_id=cid, has_side_effects=True),
-        name="gather_dp",
-    )(x)
-
-
 def scatter_pairs(me, chunks, p_ref, out_ref, from_b, from_a, from_far, send_sem, recv_sem):
     rows = p_ref.shape[1] // chunks
     other = me.dp + me.pair
@@ -630,185 +608,369 @@
     )(p, x)
 
 
-def scatter_line(me, p_ref, out_ref, from_b, from_a, from_z, send_sem, recv_sem):
-    rows = p_ref.shape[1]
+def experts_kernel(
+    x_ref, c_ref, g_ref, gate_ref, up_ref, down_ref,
+    moe_ref, two_ref, gu_out, down_out, xg_ref,
+    wgu, wd, ag, ggu, p, from_b, from_a, from_z, xb, cb,
+    g_send, g_recv, b_send, b_recv, a_send, a_recv, z_send, z_recv, w_send, w_recv, load_sem, tile_sem, keep_sem,
+):
+    me = Place()
+    rows, width = x_ref.shape
+    hidden = wd.shape[1]
+    half = hidden // 2
     low = me.z < 2
     depth = jnp.where(low, me.z, 3 - me.z)
     away = jnp.where(low, 1, 0)
-    items = [(t, jnp.where(low, t, 3 - t)) for t in (3, 2, 1, 0)]
-
-    def copy(src, dst, slot, to):
-        return me.copy(src, dst, send_sem.at[slot], recv_sem.at[slot], to)
-
-    def send_b(g, z):
-        return copy(p_ref.at[me.at_z(z) + me.db + g * me.da], from_b.at[g, z], g * 4 + z, me.dp + me.db)
-
-    def send_a(z):
-        return copy(from_b.at[1, z], from_a.at[z], 8 + z, me.dp + me.da)
-
-    def send_z(z, up):
-        return copy(from_b.at[0, z], from_z.at[up, z], 12 + 4 * up + z, me.dp - 4 + 8 * up)
-
-    for _, z in items:
-        send_b(1, z).start()
-        send_b(0, z).start()
-    yield
-
-    def first(item):
-        _, z = item
-        send_b(1, z).wait_recv()
-        add_rows(from_b.at[1, z], (p_ref.at[me.at_z(z) + me.da], from_b.at[1, z]), rows)
-        send_a(z).start()
-
-    def second(item):
-        t, z = item
-        up = away if t else 1 - away
-        send_b(0, z).wait_recv()
-        send_a(z).wait_recv()
-        terms = (p_ref.at[me.at_z(z)], from_b.at[0, z], from_a.at[z])
-        joins = (depth == 1) & (t != 1) if t < 2 else depth == 1
-
-        def alone():
-            add_rows(from_b.at[0, z], terms, rows)
-
-        def join():
-            send_z(z, up).wait_recv()
-            add_rows(from_b.at[0, z], terms + (from_z.at[up, z],), rows)
-
-        pl.when(joins)(join)
-        pl.when(jnp.logical_not(joins))(alone)
-        pl.when((depth < t) if t else (depth == 1))(lambda: send_z(z, up).start())
-
-    yield from lagged(items, first, second, 1)
-    here = from_b.at[0, me.z]
-    pl.when(me.z > 0)(lambda: send_z(me.z, 1).wait_recv())
-    pl.when(me.z < 3)(lambda: send_z(me.z, 0).wait_recv())
-    pl.when(me.z == 0)(lambda: add_rows(out_ref, (here, from_z.at[0, me.z]), rows))
-    pl.when(me.z == 3)(lambda: add_rows(out_ref, (here, from_z.at[1, me.z]), rows))
-    pl.when(depth == 1)(lambda: add_rows(out_ref, (here, from_z.at[0, me.z], from_z.at[1, me.z]), rows))
-    yield
-    for z in range(4):
-        send_b(0, z).wait_send()
-        send_b(1, z).wait_send()
-        send_a(z).wait_send()
-        pl.when(me.z < z)(lambda: send_z(z, 1).wait_send())
-        pl.when(me.z > z)(lambda: send_z(z, 0).wait_send())
-
-
-def scatter_rows_kernel(number, *refs):
-    p_refs, out_refs = refs[:number], refs[number : 2 * number]
-    from_b, from_a, from_z, send_sem, recv_sem = refs[2 * number :]
-    me = Place()
-    me.greet(line=True, near=True)
-    run(
-        *(
-            scatter_line(me, p_refs[i], out_refs[i], from_b.at[i], from_a.at[i], from_z.at[i], send_sem.at[i], recv_sem.at[i])
-            for i in range(number)
+    dot = functools.partial(jnp.dot, preferred_element_type=jnp.float32)
+    dot_t = functools.partial(lax.dot_general, dimension_numbers=(((1,), (1,)), ((), ())), preferred_element_type=jnp.float32)
+    t_dot = functools.partial(lax.dot_general, dimension_numbers=(((0,), (0,)), ((), ())), preferred_element_type=jnp.float32)
+    upper, lower = pl.ds(rows, rows), pl.ds(0, rows)
+
+    def z_of(m):
+        t = jnp.where(m == 0, 1 - depth, jnp.where(m == 1, 2, jnp.where(m == 2, 3, depth)))
+        return jnp.where(low, t, 3 - t)
+
+    def block(n):
+        return me.at_z(z_of(n // 2)) + (n % 2) * me.da
+
+    def part(source, to, slot, own=False):
+        return me.copy(x_ref if own else xg_ref.at[source], xg_ref.at[source], g_send.at[slot], g_recv.at[source], to)
+
+    def onward(m):
+        below = z_of(m) < me.z
+        return jnp.logical_or(jnp.logical_and(below, me.z < 3), jnp.logical_and(jnp.logical_not(below), me.z > 0)), jnp.where(below, 4, -4)
+
+    def arrive(m):
+        source = me.at_z(z_of(m))
+        part(source, me.dp, 0).wait_recv()
+        goes, step = onward(m)
+        pl.when(goes)(lambda: part(source, me.dp + step, 4 + 3 * m).start())
+        part(source, me.dp + me.db, 6 + 3 * m).start()
+        part(source, me.dp + me.da, 5 + 3 * m).start()
+
+    def arrive_a(m):
+        source = me.at_z(z_of(m)) + me.da
+        part(source, me.dp, 0).wait_recv()
+        part(source, me.dp + me.db, 13 + m).start()
+
+    def loads(n):
+        slot = n % 2
+        copies = []
+        for j, source in enumerate((block(n), block(n) + me.db)):
+            at = pl.ds(j * rows, rows)
+            copies.append(pltpu.make_async_copy(xg_ref.at[source], xb.at[slot, at], load_sem.at[slot, j]))
+            copies.append(pltpu.make_async_copy(c_ref.at[source], cb.at[slot, at], load_sem.at[slot, 2 + j]))
+        return copies
+
+    def fetch(n):
+        part(block(n) + me.db, me.dp, 0).wait_recv()
+        for c in loads(n):
+            c.start()
+
+    def send_b(i, n):
+        return me.copy(p.at[i, n, upper], from_b.at[i, n], b_send.at[i, n], b_recv.at[i, n], me.dp + me.db)
+
+    def send_a(i, m):
+        return me.copy(from_b.at[i, 2 * m + 1], from_a.at[i, m], a_send.at[i, m], a_recv.at[i, m], me.dp + me.da)
+
+    def slot_z(z, up, at):
+        return jnp.where(up == 1, z, jnp.where(z == at, 4, z))
+
+    def send_z(i, m, up):
+        z = z_of(m)
+        slot = slot_z(z, up, me.z - 1)
+        return me.copy(from_b.at[i, 2 * m], from_z.at[i, slot], z_send.at[i, m], z_recv.at[i, slot], me.dp - 4 + 8 * up)
+
+    def wait_z(i, z, up):
+        slot = slot_z(z, up, me.z)
+        me.copy(from_z.at[i, slot], from_z.at[i, slot], z_send.at[i, 0], z_recv.at[i, slot], me.dp).wait_recv()
+        return from_z.at[i, slot]
+
+    def first(m):
+        for i in range(2):
+            n = 2 * m + 1
+            send_b(i, n).wait_recv()
+            add_rows(from_b.at[i, n], (p.at[i, n, lower], from_b.at[i, n]), rows)
+            send_a(i, m).start()
+
+    def second(m):
+        for i in range(2):
+            n = 2 * m
+            send_b(i, n).wait_recv()
+            send_a(i, m).wait_recv()
+            terms = (p.at[i, n, lower], from_b.at[i, n], from_a.at[i, m])
+            if m in (1, 2):
+                pl.when(depth == 0)(lambda: add_rows(from_b.at[i, n], terms, rows))
+                pl.when(depth == 1)(lambda: add_rows(from_b.at[i, n], terms + (wait_z(i, z_of(m), away),), rows))
+                send_z(i, m, away).start()
+            else:
+                add_rows(from_b.at[i, n], terms, rows)
+                if m == 0:
+                    pl.when(depth == 0)(lambda: send_z(i, 0, away).start())
+
+    own = p.at[1, 7, lower]
+    load = pltpu.make_async_copy(x_ref, own, keep_sem.at[0])
+    store = pltpu.make_async_copy(own, xg_ref.at[me.dp], keep_sem.at[1])
+    load.start()
+
+    def half_of(core):
+        at = core * half
+        return (
+            wgu.at[:, pl.ds(pl.multiple_of(at, 128), half)],
+            wgu.at[:, pl.ds(pl.multiple_of(hidden + at, 128), half)],
+            wd.at[:, pl.ds(pl.multiple_of(at, 128), half)],
         )
-    )
-
-
-def scatter_dp(arrays, cid):
-    number = len(arrays)
-    _, rows, columns = arrays[0].shape
-    dtype = arrays[0].dtype
-    vmem = pl.BlockSpec(memory_space=pltpu.VMEM)
+
+    mine = (gate_ref, up_ref, down_ref)
+    locals_ = [pltpu.make_async_copy(src, dst, keep_sem.at[2 + j]) for j, (src, dst) in enumerate(zip(mine, half_of(me.core)))]
+    for c in locals_:
+        c.start()
+    me.greet(line=True, near=True, partner=True)
+    pl.when(me.z < 3)(lambda: part(me.dp, me.dp + 4, 0, True).start())
+    pl.when(me.z > 0)(lambda: part(me.dp, me.dp - 4, 1, True).start())
+    part(me.dp, me.dp + me.db, 3, True).start()
+    part(me.dp, me.dp + me.da, 2, True).start()
+    shares = [
+        me.copy(src, dst, w_send.at[j], w_recv.at[j], me.dp, 1 - me.core) for j, (src, dst) in enumerate(zip(mine, half_of(me.core)))
+    ]
+    for c in shares:
+        c.start()
+    load.wait()
+    store.start()
+    arrive_a(3)
+    arrive(0)
+    store.wait()
+    for c in locals_:
+        c.wait()
+    for j, dst in enumerate(half_of(1 - me.core)):
+        me.copy(dst, dst, w_send.at[j], w_recv.at[j], me.dp).wait_recv()
+    fetch(0)
+
+    tile = 256
+
+    def step(n, _):
+        slot = n % 2
+        for c in loads(n):
+            c.wait()
+        gates = jnp.concatenate([g_ref[block(n)], g_ref[block(n) + me.db]], axis=0)
+
+        def inner(j, _):
+            at, at_up = pl.ds(pl.multiple_of(j * tile, tile), tile), pl.ds(pl.multiple_of(hidden + j * tile, tile), tile)
+            gate, up, grad = dot(xb[slot], wgu[:, at]), dot(xb[slot], wgu[:, at_up]), dot(cb[slot], wd[:, at]) * gates
+            sig = 1.0 / (1.0 + jnp.exp(-gate))
+            act = gate * sig
+            ag[n, :, at] = (act * up * gates).astype(ag.dtype)
+            ggu[n, :, at] = (grad * up * sig * (1.0 + gate * (1.0 - sig))).astype(ggu.dtype)
+            ggu[n, :, at_up] = (grad * act).astype(ggu.dtype)
+            return 0
+
+        lax.fori_loop(0, hidden // tile, inner, 0)
+
+        def at_step(k, *calls):
+            def go():
+                for call, m in calls:
+                    call(m)
+
+            pl.when(n == k)(go)
+
+        at_step(0, (arrive, 1), (arrive_a, 0))
+        at_step(1, (arrive, 2))
+        at_step(2, (arrive_a, 1))
+        at_step(3, (arrive_a, 2))
+        pl.when(n < 7)(lambda: fetch(n + 1))
+
+        def outer(j, _):
+            at = pl.ds(pl.multiple_of(j * 2 * tile, 2 * tile), 2 * tile)
+            p[0, n, :, at] = dot_t(ag[n], wd[at, :]).astype(p.dtype)
+            p[1, n, :, at] = dot_t(ggu[n], wgu[at, :]).astype(p.dtype)
+            return 0
+
+        lax.fori_loop(0, width // (2 * tile), outer, 0)
+        send_b(0, n).start()
+        send_b(1, n).start()
+        at_step(4, (first, 0))
+        at_step(6, (second, 0))
+        at_step(7, (first, 1))
+        return 0
+
+    lax.fori_loop(0, 8, step, 0)
+
+    def tiles(i):
+        slot = i % 2
+        cols = pl.ds(pl.multiple_of(i * tile, tile), tile)
+        copies = []
+        for which, src in enumerate((xg_ref, c_ref)):
+            to = pl.ds(pl.multiple_of((2 * which + slot) * tile, tile), tile)
+
+            def one(n, side, which=which, src=src, to=to):
+                at = pl.ds(pl.multiple_of((2 * n + side) * rows, rows), rows)
+                return pltpu.make_async_copy(src.at[block(n) + side * me.db, :, cols], wgu.at[at, to], tile_sem.at[which, slot, 2 * n + side])
+
+            copies.append(one)
+        return copies
+
+    def each_tile(i, act):
+        for one in tiles(i):
+
+            def body(n, _):
+                for side in (0, 1):
+                    act(one(n, side))
+                return 0
+
+            lax.fori_loop(0, 8, body, 0)
+
+    def outs(i):
+        slot = i % 2
+        at = pl.ds(pl.multiple_of(i * tile, tile), tile)
+        return (
+            pltpu.make_async_copy(xb.at[slot, :, pl.ds(0, 2 * hidden)], gu_out.at[at], load_sem.at[slot, 0]),
+            pltpu.make_async_copy(cb.at[slot, :, pl.ds(0, hidden)], down_out.at[at], load_sem.at[slot, 1]),
+        )
+
+    each_tile(0, lambda c: c.start())
+
+    def weight_step(i, _):
+        slot = i % 2
+        pl.when(i < 7)(lambda: each_tile(i + 1, lambda c: c.start()))
+        each_tile(i, lambda c: c.wait())
+
+        def free():
+            for c in outs(i - 2):
+                c.wait()
+
+        pl.when(i >= 2)(free)
+        x_tile = wgu[:, pl.ds(pl.multiple_of(slot * tile, tile), tile)]
+        xb[slot, :, pl.ds(0, 2 * hidden)] = t_dot(x_tile, ggu[...].reshape(-1, 2 * hidden)).astype(xb.dtype)
+        c_tile = wgu[:, pl.ds(pl.multiple_of((2 + slot) * tile, tile), tile)]
+        cb[slot, :, pl.ds(0, hidden)] = t_dot(c_tile, ag[...].reshape(-1, hidden)).astype(cb.dtype)
+        for c in outs(i):
+            c.start()
+        pl.when(i == 1)(lambda: second(1))
+        pl.when(i == 2)(lambda: first(2))
+        pl.when(i == 4)(lambda: second(2))
+        pl.when(i == 5)(lambda: first(3))
+        return 0
+
+    lax.fori_loop(0, 8, weight_step, 0)
+    second(3)
+
+    def pass_back():
+        for i in range(2):
+            add_rows(from_b.at[i, 0], (from_b.at[i, 0], wait_z(i, z_of(0), 1 - away)), rows)
+            send_z(i, 0, 1 - away).start()
+
+    pl.when(depth == 1)(pass_back)
+    for i, out_ref in enumerate((moe_ref, two_ref)):
+        here = from_b.at[i, 6]
+        pl.when(me.z == 0)(lambda: add_rows(out_ref, (here, wait_z(i, me.z, 0)), rows))
+        pl.when(me.z == 3)(lambda: add_rows(out_ref, (here, wait_z(i, me.z, 1)), rows))
+        pl.when(depth == 1)(lambda: add_rows(out_ref, (here, wait_z(i, me.z, 0), wait_z(i, me.z, 1)), rows))
+
+    for i in (6, 7):
+        for c in outs(i):
+            c.wait()
+    for c in shares:
+        c.wait_send()
+    pl.when(me.z < 3)(lambda: part(me.dp, me.dp, 0).wait_send())
+    pl.when(me.z > 0)(lambda: part(me.dp, me.dp, 1).wait_send())
+    part(me.dp, me.dp, 2).wait_send()
+    part(me.dp, me.dp, 3).wait_send()
+    for m in range(4):
+        if m < 3:
+            pl.when(onward(m)[0])(lambda: part(me.dp, me.dp, 4 + 3 * m).wait_send())
+            part(me.dp, me.dp, 5 + 3 * m).wait_send()
+            part(me.dp, me.dp, 6 + 3 * m).wait_send()
+        part(me.dp, me.dp, 13 + m).wait_send()
+        for i in range(2):
+            send_b(i, 2 * m).wait_send()
+            send_b(i, 2 * m + 1).wait_send()
+            send_a(i, m).wait_send()
+            if m < 3:
+                send_z(i, m, away).wait_send()
+
+
+def expert_layer(x, grads, gates, gate, up, down, cid):
+    rows, width = x.shape
+    half = gate.shape[1]
+    hbm, vmem = pl.BlockSpec(memory_space=pl.ANY), pl.BlockSpec(memory_space=pltpu.VMEM)
+    dma = pltpu.SemaphoreType.DMA
+    dtype = x.dtype
     return pl.pallas_call(
-        functools.partial(scatter_rows_kernel, number),
-        out_shape=[jax.ShapeDtypeStruct((rows, columns), jnp.float32)] * number,
-        in_specs=[vmem] * number,
-        out_specs=[vmem] * number,
+        experts_kernel,
+        out_shape=[
+            jax.ShapeDtypeStruct((rows, width), jnp.float32),
+            jax.ShapeDtypeStruct((rows, width), jnp.float32),
+            jax.ShapeDtypeStruct((width, 4 * half), dtype),
+            jax.ShapeDtypeStruct((width, 2 * half), dtype),
+            jax.ShapeDtypeStruct((16, rows, width), dtype),
+        ],
+        in_specs=[hbm, hbm, vmem, hbm, hbm, hbm],
+        out_specs=[vmem, vmem, hbm, hbm, hbm],
         scratch_shapes=[
-            pltpu.VMEM((number, 2, 4, rows, columns), dtype),
-            pltpu.VMEM((number, 4, rows, columns), dtype),
-            pltpu.VMEM((number, 2, 4, rows, columns), dtype),
-            pltpu.SemaphoreType.DMA((number, 20)),
-            pltpu.SemaphoreType.DMA((number, 20)),
+            pltpu.VMEM((width, 4 * half), dtype),
+            pltpu.VMEM((width, 2 * half), dtype),
+            pltpu.VMEM((8, 2 * rows, 2 * half), dtype),
+            pltpu.VMEM((8, 2 * rows, 4 * half), dtype),
+            pltpu.VMEM((2, 8, 2 * rows, width), dtype),
+            pltpu.VMEM((2, 8, rows, width), dtype),
+            pltpu.VMEM((2, 4, rows, width), dtype),
+            pltpu.VMEM((2, 5, rows, width), dtype),
+            pltpu.VMEM((2, 2 * rows, width), dtype),
+            pltpu.VMEM((2, 2 * rows, width), dtype),
+            dma((17,)), dma((16,)),
+            dma((2, 8)), dma((2, 8)),
+            dma((2, 4)), dma((2, 4)),
+            dma((2, 4)), dma((2, 5)),
+            dma((3,)), dma((3,)),
+            dma((2, 4)), dma((2, 2, 16)), dma((5,)),
         ],
-        compiler_params=pltpu.CompilerParams(collective_id=cid, has_side_effects=True, vmem_limit_bytes=LIMIT),
-        name="scatter_dp",
-    )(*arrays)
-
-
-def join_cores_kernel(number, *refs):
-    ins, outs = refs[:number], refs[number : 2 * number]
-    send_sem, recv_sem, copy_sem = refs[2 * number :]
+        compiler_params=pltpu.CompilerParams(collective_id=cid, has_side_effects=True, vmem_limit_bytes=67_043_328),
+        name="experts",
+    )(x, grads, gates, gate, up, down)
+
+
+def sum_cores_kernel(gu_ref, down_ref, gate_out, up_out, down_out, held, send_sem, recv_sem):
     me = Place()
     me.greet(partner=True)
-    columns = ins[0].shape[1]
-    cols = pl.ds(pl.multiple_of(me.core * columns, 128), columns)
-    copies = []
-    for i, (src, dst) in enumerate(zip(ins, outs)):
-        copies.append(me.copy(src, dst.at[:, cols], send_sem.at[i], recv_sem.at[i], me.dp, 1 - me.core))
-        copies.append(pltpu.make_async_copy(src, dst.at[:, cols], copy_sem.at[i]))
-    for c in copies:
-        c.start()
-    for c in copies[1::2]:
-        c.wait()
-    other = pl.ds(pl.multiple_of((1 - me.core) * columns, 128), columns)
-    for i, (src, dst) in enumerate(zip(ins, outs)):
-        me.copy(src, dst.at[:, other], send_sem.at[i], recv_sem.at[i], me.dp, 1 - me.core).wait_recv()
-        copies[2 * i].wait_send()
-
-
-def join_cores(arrays, cid):
-    number = len(arrays)
-    rows, columns = arrays[0].shape
-    hbm, vmem = pl.BlockSpec(memory_space=pl.ANY), pl.BlockSpec(memory_space=pltpu.VMEM)
-    return pl.pallas_call(
-        functools.partial(join_cores_kernel, number),
-        out_shape=[jax.ShapeDtypeStruct((rows, 2 * columns), arrays[0].dtype)] * number,
-        in_specs=[vmem] * number,
-        out_specs=[hbm] * number,
-        scratch_shapes=[pltpu.SemaphoreType.DMA((number,))] * 3,
-        compiler_params=pltpu.CompilerParams(collective_id=cid, has_side_effects=True),
-        name="join_cores",
-    )(*arrays)
-
-
-def sum_cores_kernel(number, *refs):
-    ins, outs = refs[:number], refs[number : 2 * number]
-    held, send_sem, recv_sem = refs[2 * number :]
-    me = Place()
-    me.greet(partner=True)
-    rows, columns = outs[0].shape
+    rows, half = gate_out.shape
     chunks = send_sem.shape[1]
     part = rows // chunks
-    cols = pl.ds(pl.multiple_of(me.core * columns, 128), columns)
-    other = pl.ds(pl.multiple_of((1 - me.core) * columns, 128), columns)
+    outs = (gate_out, up_out, down_out)
+
+    def view(i, at, core):
+        return (gu_ref, gu_ref, down_ref)[i].at[at, pl.ds(pl.multiple_of((2 * half if i == 1 else 0) + core * half, 128), half)]
 
     def send(i, k):
         at = pl.ds(k * part, part)
-        return me.copy(ins[i].at[at, other], held.at[i, at], send_sem.at[i, k], recv_sem.at[i, k], me.dp, 1 - me.core)
-
-    every = [(i, k) for i in range(number) for k in range(chunks)]
+        return me.copy(view(i, at, 1 - me.core), held.at[i, at], send_sem.at[i, k], recv_sem.at[i, k], me.dp, 1 - me.core)
+
+    every = [(i, k) for i in range(3) for k in range(chunks)]
     for i, k in every:
         send(i, k).start()
     for i, k in every:
         send(i, k).wait_recv()
         at = pl.ds(k * part, part)
-        add_rows(outs[i].at[at], (ins[i].at[at, cols], held.at[i, at]), part, 64)
+        add_rows(outs[i].at[at], (view(i, at, me.core), held.at[i, at]), part, 64)
     for i, k in every:
         send(i, k).wait_send()
 
 
-def sum_cores(arrays, cid, chunks=4):
-    number = len(arrays)
-    rows, columns = arrays[0].shape[0], arrays[0].shape[1] // 2
+def sum_cores(gu, down, cid, chunks=4):
+    rows, half = down.shape[0], down.shape[1] // 2
     vmem = pl.BlockSpec(memory_space=pltpu.VMEM)
     return pl.pallas_call(
-        functools.partial(sum_cores_kernel, number),
-        out_shape=[jax.ShapeDtypeStruct((rows, columns), arrays[0].dtype)] * number,
-        in_specs=[vmem] * number,
-        out_specs=[vmem] * number,
+        sum_cores_kernel,
+        out_shape=[jax.ShapeDtypeStruct((rows, half), down.dtype)] * 3,
+        in_specs=[vmem] * 2,
+        out_specs=[vmem] * 3,
         scratch_shapes=[
-            pltpu.VMEM((number, rows, columns), arrays[0].dtype),
-            pltpu.SemaphoreType.DMA((number, chunks)),
-            pltpu.SemaphoreType.DMA((number, chunks)),
+            pltpu.VMEM((3, rows, half), down.dtype),
+            pltpu.SemaphoreType.DMA((3, chunks)),
+            pltpu.SemaphoreType.DMA((3, chunks)),
         ],
         compiler_params=pltpu.CompilerParams(collective_id=cid, has_side_effects=True, vmem_limit_bytes=LIMIT),
         name="sum_cores",
-    )(*arrays)
+    )(gu, down)
 
 
 def per_device_any(
@@ -1090,7 +1252,7 @@
     swap_weights = functools.partial(lax.all_to_all, axis_name="dp", split_axis=0, concat_axis=1, tiled=True)
     gate_mine, up_mine, down_mine = [swap_weights(w)[0] for w in (w_gate, w_up, jnp.transpose(w_down, (0, 2, 1)))]
     weights, rows_grad, gates = gather_first(halves, cotangent, gates, 1)
-    weights, rows_grad, gates = weights.reshape(-1, weights.shape[2]), rows_grad.reshape(-1, width), gates[:, 0].reshape(-1, 1)
+    weights, gates = weights.reshape(-1, weights.shape[2]), gates[:, 0][:, :, None]
     proj_cols = q_cols + 2 * kv_cols
     w_proj, w_back = weights[:, :proj_cols], weights[:, proj_cols:]
 
@@ -1116,24 +1278,9 @@
     mixed = jnp.einsum("bgqs,bsd->bqgd", probs_low, value_low, preferred_element_type=jnp.float32).astype(low).reshape(2 * seq_len, q_cols)
     hidden = residual + scatter_four(dot_t(mixed, w_back).astype(low).reshape(2, 2, rows, width), 5)
     inverse_two = rms_inverse(hidden)
-    rows_in = gather_dp((hidden * inverse_two * ffn_gain).astype(low), 6).reshape(-1, width)
-    gate_full, up_full, down_full = join_cores((gate_mine, up_mine, down_mine), 2)
-
-    gate_pre = dot(rows_in, gate_full)
-    up_pre = dot(rows_in, up_full)
-    sigmoid_gate = jax.nn.sigmoid(gate_pre)
-    act = (gate_pre * sigmoid_gate * up_pre).astype(low)
-    expert_out = (dot_t(act, down_full) * gates).astype(low)
-    grad_out = (rows_grad.astype(jnp.float32) * gates).astype(low)
-    grad_act = dot(grad_out, down_full)
-    grad_gate = (grad_act * up_pre * sigmoid_gate * (1.0 + gate_pre * (1.0 - sigmoid_gate))).astype(low)
-    grad_up = (grad_act * gate_pre * sigmoid_gate).astype(low)
-    grad_in = (dot_t(grad_gate, gate_full) + dot_t(grad_up, up_full)).astype(low)
-    moe, grad_two = scatter_dp([v.reshape(-1, rows, width) for v in (expert_out, grad_in)], 7)
-    w_gate_part = t_dot(rows_in, grad_gate).astype(low)
-    w_up_part = t_dot(rows_in, grad_up).astype(low)
-    w_down_part = t_dot(grad_out, act).astype(low)
-    owned = sum_cores((w_gate_part, w_up_part, w_down_part), 8)
+    normed_two = (hidden * inverse_two * ffn_gain).astype(low)
+    moe, grad_two, gu_part, down_part, _ = expert_layer(normed_two, rows_grad, gates, gate_mine, up_mine, down_mine, 2)
+    owned = sum_cores(gu_part, down_part, 8)
     swap_grads = functools.partial(lax.all_to_all, axis_name="dp", split_axis=0, concat_axis=0, tiled=True)
     grad_w_gate, grad_w_up, grad_w_down = [swap_grads(v.reshape(experts, rows, -1)).astype(jnp.float32) for v in owned]
     grad_w_down = jnp.transpose(grad_w_down, (0, 2, 1))

time: 981 us -> 907 us (0.925)
  matrix products: 135 us -> 37.1 us
  Pallas kernels: 678 us -> 714 us
  other arithmetic: 55.6 us -> 44.1 us
    dot_general x9 -> x0, matrix products: 97.9 us -> none  [the longest x1 14.9 us: per_device_relay(): grad_act = dot(grad_out, down_full)]
    pallas_call x2, Pallas kernels: 55.9 us -> 77.7 us  [gather_four(): pl.pallas_call(gather_four_kernel, out_shape=jax.ShapeDtypeStruct((2, 2,...]
    pallas_call x4 -> x2, Pallas kernels: 270 us -> 292 us  [the longest x1 278 us: expert_layer(): pl.pallas_call(experts_kernel, out_shape=[jax.ShapeDtypeStruct((rows, wid...]
  transfers between devices with their start and end apart: 6 -> 6, of which waited for: 1 -> 1; matrix products, arithmetic and copies ran while one was open for 14% -> 12% of each run, Pallas kernels for 68% -> 47%
where the time goes in v3:
time: 907 us; the launch traced here: 899 us
  Pallas kernels  714 us (79%)
  other arithmetic  44.1 us (5%)
  starting transfers between devices  43.5 us (5%)
  local copies, waits for them, and re-layouts  37.8 us (4%)
  matrix products  37.1 us (4%)
  waiting for transfers between devices  19.8 us (2%)
    pallas_call x1, Pallas kernels, expert_layer(): pl.pallas_call(experts_kernel, out_shape=[jax.ShapeDtypeStruct((rows, wid...  278 us
    pallas_call x1, Pallas kernels, gather_first(): pl.pallas_call(gather_first_kernel, out_shape=[jax.ShapeDtypeStruct((16,)...  158 us
    pallas_call x1, Pallas kernels, scatter_last(): pl.pallas_call(functools.partial(scatter_last_kernel, chunks), out_shape=...  127 us
    pallas_call x2, Pallas kernels, gather_four(): pl.pallas_call(gather_four_kernel, out_shape=jax.ShapeDtypeStruct((2, 2,...  77.7 us
    pallas_call x2, Pallas kernels, scatter_four(): pl.pallas_call(scatter_four_kernel, out_shape=jax.ShapeDtypeStruct((rows,...  59.8 us
    all_to_all x3, starting transfers between devices, per_device_relay(): swap_grads(v.reshape(experts, rows, -1)).astype(jnp.float32)  21.9 us
    all_to_all x3, starting transfers between devices, per_device_relay(): swap_weights(w)[0]  21.6 us
    all_to_all x3, waiting for transfers between devices, per_device_relay(): swap_weights(w)[0]  19.8 us
  transfers between devices with their start and end apart: 6, of which 1 were waited for; matrix products, arithmetic and copies ran while one was open for 12% of the time, Pallas kernels for 47%

profile of v3, /device:TPU:0, one launch (start us, length us, event | category | flops | bytes accessed | tf_op | source)
XLA Modules:
  0.0 898.9 jit_solution(13368827693895306161)
XLA Ops:
  0.7 8.5 all-to-all-start.2
  11.7 39.1 %gather_four.2 = bf16[2,2,128,2048]{3,2,1,0:T(8,128)(2,1)} custom-call(bf16[128,2048]{1,0:T(8,128)(2,1)} %fusion.36.x_ref), custom_call_target="tpu_custom_call" | custom-call | tf_op jit(solution)/shard_map/gather_four/pallas_call | solution.py:238
  52.9 158.2 %gather_first.1 = (bf16[16,128,2304]{2,1,0:T(8,128)(2,1)}, bf16[16,128,2048]{2,1,0:T(8,128)(2,1)}, f32[16,8,128]{2,1,0:T(8,128)}) custom-call(bf16[2,128,2304]{2,1,0:T(8,128)(2,1)} %pad_maximum_fusion.3.w_ref, bf16[128,2048]{1,0:T(8,128)(2,1)} %c_ref.1, f32[16,8,128]{2,1,0:T(8,128)} %broadcast_in_dim.24.g_ref), custom_call_target="tpu_custom_call" | custom-call | tf_op jit(solution)/shard_map/gather_first/pallas_call | solution.py:476
  211.1 4.4 all-to-all-start
  215.6 5.5 fusion.2
  230.1 19.8 %all-to-all-done = bf16[16,128,384]{2,1,0:T(8,128)(2,1)} async-done(((bf16[16,128,384]{2,1,0:T(8,128)(2,1)}), bf16[16,128,384]{2,1,0:T(8,128)(2,1)}, u32[]{:S(2)}, u32[]{:S(2)}) %all-to-all-start) | async-done | bytes 1572896 | tf_op jit(solution)/shard_map/all_to_all | solution.py:1253
  249.9 8.7 all-to-all-start.1
  264.8 5.9 fusion.13
  270.6 27.4 %scatter_four.2 = f32[128,2048]{1,0:T(8,128)} custom-call(bf16[2,2,128,2048]{3,2,1,0:T(8,128)(2,1)} %bitcast.202), custom_call_target="tpu_custom_call" | custom-call | tf_op jit(solution)/shard_map/scatter_four/pallas_call | solution.py:276
  309.7 278.0 %experts.1 = (f32[128,2048]{1,0:T(8,128)}, f32[128,2048]{1,0:T(8,128)}, bf16[2048,1536]{1,0:T(8,128)(2,1)}, bf16[2048,768]{1,0:T(8,128)(2,1)}, bf16[16,128,2048]{2,1,0:T(8,128)(2,1)}) custom-call(bf16[128,2048]{1,0:T(8,128)(2,1)} %multiply_convert_fusion.x_ref, bf16[16,128,2048]{2,1,0:T(8,128)(2,1)} %get-tuple-element.26.c_ref, f32[16,128,1]{2,1,0:T(8,128)} %copy.163.g_ref, ...), custom_call_target="tpu_custom_call" | custom-call | tf_op jit(solution)/shard_map/experts/pallas_call | solution.py:898
  587.7 14.2 %sum_cores.1 = (bf16[2048,384]{1,0:T(8,128)(2,1)}, bf16[2048,384]{1,0:T(8,128)(2,1)}, bf16[2048,384]{1,0:T(8,128)(2,1)}) custom-call(bf16[2048,1536]{1,0:T(8,128)(2,1)} %get-tuple-element.31.gu_ref, bf16[2048,768]{1,0:T(8,128)(2,1)} %get-tuple-element.32.down_ref), custom_call_target="tpu_custom_call" | custom-call | tf_op jit(solution)/shard_map/sum_cores/pallas_call | solution.py:961
  604.5 9.3 %all-to-all-start.5 = ((bf16[16,128,384]{1,2,0:T(8,128)(2,1)}), bf16[16,128,384]{1,2,0:T(8,128)(2,1)}, u32[]{:S(2)}, u32[]{:S(2)}) async-start(bf16[16,128,384]{1,2,0:T(8,128)(2,1)} %copy.179), calls=%async_computation.5 | async-start | bytes 3145728 | tf_op jit(solution)/shard_map/all_to_all | solution.py:1285
  616.9 38.6 %gather_four.3 = bf16[2,2,128,2048]{3,2,1,0:T(8,128)(2,1)} custom-call(bf16[128,2048]{1,0:T(8,128)(2,1)} %get-tuple-element.123.x_ref), custom_call_target="tpu_custom_call" | custom-call | tf_op jit(solution)/shard_map/gather_four/pallas_call | solution.py:238
  655.5 5.3 fusion.28
  679.9 6.3 all-to-all-start.3
  687.5 6.7 fusion.16
  694.2 32.4 %scatter_four.3 = f32[128,2048]{1,0:T(8,128)} custom-call(bf16[2,2,128,2048]{3,2,1,0:T(8,128)(2,1)} %bitcast.203), custom_call_target="tpu_custom_call" | custom-call | tf_op jit(solution)/shard_map/scatter_four/pallas_call | solution.py:276
  726.7 4.0 copy.178
  731.1 4.3 convolution_convert_fusion.1
  738.6 4.0 pad_maximum_fusion.p_ref
  742.6 6.3 all-to-all-start.4
  749.6 126.7 %scatter_last.1 = (bf16[2,128,2304]{2,1,0:T(8,128)(2,1)}, f32[40,128]{1,0:T(8,128)}) custom-call(bf16[16,128,2304]{2,1,0:T(8,128)(2,1)} %pad_maximum_fusion.p_ref, f32[40,128]{1,0:T(8,128)} %fusion.55.x_ref), custom_call_target="tpu_custom_call" | custom-call | tf_op jit(solution)/shard_map/scatter_last/pallas_call | solution.py:591
  888.5 3.4 convert_element_type.96
  895.3 3.4 convert_element_type.97
  (220 shorter events, 76.4 us)
Async XLA Ops:
  0.7 10.1 %copy-start.42 = (f32[2048]{0:T(1024)S(1)}, f32[2048]{0:T(1024)}, u32[]{:S(2)}) copy-start(f32[2048]{0:T(1024)} %param.26) | copy-start | bytes 24580
  0.7 210.5 %all-to-all-start.2 = ((bf16[16,128,384]{1,2,0:T(8,128)(2,1)}), bf16[16,128,384]{1,2,0:T(8,128)(2,1)}, u32[]{:S(2)}, u32[]{:S(2)}) async-start(bf16[16,128,384]{1,2,0:T(8,128)(2,1)} %bitcast.207), calls=%async_computation.2 | async-start | bytes 3145728 | tf_op jit(solution)/shard_map/all_to_all | solution.py:1253
  9.5 41.4 %copy-start.61 = (f32[256,8]{0,1:T(8,128)S(1)}, f32[256,8]{0,1:T(8,128)}, u32[]{:S(2)}) copy-start(f32[256,8]{0,1:T(8,128)} %param.18) | copy-start | bytes 24580
  9.5 41.4 %copy-start.62 = (s32[256,8]{0,1:T(8,128)S(1)}, s32[256,8]{0,1:T(8,128)}, u32[]{:S(2)}) copy-start(s32[256,8]{0,1:T(8,128)} %param.17) | copy-start | bytes 24580
  9.5 41.4 %copy-start.46 = (bf16[128,256]{1,0:T(8,128)(2,1)S(1)}, bf16[128,256]{1,0:T(8,128)(2,1)}, u32[]{:S(2)}) copy-start(bf16[128,256]{1,0:T(8,128)(2,1)} %param.20) | copy-start | bytes 196612
  9.5 41.5 %copy-start.47 = (bf16[128,256]{1,0:T(8,128)(2,1)S(1)}, bf16[128,256]{1,0:T(8,128)(2,1)}, u32[]{:S(2)}) copy-start(bf16[128,256]{1,0:T(8,128)(2,1)} %param.21) | copy-start | bytes 196612
  11.7 39.3 %copy-start.37 = (bf16[128,2048]{1,0:T(8,128)(2,1)S(1)}, bf16[128,2048]{1,0:T(8,128)(2,1)}, u32[]{:S(2)}) copy-start(bf16[128,2048]{1,0:T(8,128)(2,1)} %param.19) | copy-start | bytes 1572868
  52.9 162.6 %copy-start.15 = (bf16[2,2,128,2048]{3,2,1,0:T(8,128)(2,1)S(1)}, bf16[2,2,128,2048]{3,2,1,0:T(8,128)(2,1)}, u32[]{:S(2)}) copy-start(bf16[2,2,128,2048]{3,2,1,0:T(8,128)(2,1)} %gather_four.2) | copy-start | bytes 6291460
  211.1 38.7 %all-to-all-start = ((bf16[16,128,384]{2,1,0:T(8,128)(2,1)}), bf16[16,128,384]{2,1,0:T(8,128)(2,1)}, u32[]{:S(2)}, u32[]{:S(2)}) async-start(bf16[16,128,384]{2,1,0:T(8,128)(2,1)} %param.23), calls=%async_computation | async-start | bytes 3145728 | tf_op jit(solution)/shard_map/all_to_all | solution.py:1253
  221.1 38.5 %copy-start.38 = (bf16[512,128]{1,0:T(8,128)(2,1)}, bf16[512,128]{1,0:T(8,128)(2,1)S(1)}, u32[]{:S(2)}) copy-start(bf16[512,128]{1,0:T(8,128)(2,1)S(1)} %slice.204) | copy-start | bytes 393220
  229.7 28.9 %copy-start.13 = (bf16[2,256,8,128]{3,1,2,0:T(8,128)(2,1)}, bf16[2,256,8,128]{3,1,2,0:T(8,128)(2,1)S(1)}, u32[]{:S(2)}) copy-start(bf16[2,256,8,128]{3,1,2,0:T(8,128)(2,1)S(1)} %fusion.24) | copy-start | bytes 3145732
  230.0 29.6 %copy-start.25 = (bf16[2,256,64]{2,1,0:T(8,128)(2,1)}, bf16[2,256,64]{2,1,0:T(8,128)(2,1)S(1)}, u32[]{:S(2)}) copy-start(bf16[2,256,64]{2,1,0:T(8,128)(2,1)S(1)} %get-tuple-element.146) | copy-start | bytes 196612
  230.0 29.6 %copy-start.27 = (bf16[2,256,64]{2,1,0:T(8,128)(2,1)}, bf16[2,256,64]{2,1,0:T(8,128)(2,1)S(1)}, u32[]{:S(2)}) copy-start(bf16[2,256,64]{2,1,0:T(8,128)(2,1)S(1)} %get-tuple-element.147) | copy-start | bytes 196612
  249.9 59.8 %all-to-all-start.1 = ((bf16[16,128,384]{2,1,0:T(8,128)(2,1)}), bf16[16,128,384]{2,1,0:T(8,128)(2,1)}, u32[]{:S(2)}, u32[]{:S(2)}) async-start(bf16[16,128,384]{2,1,0:T(8,128)(2,1)} %param.24), calls=%async_computation.1 | async-start | bytes 3145728 | tf_op jit(solution)/shard_map/all_to_all | solution.py:1253
  270.6 30.4 %copy-start.16 = (bf16[2,2,128,2048]{3,2,1,0:T(8,128)(2,1)S(1)}, bf16[2,2,128,2048]{3,2,1,0:T(8,128)(2,1)}, u32[]{:S(2)}) copy-start(bf16[2,2,128,2048]{3,2,1,0:T(8,128)(2,1)} %gather_four.2) | copy-start | bytes 6291460
  604.5 9.4 %copy-start.6 = (f32[128,2048]{1,0:T(8,128)S(1)}, f32[128,2048]{1,0:T(8,128)}, u32[]{:S(2)}) copy-start(f32[128,2048]{1,0:T(8,128)} %copy-done.5) | copy-start | bytes 3145732
  604.5 9.4 %copy-start.18 = (f32[128,2048]{1,0:T(8,128)S(1)}, f32[128,2048]{1,0:T(8,128)}, u32[]{:S(2)}) copy-start(f32[128,2048]{1,0:T(8,128)} %get-tuple-element.29) | copy-start | bytes 3145732
  604.5 9.4 %copy-start.41 = (f32[2048]{0:T(1024)S(1)}, f32[2048]{0:T(1024)}, u32[]{:S(2)}) copy-start(f32[2048]{0:T(1024)} %param.27) | copy-start | bytes 24580
  604.5 9.4 %copy-start.60 = (f32[128]{0:T(128)S(1)}, f32[128]{0:T(128)}, u32[]{:S(2)}) copy-start(f32[128]{0:T(128)} %copy-done.59) | copy-start | bytes 1540
  604.5 9.7 %copy-start.23 = (bf16[128,2048]{1,0:T(8,128)(2,1)S(1)}, bf16[128,2048]{1,0:T(8,128)(2,1)}, u32[]{:S(2)}) copy-start(bf16[128,2048]{1,0:T(8,128)(2,1)} %c_ref.1) | copy-start | bytes 1572868
  604.5 9.7 %copy-start.64 = (f32[128]{0:T(128)S(1)}, f32[128]{0:T(128)}, u32[]{:S(2)}) copy-start(f32[128]{0:T(128)} %get-tuple-element.166) | copy-start | bytes 1540
  604.5 75.3 %all-to-all-start.5 = ((bf16[16,128,384]{1,2,0:T(8,128)(2,1)}), bf16[16,128,384]{1,2,0:T(8,128)(2,1)}, u32[]{:S(2)}, u32[]{:S(2)}) async-start(bf16[16,128,384]{1,2,0:T(8,128)(2,1)} %copy.179), calls=%async_computation.5 | async-start | bytes 3145728 | tf_op jit(solution)/shard_map/all_to_all | solution.py:1285
  679.9 62.7 %all-to-all-start.3 = ((bf16[16,128,384]{2,1,0:T(8,128)(2,1)}), bf16[16,128,384]{2,1,0:T(8,128)(2,1)}, u32[]{:S(2)}, u32[]{:S(2)}) async-start(bf16[16,128,384]{2,1,0:T(8,128)(2,1)} %bitcast.51), calls=%async_computation.3 | async-start | bytes 3145728 | tf_op jit(solution)/shard_map/all_to_all | solution.py:1285
  742.6 152.7 %all-to-all-start.4 = ((bf16[16,128,384]{2,1,0:T(8,128)(2,1)}), bf16[16,128,384]{2,1,0:T(8,128)(2,1)}, u32[]{:S(2)}, u32[]{:S(2)}) async-start(bf16[16,128,384]{2,1,0:T(8,128)(2,1)} %bitcast.52), calls=%async_computation.4 | async-start | bytes 3145728 | tf_op jit(solution)/shard_map/all_to_all | solution.py:1285
  (47 other events, 127.7 us)

commit v4 on v3

--- a/solution.py
+++ b/solution.py
@@ -218,21 +218,10 @@
 def gather_four_kernel(x_ref, out_ref, send_sem, recv_sem):
     me = Place()
     me.greet(chain=True, partner=True)
-    mine, theirs = out_ref.at[me.half, me.core], out_ref.at[1 - me.half, me.core]
-    across = me.copy(x_ref, mine, send_sem.at[0], recv_sem.at[0], me.dp + me.pair)
-    across.start()
-    beside = me.copy(x_ref, mine, send_sem.at[1], recv_sem.at[1], me.dp, 1 - me.core)
-    beside.start()
-    mine[...] = x_ref[...]
-    across.wait_recv()
-    relay = me.copy(theirs, theirs, send_sem.at[2], recv_sem.at[2], me.dp, 1 - me.core)
-    relay.start()
-    across.wait_send()
-    beside.wait()
-    relay.wait()
-
-
-def gather_four(x, cid):
+    run(gather_four(me, x_ref, out_ref, send_sem, recv_sem))
+
+
+def gather_pair_rows(x, cid):
     rows, columns = x.shape
     vmem = pl.BlockSpec(memory_space=pltpu.VMEM)
     return pl.pallas_call(
@@ -453,49 +442,107 @@
     return finish
 
 
-def gather_first_kernel(w_ref, c_ref, g_ref, w_out, c_out, g_out, w_own, c_own, w_send, w_recv, c_send, c_recv, g_send, g_recv, copy_sem):
+def share_experts(me, ins, outs, send_sem, recv_sem):
+    depth = ins[0].shape[1]
+
+    def sends(r):
+        to = (me.dp + r) % 16
+        at = pl.ds(pl.multiple_of(me.dp * depth, depth), depth)
+        pairs = ((ins[0].at[to], outs[0].at[at]), (ins[1].at[to], outs[1].at[at]), (ins[2].at[to], outs[2].at[:, at]))
+        return [me.copy(src, dst, send_sem.at[r, j], recv_sem.at[r, j], to) for j, (src, dst) in enumerate(pairs)]
+
+    for r in (8, 7, 9, 4, 12, 5, 11, 6, 10, 3, 13, 2, 14, 1, 15):
+        for c in sends(r):
+            c.start()
+    yield
+    for r in range(1, 16):
+        at = pl.ds(pl.multiple_of((me.dp + 16 - r) % 16 * depth, depth), depth)
+        for j, dst in enumerate((outs[0].at[at], outs[1].at[at], outs[2].at[:, at])):
+            me.copy(dst, dst, send_sem.at[r, j], recv_sem.at[r, j], me.dp).wait_recv()
+    for r in range(1, 16):
+        for c in sends(r):
+            c.wait_send()
+
+
+def gather_four(me, x_ref, out_ref, send_sem, recv_sem):
+    mine, theirs = out_ref.at[me.half, me.core], out_ref.at[1 - me.half, me.core]
+    across = me.copy(x_ref, mine, send_sem.at[0], recv_sem.at[0], me.dp + me.pair)
+    across.start()
+    beside = me.copy(x_ref, mine, send_sem.at[1], recv_sem.at[1], me.dp, 1 - me.core)
+    beside.start()
+    mine[...] = x_ref[...]
+    yield
+    across.wait_recv()
+    relay = me.copy(theirs, theirs, send_sem.at[2], recv_sem.at[2], me.dp, 1 - me.core)
+    relay.start()
+    yield
+    across.wait_send()
+    beside.wait()
+    relay.wait()
+
+
+def gather_first_kernel(
+    w_ref, c_ref, g_ref, x_ref, gate_ref, up_ref, down_ref,
+    w_out, c_out, g_out, x_out, gate_out, up_out, down_out,
+    w_own, c_own, e_own, w_send, w_recv, c_send, c_recv, g_send, g_recv, x_send, x_recv, e_send, e_recv, copy_sem,
+):
     me = Place()
+    depth = gate_ref.shape[1]
+    at = pl.ds(pl.multiple_of(me.dp * depth, depth), depth)
     ends = [
         keep_own(w_ref.at[me.half], w_own, w_out.at[me.dp], copy_sem.at[0]),
         keep_own(c_ref, c_own, c_out.at[me.dp], copy_sem.at[1]),
+        keep_own(gate_ref.at[me.dp], e_own.at[0], gate_out.at[at], copy_sem.at[2]),
+        keep_own(up_ref.at[me.dp], e_own.at[1], up_out.at[at], copy_sem.at[3]),
     ]
+    flat = pltpu.make_async_copy(down_ref.at[me.dp], down_out.at[:, at], copy_sem.at[4, 0])
+    flat.start()
     g_out[me.dp] = g_ref[me.dp]
-    me.greet(everyone=True)
+    me.greet(everyone=True, partner=True)
     run(
+        gather_four(me, x_ref, x_out, x_send, x_recv),
         gather_pairs(me, w_ref, w_out, w_send, w_recv),
         gather_line(me, c_ref, c_out, c_send, c_recv),
         swap_rows(me, g_ref, g_out, g_send, g_recv),
+        share_experts(me, (gate_ref, up_ref, down_ref), (gate_out, up_out, down_out), e_send, e_recv),
     )
     for end in ends:
         end()
-
-
-def gather_first(weights, rows, gates, cid):
+    flat.wait()
+
+
+def gather_first(weights, rows, gates, normed, experts, cid):
     hbm, vmem = pl.BlockSpec(memory_space=pl.ANY), pl.BlockSpec(memory_space=pltpu.VMEM)
     dma = pltpu.SemaphoreType.DMA
+    dtype = rows.dtype
+    _, depth, hidden = experts[0].shape
     return pl.pallas_call(
         gather_first_kernel,
         out_shape=[
-            jax.ShapeDtypeStruct((16,) + weights.shape[1:], weights.dtype),
-            jax.ShapeDtypeStruct((16,) + rows.shape, rows.dtype),
+            jax.ShapeDtypeStruct((16,) + weights.shape[1:], dtype),
+            jax.ShapeDtypeStruct((16,) + rows.shape, dtype),
             jax.ShapeDtypeStruct(gates.shape, gates.dtype),
+            jax.ShapeDtypeStruct((2, 2) + normed.shape, dtype),
+            jax.ShapeDtypeStruct((16 * depth, hidden), dtype),
+            jax.ShapeDtypeStruct((16 * depth, hidden), dtype),
+            jax.ShapeDtypeStruct((hidden, 16 * depth), dtype),
         ],
-        in_specs=[hbm, hbm, vmem],
-        out_specs=[hbm, hbm, vmem],
+        in_specs=[hbm, hbm, vmem, vmem, hbm, hbm, hbm],
+        out_specs=[hbm, hbm, vmem, vmem, hbm, hbm, hbm],
         scratch_shapes=[
-            pltpu.VMEM(weights.shape[1:], weights.dtype),
-            pltpu.VMEM(rows.shape, rows.dtype),
-            dma((15,)),
-            dma((16,)),
-            dma((29,)),
-            dma((16,)),
-            dma((16,)),
-            dma((16,)),
-            dma((2, 2)),
+            pltpu.VMEM(weights.shape[1:], dtype),
+            pltpu.VMEM(rows.shape, dtype),
+            pltpu.VMEM((2, depth, hidden), dtype),
+            dma((15,)), dma((16,)),
+            dma((29,)), dma((16,)),
+            dma((16,)), dma((16,)),
+            dma((3,)), dma((3,)),
+            dma((16, 3)), dma((16, 3)),
+            dma((5, 2)),
         ],
         compiler_params=pltpu.CompilerParams(collective_id=cid, has_side_effects=True),
         name="gather_first",
-    )(weights, rows, gates)
+    )(weights, rows, gates, normed, *experts)
 
 
 def scatter_pairs(me, chunks, p_ref, out_ref, from_b, from_a, from_far, send_sem, recv_sem):
@@ -575,37 +622,96 @@
         yield
 
 
-def scatter_last_kernel(chunks, p_ref, x_ref, out_ref, sum_ref, from_b, from_a, from_far, held, send_sem, recv_sem, sum_send, sum_recv):
+def return_experts(me, gu_ref, down_ref, outs, own, held, core_send, core_recv, send_sem, recv_sem, copy_sem):
+    rows, half = outs[0].shape[1:]
+
+    def views(d, core):
+        at = pl.ds(pl.multiple_of(d * rows, rows), rows)
+        starts = ((gu_ref, core * half), (gu_ref, 2 * half + core * half), (down_ref, core * half))
+        return [ref.at[at, pl.ds(pl.multiple_of(start, 128), half)] for ref, start in starts]
+
+    def beside(r):
+        d = (me.dp + r) % 16
+        return [
+            me.copy(src, held.at[j, r], core_send.at[r, j], core_recv.at[r, j], me.dp, 1 - me.core)
+            for j, src in enumerate(views(d, 1 - me.core))
+        ]
+
+    def loads(r):
+        d = (me.dp + r) % 16
+        return [pltpu.make_async_copy(src, own.at[j, r], copy_sem.at[r, j]) for j, src in enumerate(views(d, me.core))]
+
+    def sends(r):
+        d = (me.dp + r) % 16
+        return [me.copy(held.at[j, r], outs[j].at[me.dp], send_sem.at[r, j], recv_sem.at[r, j], d) for j in range(3)]
+
+    order = (8, 7, 9, 4, 12, 5, 11, 6, 10, 3, 13, 2, 14, 1, 15, 0)
+    for r in order:
+        for c in beside(r) + loads(r):
+            c.start()
+    yield
+    keep = [pltpu.make_async_copy(held.at[j, 0], outs[j].at[me.dp], copy_sem.at[16, j]) for j in range(3)]
+    for n, r in enumerate(order):
+        for j, (arrives, load) in enumerate(zip(beside(r), loads(r))):
+            arrives.wait_recv()
+            load.wait()
+            add_rows(held.at[j, r], (own.at[j, r], held.at[j, r]), rows, 64)
+        for c in sends(r) if r else keep:
+            c.start()
+        if n % 2:
+            yield
+    for r in range(1, 16):
+        s = (me.dp + 16 - r) % 16
+        for j in range(3):
+            dst = outs[j].at[s]
+            me.copy(dst, dst, send_sem.at[r, j], recv_sem.at[r, j], me.dp).wait_recv()
+    for c in keep:
+        c.wait()
+    for r in range(16):
+        for c in beside(r) + (sends(r) if r else []):
+            c.wait_send()
+
+
+def scatter_last_kernel(
+    chunks, p_ref, x_ref, gu_ref, down_ref, out_ref, sum_ref, gate_out, up_out, down_out,
+    from_b, from_a, from_far, total, own, held, send_sem, recv_sem, sum_send, sum_recv, core_send, core_recv, e_send, e_recv, copy_sem,
+):
     me = Place()
-    me.greet(near=True, chain=True, partner=True)
+    me.greet(everyone=True, partner=True)
     run(
+        return_experts(me, gu_ref, down_ref, (gate_out, up_out, down_out), own, held, core_send, core_recv, e_send, e_recv, copy_sem),
         scatter_pairs(me, chunks, p_ref, out_ref, from_b, from_a, from_far, send_sem, recv_sem),
-        sum_all(me, x_ref, sum_ref, held, sum_send, sum_recv),
-    )
-
-
-def scatter_last(p, x, cid, chunks=2):
+        sum_all(me, x_ref, sum_ref, total, sum_send, sum_recv),
+    )
+
+
+def scatter_last(p, x, gu, down, cid, chunks=2):
     _, rows, columns = p.shape
-    vmem = pl.BlockSpec(memory_space=pltpu.VMEM)
+    half = down.shape[1] // 2
+    hbm, vmem = pl.BlockSpec(memory_space=pl.ANY), pl.BlockSpec(memory_space=pltpu.VMEM)
     dma = pltpu.SemaphoreType.DMA
     return pl.pallas_call(
         functools.partial(scatter_last_kernel, chunks),
-        out_shape=[jax.ShapeDtypeStruct((2, rows, columns), p.dtype), jax.ShapeDtypeStruct(x.shape, x.dtype)],
-        in_specs=[vmem] * 2,
-        out_specs=[vmem] * 2,
+        out_shape=[jax.ShapeDtypeStruct((2, rows, columns), p.dtype), jax.ShapeDtypeStruct(x.shape, x.dtype)]
+        + [jax.ShapeDtypeStruct((16, rows, half), p.dtype)] * 3,
+        in_specs=[vmem, vmem, hbm, hbm],
+        out_specs=[vmem, vmem, hbm, hbm, hbm],
         scratch_shapes=[
             pltpu.VMEM((2, 4, rows, columns), p.dtype),
             pltpu.VMEM((4, rows, columns), p.dtype),
             pltpu.VMEM((2, rows, columns), p.dtype),
             pltpu.VMEM((2, 5) + x.shape, x.dtype),
-            dma((15, chunks)),
-            dma((15, chunks)),
-            dma((5,)),
-            dma((5,)),
+            pltpu.VMEM((3, 16, rows, half), p.dtype),
+            pltpu.VMEM((3, 16, rows, half), p.dtype),
+            dma((15, chunks)), dma((15, chunks)),
+            dma((5,)), dma((5,)),
+            dma((16, 3)), dma((16, 3)),
+            dma((16, 3)), dma((16, 3)),
+            dma((17, 3)),
         ],
         compiler_params=pltpu.CompilerParams(collective_id=cid, has_side_effects=True, vmem_limit_bytes=LIMIT),
         name="scatter_last",
-    )(p, x)
+    )(p, x, gu, down)
 
 
 def experts_kernel(
@@ -616,7 +722,7 @@
 ):
     me = Place()
     rows, width = x_ref.shape
-    hidden = wd.shape[1]
+    hidden = wd.shape[0]
     half = hidden // 2
     low = me.z < 2
     depth = jnp.where(low, me.z, 3 - me.z)
@@ -718,7 +824,7 @@
         return (
             wgu.at[:, pl.ds(pl.multiple_of(at, 128), half)],
             wgu.at[:, pl.ds(pl.multiple_of(hidden + at, 128), half)],
-            wd.at[:, pl.ds(pl.multiple_of(at, 128), half)],
+            wd.at[pl.ds(pl.multiple_of(at, 128), half)],
         )
 
     mine = (gate_ref, up_ref, down_ref)
@@ -756,7 +862,7 @@
 
         def inner(j, _):
             at, at_up = pl.ds(pl.multiple_of(j * tile, tile), tile), pl.ds(pl.multiple_of(hidden + j * tile, tile), tile)
-            gate, up, grad = dot(xb[slot], wgu[:, at]), dot(xb[slot], wgu[:, at_up]), dot(cb[slot], wd[:, at]) * gates
+            gate, up, grad = dot(xb[slot], wgu[:, at]), dot(xb[slot], wgu[:, at_up]), dot_t(cb[slot], wd[at, :]) * gates
             sig = 1.0 / (1.0 + jnp.exp(-gate))
             act = gate * sig
             ag[n, :, at] = (act * up * gates).astype(ag.dtype)
@@ -781,7 +887,7 @@
 
         def outer(j, _):
             at = pl.ds(pl.multiple_of(j * 2 * tile, 2 * tile), 2 * tile)
-            p[0, n, :, at] = dot_t(ag[n], wd[at, :]).astype(p.dtype)
+            p[0, n, :, at] = dot(ag[n], wd[:, at]).astype(p.dtype)
             p[1, n, :, at] = dot_t(ggu[n], wgu[at, :]).astype(p.dtype)
             return 0
 
@@ -908,7 +1014,7 @@
         out_specs=[vmem, vmem, hbm, hbm, hbm],
         scratch_shapes=[
             pltpu.VMEM((width, 4 * half), dtype),
-            pltpu.VMEM((width, 2 * half), dtype),
+            pltpu.VMEM((2 * half, width), dtype),
             pltpu.VMEM((8, 2 * rows, 2 * half), dtype),
             pltpu.VMEM((8, 2 * rows, 4 * half), dtype),
             pltpu.VMEM((2, 8, 2 * rows, width), dtype),
@@ -927,50 +1033,6 @@
         compiler_params=pltpu.CompilerParams(collective_id=cid, has_side_effects=True, vmem_limit_bytes=67_043_328),
         name="experts",
     )(x, grads, gates, gate, up, down)
-
-
-def sum_cores_kernel(gu_ref, down_ref, gate_out, up_out, down_out, held, send_sem, recv_sem):
-    me = Place()
-    me.greet(partner=True)
-    rows, half = gate_out.shape
-    chunks = send_sem.shape[1]
-    part = rows // chunks
-    outs = (gate_out, up_out, down_out)
-
-    def view(i, at, core):
-        return (gu_ref, gu_ref, down_ref)[i].at[at, pl.ds(pl.multiple_of((2 * half if i == 1 else 0) + core * half, 128), half)]
-
-    def send(i, k):
-        at = pl.ds(k * part, part)
-        return me.copy(view(i, at, 1 - me.core), held.at[i, at], send_sem.at[i, k], recv_sem.at[i, k], me.dp, 1 - me.core)
-
-    every = [(i, k) for i in range(3) for k in range(chunks)]
-    for i, k in every:
-        send(i, k).start()
-    for i, k in every:
-        send(i, k).wait_recv()
-        at = pl.ds(k * part, part)
-        add_rows(outs[i].at[at], (view(i, at, me.core), held.at[i, at]), part, 64)
-    for i, k in every:
-        send(i, k).wait_send()
-
-
-def sum_cores(gu, down, cid, chunks=4):
-    rows, half = down.shape[0], down.shape[1] // 2
-    vmem = pl.BlockSpec(memory_space=pltpu.VMEM)
-    return pl.pallas_call(
-        sum_cores_kernel,
-        out_shape=[jax.ShapeDtypeStruct((rows, half), down.dtype)] * 3,
-        in_specs=[vmem] * 2,
-        out_specs=[vmem] * 3,
-        scratch_shapes=[
-            pltpu.VMEM((3, rows, half), down.dtype),
-            pltpu.SemaphoreType.DMA((3, chunks)),
-            pltpu.SemaphoreType.DMA((3, chunks)),
-        ],
-        compiler_params=pltpu.CompilerParams(collective_id=cid, has_side_effects=True, vmem_limit_bytes=LIMIT),
-        name="sum_cores",
-    )(gu, down)
 
 
 def per_device_any(
@@ -1249,16 +1311,14 @@
             for h in range(2)
         ]
     )
-    swap_weights = functools.partial(lax.all_to_all, axis_name="dp", split_axis=0, concat_axis=1, tiled=True)
-    gate_mine, up_mine, down_mine = [swap_weights(w)[0] for w in (w_gate, w_up, jnp.transpose(w_down, (0, 2, 1)))]
-    weights, rows_grad, gates = gather_first(halves, cotangent, gates, 1)
-    weights, gates = weights.reshape(-1, weights.shape[2]), gates[:, 0][:, :, None]
+    residual = tokens.astype(jnp.float32)
+    inverse_one = rms_inverse(residual)
+    normed_one = (residual * inverse_one * attn_gain).astype(low)
+    weights, rows_grad, gates, seq_normed, *projections = gather_first(halves, cotangent, gates, normed_one, (w_gate, w_up, w_down), 1)
+    weights, gates, seq_normed = weights.reshape(-1, weights.shape[2]), gates[:, 0][:, :, None], seq_normed.reshape(-1, width)
     proj_cols = q_cols + 2 * kv_cols
     w_proj, w_back = weights[:, :proj_cols], weights[:, proj_cols:]
 
-    residual = tokens.astype(jnp.float32)
-    inverse_one = rms_inverse(residual)
-    seq_normed = gather_four((residual * inverse_one * attn_gain).astype(low), 4).reshape(-1, width)
     seq_len = 2 * rows
     group = q_cols // head_dim
     scale = head_dim ** (-0.5)
@@ -1279,16 +1339,11 @@
     hidden = residual + scatter_four(dot_t(mixed, w_back).astype(low).reshape(2, 2, rows, width), 5)
     inverse_two = rms_inverse(hidden)
     normed_two = (hidden * inverse_two * ffn_gain).astype(low)
-    moe, grad_two, gu_part, down_part, _ = expert_layer(normed_two, rows_grad, gates, gate_mine, up_mine, down_mine, 2)
-    owned = sum_cores(gu_part, down_part, 8)
-    swap_grads = functools.partial(lax.all_to_all, axis_name="dp", split_axis=0, concat_axis=0, tiled=True)
-    grad_w_gate, grad_w_up, grad_w_down = [swap_grads(v.reshape(experts, rows, -1)).astype(jnp.float32) for v in owned]
-    grad_w_down = jnp.transpose(grad_w_down, (0, 2, 1))
-
+    moe, grad_two, gu_part, down_part, _ = expert_layer(normed_two, rows_grad, gates, *projections, 2)
     output = (hidden + moe).astype(low)
     ffn_gain_part = jnp.sum(grad_two * hidden * inverse_two, axis=0)
     grad_hidden = cotangent.astype(jnp.float32) + norm_backward(grad_two, hidden, inverse_two, ffn_gain)
-    grad_attn = gather_four(grad_hidden.astype(low), 9).reshape(-1, width)
+    grad_attn = gather_pair_rows(grad_hidden.astype(low), 9).reshape(-1, width)
     grad_mixed = dot(grad_attn, w_back).astype(low).reshape(2, seq_len, group, head_dim)
     grad_probs = jnp.einsum("bqgd,bsd->bgqs", grad_mixed, value_low, preferred_element_type=jnp.float32)
     delta_sum = jnp.sum(grad_probs * probs, axis=-1, keepdims=True)
@@ -1308,7 +1363,9 @@
     attn_gain_part = jnp.sum(grad_one * residual * inverse_one, axis=0)
     gains = jnp.concatenate([attn_gain_part, ffn_gain_part, query_gain_part, key_gain_part])
     gains = jnp.pad(gains, (0, -gains.shape[0] % 1024)).reshape(-1, 128)
-    shares, totals = scatter_last(w_parts.reshape(-1, rows, w_parts.shape[1]), gains, 11)
+    shares, totals, *grads_moe = scatter_last(w_parts.reshape(-1, rows, w_parts.shape[1]), gains, gu_part, down_part, 11)
+    grad_w_gate, grad_w_up, grad_w_down = [v.astype(jnp.float32) for v in grads_moe]
+    grad_w_down = jnp.transpose(grad_w_down, (0, 2, 1))
     shares, totals = shares.astype(jnp.float32), totals.reshape(-1)
     stops = (0, q_cols, q_cols + kv_cols, proj_cols, proj_cols + q_cols)
     grads = [jnp.concatenate([shares[0, :, a:b], shares[1, :, a:b]], axis=1) for a, b in zip(stops, stops[1:])]

time: 907 us -> 933 us (1.029)
  Pallas kernels: 714 us -> 793 us
  starting transfers between devices: 43.5 us -> 0 us
  waiting for transfers between devices: 19.8 us -> 0 us
    pallas_call x1, Pallas kernels: 158 us -> 256 us  [gather_first(): pl.pallas_call(gather_first_kernel, out_shape=[jax.ShapeDtypeStruct((16,)...]
    pallas_call x3 -> x1, Pallas kernels: 91.9 us -> 15.4 us  [gather_pair_rows(): pl.pallas_call(gather_four_kernel, out_shape=jax.ShapeDtypeStruct((2, 2,...]
    pallas_call x1, Pallas kernels: 127 us -> 189 us  [scatter_last(): pl.pallas_call(functools.partial(scatter_last_kernel, chunks), out_shape=...]
    all_to_all x6 -> x0, starting transfers between devices: 43.5 us -> none  [the longest x3 21.9 us: per_device_relay(): swap_grads(v.reshape(experts, rows, -1)).astype(jnp.float32)]
    all_to_all x6 -> x0, waiting for transfers between devices: 19.8 us -> none  [the longest x3 19.8 us: per_device_relay(): swap_weights(w)[0]]
  transfers between devices with their start and end apart: 6 -> 0, of which waited for: 1 -> 0; matrix products, arithmetic and copies ran while one was open for 12% -> 0% of each run, Pallas kernels for 47% -> 0%
where the time goes in v4:
time: 933 us; the launch traced here: 925 us
  Pallas kernels  793 us (85%)
  other arithmetic  51.1 us (5%)
  matrix products  40.3 us (4%)
  local copies, waits for them, and re-layouts  38 us (4%)
    pallas_call x1, Pallas kernels, expert_layer(): pl.pallas_call(experts_kernel, out_shape=[jax.ShapeDtypeStruct((rows, wid...  280 us
    pallas_call x1, Pallas kernels, gather_first(): pl.pallas_call(gather_first_kernel, out_shape=[jax.ShapeDtypeStruct((16,)...  256 us
    pallas_call x1, Pallas kernels, scatter_last(): pl.pallas_call(functools.partial(scatter_last_kernel, chunks), out_shape=...  189 us
    pallas_call x2, Pallas kernels, scatter_four(): pl.pallas_call(scatter_four_kernel, out_shape=jax.ShapeDtypeStruct((rows,...  53.3 us

profile of v4, /device:TPU:0, one launch (start us, length us, event | category | flops | bytes accessed | tf_op | source)
XLA Modules:
  0.0 924.8 jit_solution(5468978001963093853)
XLA Ops:
  5.8 255.8 %gather_first.1 = (bf16[16,128,2304]{2,1,0:T(8,128)(2,1)}, bf16[16,128,2048]{2,1,0:T(8,128)(2,1)}, f32[16,8,128]{2,1,0:T(8,128)}, bf16[2,2,128,2048]{3,2,1,0:T(8...) custom-call(bf16[2,128,2304]{2,1,0:T(8,128)(2,1)} %pad_maximum_fusion.3.w_ref, ...), custom_call_target="tpu_custom_call" | custom-call | tf_op jit(solution)/shard_map/gather_first/pallas_call | solution.py:519
  261.7 6.0 fusion.2
  280.1 2.0 fusion.31
  284.0 6.3 fusion.13
  290.3 32.7 %scatter_four.2 = f32[128,2048]{1,0:T(8,128)} custom-call(bf16[2,2,128,2048]{3,2,1,0:T(8,128)(2,1)} %bitcast.195), custom_call_target="tpu_custom_call" | custom-call | tf_op jit(solution)/shard_map/scatter_four/pallas_call | solution.py:265
  328.6 280.3 %experts.1 = (f32[128,2048]{1,0:T(8,128)}, f32[128,2048]{1,0:T(8,128)}, bf16[2048,1536]{1,0:T(8,128)(2,1)}, bf16[2048,768]{1,0:T(8,128)(2,1)}, bf16[16,128,2048]{2,1,0:T(8,128)(2,1)}) custom-call(bf16[128,2048]{1,0:T(8,128)(2,1)} %multiply_convert_fusion.x_ref, bf16[16,128,2048]{2,1,0:T(8,128)(2,1)} %get-tuple-element.31.c_ref, f32[16,128,1]{2,1,0:T(8,128)} %copy.157.g_ref, ...), custom_call_target="tpu_custom_call" | custom-call | tf_op jit(solution)/shard_map/experts/pallas_call | solution.py:1004
  611.1 3.2 fusion.63
  614.3 15.4 %gather_four.1 = bf16[2,2,128,2048]{3,2,1,0:T(8,128)(2,1)} custom-call(bf16[128,2048]{1,0:T(8,128)(2,1)} %get-tuple-element.131.x_ref), custom_call_target="tpu_custom_call" | custom-call | tf_op jit(solution)/shard_map/gather_four/pallas_call | solution.py:227
  629.8 5.3 fusion.28
  645.3 2.5 copy.163
  651.6 5.1 fusion.23
  657.8 2.1 multiply_reduce_fusion.5
  663.9 4.3 fusion.16
  668.1 20.6 %scatter_four.3 = f32[128,2048]{1,0:T(8,128)} custom-call(bf16[2,2,128,2048]{3,2,1,0:T(8,128)(2,1)} %bitcast.194), custom_call_target="tpu_custom_call" | custom-call | tf_op jit(solution)/shard_map/scatter_four/pallas_call | solution.py:265
  690.9 2.5 copy.171
  693.4 7.2 convolution_convert_fusion
  700.7 2.5 copy.172
  704.8 4.1 convolution_convert_fusion.1
  708.9 4.0 pad_maximum_fusion.p_ref
  712.9 188.5 %scatter_last.1 = (bf16[2,128,2304]{2,1,0:T(8,128)(2,1)}, f32[40,128]{1,0:T(8,128)}, bf16[16,128,384]{2,1,0:T(8,128)(2,1)}, bf16[16,128,384]{2,1,0:T(8,128)(2,1)}, bf16[16,128,384]{2,1,0:T(8,128)(2,1)}) custom-call(bf16[16,128,2304]{2,1,0:T(8,128)(2,1)} %pad_maximum_fusion.p_ref, f32[40,128]{1,0:T(8,128)} %fusion.55.x_ref, ...), custom_call_target="tpu_custom_call" | custom-call | tf_op jit(solution)/shard_map/scatter_last/pallas_call | solution.py:693
  905.0 2.5 copy.173
  907.6 3.4 convert_bitcast_fusion
  911.0 3.5 copy.174
  915.9 2.3 pad_maximum_fusion.4
  (217 shorter events, 60.6 us)
Async XLA Ops:
  4.9 256.8 %copy-start.55 = (f32[128]{0:T(128)}, f32[128]{0:T(128)S(1)}, u32[]{:S(2)}) copy-start(f32[128]{0:T(128)S(1)} %get-tuple-element.173) | copy-start | bytes 1540
  272.5 4.2 copy-start.19
  272.5 4.2 copy-start.21
  273.5 3.1 copy-start.53
  274.1 3.9 copy-start.11
  278.0 4.0 copy-start.44
  284.0 6.3 copy-start.18
  629.8 5.6 copy-start.3
  651.6 5.2 copy-start.12
  656.8 5.8 copy-start.32
  656.8 4.5 copy-start.4
  657.6 3.8 copy-start.34
  657.6 5.0 slice-start.2
  668.1 20.6 %copy-start.8 = (bf16[128,2048]{1,0:T(8,128)(2,1)S(1)}, bf16[128,2048]{1,0:T(8,128)(2,1)}, u32[]{:S(2)}) copy-start(bf16[128,2048]{1,0:T(8,128)(2,1)} %param.15) | copy-start | bytes 1572868
  668.1 20.6 %copy-start.43 = (f32[2048]{0:T(1024)S(1)}, f32[2048]{0:T(1024)}, u32[]{:S(2)}) copy-start(f32[2048]{0:T(1024)} %param.26) | copy-start | bytes 24580
  668.1 20.6 %copy-start.56 = (f32[128]{0:T(128)S(1)}, f32[128]{0:T(128)}, u32[]{:S(2)}) copy-start(f32[128]{0:T(128)} %copy-done.55) | copy-start | bytes 1540
  668.1 22.8 %copy-start.23 = (bf16[2,2,128,2048]{3,2,1,0:T(8,128)(2,1)S(1)}, bf16[2,2,128,2048]{3,2,1,0:T(8,128)(2,1)}, u32[]{:S(2)}) copy-start(bf16[2,2,128,2048]{3,2,1,0:T(8,128)(2,1)} %get-tuple-element.29) | copy-start | bytes 6291460
  693.4 7.2 copy-start.14
  703.1 5.7 slice-start
  704.8 4.1 slice-start.1
  914.5 3.6 copy-start.25
  920.1 3.1 copy-start.10
  920.1 3.1 copy-start.16
  920.1 3.1 copy-start.63
  (46 other events, 76.3 us)

commit v5 on v4

--- a/solution.py
+++ b/solution.py
@@ -171,7 +171,16 @@
     def at_z(self, z):
         return self.dp + 4 * (z - self.z)
 
-    def greet(self, line=False, near=False, chain=False, everyone=False, partner=False):
+    def z_of(self, m):
+        low = self.z < 2
+        depth = jnp.where(low, self.z, 3 - self.z)
+        t = jnp.where(m == 0, depth, jnp.where(m == 1, 1 - depth, m))
+        return jnp.where(low, t, 3 - t)
+
+    def block(self, n):
+        return self.at_z(self.z_of(n // 2)) + (n % 2) * self.da
+
+    def greet(self, line=False, column=False, near=False, chain=False, everyone=False, partner=False):
         barrier = pltpu.get_barrier_semaphore()
         count = 0
 
@@ -193,6 +202,10 @@
                 if near:
                     signal(self.dp + self.far, self.core)
                     count = count + 1
+            if column:
+                for r in range(1, 4):
+                    signal((self.dp + 4 * r) % 16, self.core)
+                count = count + 3
             if line:
                 pl.when(self.z > 0)(lambda: signal(self.dp - 4, self.core))
                 pl.when(self.z < 3)(lambda: signal(self.dp + 4, self.core))
@@ -213,26 +226,6 @@
         return 0
 
     lax.fori_loop(0, rows // block, body, 0)
-
-
-def gather_four_kernel(x_ref, out_ref, send_sem, recv_sem):
-    me = Place()
-    me.greet(chain=True, partner=True)
-    run(gather_four(me, x_ref, out_ref, send_sem, recv_sem))
-
-
-def gather_pair_rows(x, cid):
-    rows, columns = x.shape
-    vmem = pl.BlockSpec(memory_space=pltpu.VMEM)
-    return pl.pallas_call(
-        gather_four_kernel,
-        out_shape=jax.ShapeDtypeStruct((2, 2, rows, columns), x.dtype),
-        in_specs=[vmem],
-        out_specs=vmem,
-        scratch_shapes=[pltpu.SemaphoreType.DMA((3,)), pltpu.SemaphoreType.DMA((3,))],
-        compiler_params=pltpu.CompilerParams(collective_id=cid, has_side_effects=True),
-        name="gather_four",
-    )(x)
 
 
 def scatter_four_kernel(p_ref, out_ref, from_core, from_pair, send_sem, recv_sem):
@@ -454,7 +447,7 @@
     for r in (8, 7, 9, 4, 12, 5, 11, 6, 10, 3, 13, 2, 14, 1, 15):
         for c in sends(r):
             c.start()
-    yield
+        yield
     for r in range(1, 16):
         at = pl.ds(pl.multiple_of((me.dp + 16 - r) % 16 * depth, depth), depth)
         for j, dst in enumerate((outs[0].at[at], outs[1].at[at], outs[2].at[:, at])):
@@ -545,8 +538,8 @@
     )(weights, rows, gates, normed, *experts)
 
 
-def scatter_pairs(me, chunks, p_ref, out_ref, from_b, from_a, from_far, send_sem, recv_sem):
-    rows = p_ref.shape[1] // chunks
+def scatter_pairs(me, chunks, share, make, out_ref, from_b, from_a, from_far, send_sem, recv_sem):
+    rows = from_a.shape[1] // chunks
     other = me.dp + me.pair
     bases = (me.dp, other, me.dp + me.far, other + me.far)
     items = [(j, k) for j in (2, 3, 1, 0) for k in range(chunks)]
@@ -558,7 +551,7 @@
         return me.copy(src, dst, send_sem.at[slot, k], recv_sem.at[slot, k], to)
 
     def send_b(g, j, k):
-        return copy(p_ref.at[bases[j] + me.db + g * me.da, at(k)], from_b.at[g, j, at(k)], g * 4 + j, k, me.dp + me.db)
+        return copy(share(bases[j] + me.db + g * me.da).at[at(k)], from_b.at[g, j, at(k)], g * 4 + j, k, me.dp + me.db)
 
     def send_a(j, k):
         return copy(from_b.at[1, j, at(k)], from_a.at[j, at(k)], 8 + j, k, me.dp + me.da)
@@ -569,22 +562,31 @@
     def swap(k):
         return copy(from_b.at[0, 1, at(k)], out_ref.at[me.half, at(k)], 14, k, other)
 
-    for j, k in items:
-        send_b(1, j, k).start()
-        send_b(0, j, k).start()
+    for j in (2, 3, 1, 0):
+        for g in (1, 0):
+            make(bases[j] + me.db + g * me.da)
+            for k in range(chunks):
+                send_b(g, j, k).start()
+        if j == 3:
+            yield
+    for j in (2, 3, 1, 0):
+        make(bases[j] + me.da)
+        make(bases[j])
+        if j == 3:
+            yield
     yield
 
     def first(item):
         j, k = item
         send_b(1, j, k).wait_recv()
-        add_rows(from_b.at[1, j, at(k)], (p_ref.at[bases[j] + me.da, at(k)], from_b.at[1, j, at(k)]), rows)
+        add_rows(from_b.at[1, j, at(k)], (share(bases[j] + me.da).at[at(k)], from_b.at[1, j, at(k)]), rows)
         send_a(j, k).start()
 
     def second(item):
         j, k = item
         send_b(0, j, k).wait_recv()
         send_a(j, k).wait_recv()
-        terms = (p_ref.at[bases[j], at(k)], from_b.at[0, j, at(k)], from_a.at[j, at(k)])
+        terms = (share(bases[j]).at[at(k)], from_b.at[0, j, at(k)], from_a.at[j, at(k)])
         if j >= 2:
             add_rows(from_b.at[0, j, at(k)], terms, rows)
             send_far(j - 2, k).start()
@@ -608,8 +610,7 @@
         send_far(1, k).wait_send()
 
 
-def sum_all(me, x_ref, out_ref, held, send_sem, recv_sem):
-    out_ref[...] = x_ref[...]
+def sum_all(me, out_ref, held, send_sem, recv_sem):
     steps = ((me.dp, 1 - me.core), (me.dp + me.da, me.core), (me.dp + me.db, me.core), (me.dp + me.pair, me.core), (me.dp + me.far, me.core))
     yield
     for n, (to, core) in enumerate(steps):
@@ -637,27 +638,34 @@
             for j, src in enumerate(views(d, 1 - me.core))
         ]
 
-    def loads(r):
-        d = (me.dp + r) % 16
-        return [pltpu.make_async_copy(src, own.at[j, r], copy_sem.at[r, j]) for j, src in enumerate(views(d, me.core))]
+    order = (8, 7, 9, 4, 12, 5, 11, 6, 10, 3, 13, 2, 14, 1, 15, 0)
+
+    def loads(n):
+        d = (me.dp + order[n]) % 16
+        return [pltpu.make_async_copy(src, own.at[j, n % 8], copy_sem.at[n % 8, j]) for j, src in enumerate(views(d, me.core))]
 
     def sends(r):
         d = (me.dp + r) % 16
         return [me.copy(held.at[j, r], outs[j].at[me.dp], send_sem.at[r, j], recv_sem.at[r, j], d) for j in range(3)]
 
-    order = (8, 7, 9, 4, 12, 5, 11, 6, 10, 3, 13, 2, 14, 1, 15, 0)
     for r in order:
-        for c in beside(r) + loads(r):
+        for c in beside(r):
+            c.start()
+    for n in range(8):
+        for c in loads(n):
             c.start()
     yield
     keep = [pltpu.make_async_copy(held.at[j, 0], outs[j].at[me.dp], copy_sem.at[16, j]) for j in range(3)]
     for n, r in enumerate(order):
-        for j, (arrives, load) in enumerate(zip(beside(r), loads(r))):
+        for j, (arrives, load) in enumerate(zip(beside(r), loads(n))):
             arrives.wait_recv()
             load.wait()
-            add_rows(held.at[j, r], (own.at[j, r], held.at[j, r]), rows, 64)
+            add_rows(held.at[j, r], (own.at[j, n % 8], held.at[j, r]), rows, 64)
         for c in sends(r) if r else keep:
             c.start()
+        if n < 8:
+            for c in loads(n + 8):
+                c.start()
         if n % 2:
             yield
     for r in range(1, 16):
@@ -672,92 +680,317 @@
             c.wait_send()
 
 
-def scatter_last_kernel(
-    chunks, p_ref, x_ref, gu_ref, down_ref, out_ref, sum_ref, gate_out, up_out, down_out,
-    from_b, from_a, from_far, total, own, held, send_sem, recv_sem, sum_send, sum_recv, core_send, core_recv, e_send, e_recv, copy_sem,
+def attention_back_kernel(
+    chunks, head_dim,
+    ga_ref, w_ref, seq_ref, raw_ref, low_ref, mixed_ref, rope_ref, gain_ref, unit_ref, x_ref, gu_ref, down_ref, share_ref,
+    one_ref, moe_ref, out_ref, sum_ref, gate_out, up_out, down_out,
+    w, ga, gmix, gproj, part, kept, dk, dv, gains, from_core, from_pair,
+    pair_b, pair_a, pair_far, total, own, held,
+    from_b, from_a, from_z, b_send, b_recv, a_send, a_recv, z_send, z_recv,
+    four_send, four_recv, back_send, back_recv, pair_send, pair_recv, sum_send, sum_recv, core_send, core_recv, e_send, e_recv,
+    copy_sem, load_sem,
 ):
     me = Place()
+    rows, width = ga_ref.shape
+    seq_len = 2 * rows
+    q_cols = mixed_ref.shape[1]
+    proj_cols = q_cols + 2 * head_dim
+    group = q_cols // head_dim
+    dot = functools.partial(jnp.dot, preferred_element_type=jnp.float32)
+    dot_t = functools.partial(lax.dot_general, dimension_numbers=(((1,), (1,)), ((), ())), preferred_element_type=jnp.float32)
+    t_dot = functools.partial(lax.dot_general, dimension_numbers=(((0,), (0,)), ((), ())), preferred_element_type=jnp.float32)
+    load = pltpu.make_async_copy(w_ref, w, load_sem.at[8])
+    load.start()
+    keeps = [pltpu.make_async_copy(share_ref.at[n, pl.ds(0, rows)], kept.at[n], load_sem.at[n]) for n in range(8)]
+    for c in keeps:
+        c.start()
     me.greet(everyone=True, partner=True)
-    run(
-        return_experts(me, gu_ref, down_ref, (gate_out, up_out, down_out), own, held, core_send, core_recv, e_send, e_recv, copy_sem),
-        scatter_pairs(me, chunks, p_ref, out_ref, from_b, from_a, from_far, send_sem, recv_sem),
-        sum_all(me, x_ref, sum_ref, total, sum_send, sum_recv),
-    )
-
-
-def scatter_last(p, x, gu, down, cid, chunks=2):
-    _, rows, columns = p.shape
+
+    def ga_at(h, core):
+        return ga.at[pl.ds(pl.multiple_of((2 * h + core) * rows, rows), rows)]
+
+    mine, theirs = ga_at(me.half, me.core), ga_at(1 - me.half, me.core)
+    across = me.copy(ga_ref, mine, four_send.at[0], four_recv.at[0], me.dp + me.pair)
+    beside = me.copy(ga_ref, mine, four_send.at[1], four_recv.at[1], me.dp, 1 - me.core)
+    relay = me.copy(theirs, theirs, four_send.at[2], four_recv.at[2], me.dp, 1 - me.core)
+    across.start()
+    beside.start()
+    mine[...] = ga_ref[...]
+    scatter = ScatterRows(
+        me, lambda n: share_ref.at[n, pl.ds(rows, rows)], lambda n: kept.at[n], from_b, from_a, from_z,
+        (b_send, b_recv, a_send, a_recv, z_send, z_recv),
+    )
+    for m in (1, 2, 3, 0):
+        scatter.send_b(2 * m + 1).start()
+        scatter.send_b(2 * m).start()
+    experts = return_experts(me, gu_ref, down_ref, (gate_out, up_out, down_out), own, held, core_send, core_recv, e_send, e_recv, copy_sem)
+    next(experts)
+    across.wait_recv()
+    relay.start()
+    across.wait_send()
+    beside.wait()
+    next(experts)
+    relay.wait()
+    load.wait()
+    for c in keeps:
+        c.wait()
+
+    def mix(j, _):
+        at = pl.ds(pl.multiple_of(j * 256, 256), 256)
+        at_w = pl.ds(pl.multiple_of(proj_cols + j * 256, 256), 256)
+        gmix[:, at] = dot(ga[...], w[:, at_w]).astype(gmix.dtype)
+        return 0
+
+    lax.fori_loop(0, q_cols // 256, mix, 0)
+    next(experts)
+    gains[...] = jnp.zeros_like(gains)
+    turn = rope_ref[1]
+    cosine = rope_ref[0]
+    causal = lax.broadcasted_iota(jnp.int32, (seq_len, seq_len), 0) >= lax.broadcasted_iota(jnp.int32, (seq_len, seq_len), 1)
+    k_at, v_at = pl.ds(q_cols, head_dim), pl.ds(q_cols + head_dim, head_dim)
+
+    def back(grad, raw, which):
+        grad = grad * cosine + pltpu.roll(grad, head_dim // 2, 1) * turn
+        inverse = lax.rsqrt(jnp.mean(raw * raw, axis=-1, keepdims=True) + epsilon)
+        gains[which] = gains[which] + jnp.sum(grad * (raw * inverse), axis=0, keepdims=True)
+        scaled = grad * gain_ref[which]
+        inner = jnp.mean(scaled * raw, axis=-1, keepdims=True)
+        return inverse * scaled - raw * (inverse * inverse * inverse) * inner
+
+    def head(n, _):
+        at = pl.ds(pl.multiple_of(n // group * seq_len, seq_len), seq_len)
+        cols = pl.ds(pl.multiple_of(n % group * head_dim, head_dim), head_dim)
+        query, key, value, grad = low_ref[at, cols], low_ref[at, k_at], low_ref[at, v_at], gmix[at, cols]
+        exp_scores = jnp.where(causal, jnp.exp(dot_t(query, key)), 0.0)
+        probs = exp_scores / jnp.sum(exp_scores, axis=-1, keepdims=True)
+        grad_probs = dot_t(grad, value)
+        delta = jnp.sum(grad_probs * probs, axis=-1, keepdims=True)
+        grad_scores = (probs * (grad_probs - delta)).astype(query.dtype)
+        grad_query = dot(grad_scores, key) * head_dim ** (-0.5)
+        grad_key = t_dot(grad_scores, query)
+        grad_value = t_dot(probs.astype(query.dtype), grad)
+
+        def begin():
+            dk[...] = grad_key
+            dv[...] = grad_value
+
+        def more():
+            dk[...] = dk[...] + grad_key
+            dv[...] = dv[...] + grad_value
+
+        pl.when(n % group == 0)(begin)
+        pl.when(n % group != 0)(more)
+        gproj[at, cols] = back(grad_query, raw_ref[at, cols], 0).astype(gproj.dtype)
+
+        def close():
+            gproj[at, k_at] = back(dk[...], raw_ref[at, k_at], 1).astype(gproj.dtype)
+            gproj[at, v_at] = dv[...].astype(gproj.dtype)
+
+        pl.when(n % group == group - 1)(close)
+        return 0
+
+    heads = 2 * group
+    quarter = heads // 4
+    for k in range(4):
+        lax.fori_loop(k * quarter, (k + 1) * quarter, head, 0)
+        next(experts)
+        scatter.first((1, 2, 3, 0)[k])
+        if k:
+            scatter.second((1, 2, 3, 0)[k - 1])
+
+    def project(j, _):
+        at = pl.ds(pl.multiple_of(j * 256, 256), 256)
+        part[:, at] = dot_t(gproj[...], w[at, pl.ds(0, proj_cols)]).astype(part.dtype)
+        return 0
+
+    lax.fori_loop(0, width // 256, project, 0)
+
+    def part_at(h, core):
+        return part.at[pl.ds(pl.multiple_of((2 * h + core) * rows, rows), rows)]
+
+    def give(h, slot):
+        return me.copy(part_at(h, 1 - me.core), from_core.at[slot], back_send.at[slot], back_recv.at[slot], me.dp, 1 - me.core)
+
+    give(1 - me.half, 0).start()
+    give(me.half, 1).start()
+    other = me.dp + me.pair
+    bases = (me.dp, other, me.dp + me.far, other + me.far)
+
+    def weight_block(d):
+        at = pl.ds(pl.multiple_of(d * rows, rows), rows)
+        w[at, pl.ds(0, proj_cols)] = t_dot(seq_ref[:, at], gproj[...]).astype(w.dtype)
+        w[at, pl.ds(proj_cols, q_cols)] = t_dot(ga[:, at], mixed_ref[...]).astype(w.dtype)
+
+    pairs = scatter_pairs(me, chunks, lambda d: w.at[pl.ds(pl.multiple_of(d * rows, rows), rows)], weight_block, out_ref, pair_b, pair_a, pair_far, pair_send, pair_recv)
+    next(pairs)
+    give(1 - me.half, 0).wait_recv()
+    add_rows(from_core.at[0], (part_at(1 - me.half, me.core), from_core.at[0]), rows)
+    over = me.copy(from_core.at[0], from_pair, back_send.at[2], back_recv.at[2], me.dp + me.pair)
+    over.start()
+    give(me.half, 1).wait_recv()
+    add_rows(from_core.at[1], (part_at(me.half, me.core), from_core.at[1]), rows)
+    next(pairs)
+    scatter.second(0)
+    next(experts)
+    next(pairs)
+    over.wait_recv()
+    add_rows(one_ref, (from_core.at[1], from_pair), rows)
+    sum_ref[...] = x_ref[...]
+    attn = jnp.sum(one_ref[...] * unit_ref[...], axis=0, keepdims=True)
+    for j in range(width // 128):
+        sum_ref[pl.ds(j, 1), :] = attn[:, j * 128 : (j + 1) * 128]
+    for j in range(2):
+        sum_ref[pl.ds(2 * width // 128 + j, 1), :] = gains[j]
+    scatter.finish(moe_ref)
+    run(pairs, experts, sum_all(me, sum_ref, total, sum_send, sum_recv))
+    scatter.drain()
+    give(0, 0).wait_send()
+    give(0, 1).wait_send()
+    over.wait_send()
+
+
+def attention_back(grad_attn, weights, seq_normed, raw, low, mixed, rope, gain, unit, sums, gu, down, share, cid, chunks=2):
+    rows, width = grad_attn.shape
+    head_dim = rope.shape[-1]
+    columns = weights.shape[1]
     half = down.shape[1] // 2
     hbm, vmem = pl.BlockSpec(memory_space=pl.ANY), pl.BlockSpec(memory_space=pltpu.VMEM)
     dma = pltpu.SemaphoreType.DMA
+    dtype = weights.dtype
+    proj_cols = raw.shape[1] + head_dim
+    whole = jax.ShapeDtypeStruct((rows, width), jnp.float32)
     return pl.pallas_call(
-        functools.partial(scatter_last_kernel, chunks),
-        out_shape=[jax.ShapeDtypeStruct((2, rows, columns), p.dtype), jax.ShapeDtypeStruct(x.shape, x.dtype)]
-        + [jax.ShapeDtypeStruct((16, rows, half), p.dtype)] * 3,
-        in_specs=[vmem, vmem, hbm, hbm],
-        out_specs=[vmem, vmem, hbm, hbm, hbm],
+        functools.partial(attention_back_kernel, chunks, head_dim),
+        out_shape=[whole, whole, jax.ShapeDtypeStruct((2, rows, columns), dtype), jax.ShapeDtypeStruct(sums.shape, sums.dtype)]
+        + [jax.ShapeDtypeStruct((16, rows, half), dtype)] * 3,
+        in_specs=[vmem, hbm] + [vmem] * 8 + [hbm] * 3,
+        out_specs=[vmem] * 4 + [hbm] * 3,
         scratch_shapes=[
-            pltpu.VMEM((2, 4, rows, columns), p.dtype),
-            pltpu.VMEM((4, rows, columns), p.dtype),
-            pltpu.VMEM((2, rows, columns), p.dtype),
-            pltpu.VMEM((2, 5) + x.shape, x.dtype),
-            pltpu.VMEM((3, 16, rows, half), p.dtype),
-            pltpu.VMEM((3, 16, rows, half), p.dtype),
+            pltpu.VMEM(weights.shape, dtype),
+            pltpu.VMEM((4 * rows, width), dtype),
+            pltpu.VMEM(mixed.shape, dtype),
+            pltpu.VMEM((4 * rows, proj_cols), dtype),
+            pltpu.VMEM((4 * rows, width), dtype),
+            pltpu.VMEM((8, rows, width), dtype),
+            pltpu.VMEM((2 * rows, head_dim), jnp.float32),
+            pltpu.VMEM((2 * rows, head_dim), jnp.float32),
+            pltpu.VMEM((2, 1, head_dim), jnp.float32),
+            pltpu.VMEM((2, rows, width), dtype),
+            pltpu.VMEM((rows, width), dtype),
+            pltpu.VMEM((2, 4, rows, columns), dtype),
+            pltpu.VMEM((4, rows, columns), dtype),
+            pltpu.VMEM((2, rows, columns), dtype),
+            pltpu.VMEM((2, 5) + sums.shape, sums.dtype),
+            pltpu.VMEM((3, 8, rows, half), dtype),
+            pltpu.VMEM((3, 16, rows, half), dtype),
+            *scatter_rows_scratch(rows, width, dtype),
+            dma((3,)), dma((3,)),
+            dma((3,)), dma((3,)),
             dma((15, chunks)), dma((15, chunks)),
             dma((5,)), dma((5,)),
             dma((16, 3)), dma((16, 3)),
             dma((16, 3)), dma((16, 3)),
-            dma((17, 3)),
+            dma((17, 3)), dma((9,)),
         ],
-        compiler_params=pltpu.CompilerParams(collective_id=cid, has_side_effects=True, vmem_limit_bytes=LIMIT),
-        name="scatter_last",
-    )(p, x, gu, down)
+        compiler_params=pltpu.CompilerParams(collective_id=cid, has_side_effects=True, vmem_limit_bytes=67_043_328),
+        name="attention_back",
+    )(grad_attn, weights, seq_normed, raw, low, mixed, rope, gain, unit, sums, gu, down, share)
+
+
+class ScatterRows:
+    def __init__(self, me, sent, kept, from_b, from_a, from_z, sems):
+        self.me, self.sent, self.kept = me, sent, kept
+        self.from_b, self.from_a, self.from_z = from_b, from_a, from_z
+        self.b_send, self.b_recv, self.a_send, self.a_recv, self.z_send, self.z_recv = sems
+        self.rows = from_b.shape[1]
+
+    def send_b(self, n):
+        me = self.me
+        return me.copy(self.sent(n), self.from_b.at[n], self.b_send.at[n], self.b_recv.at[n], me.dp + me.db)
+
+    def send_a(self, m):
+        me = self.me
+        return me.copy(self.from_b.at[2 * m + 1], self.from_a.at[m], self.a_send.at[m], self.a_recv.at[m], me.dp + me.da)
+
+    def send_z(self, m):
+        me = self.me
+        return me.copy(self.from_b.at[2 * m], self.from_z.at[me.z], self.z_send.at[m], self.z_recv.at[me.z], me.at_z(me.z_of(m)))
+
+    def first(self, m):
+        n = 2 * m + 1
+        self.send_b(n).wait_recv()
+        add_rows(self.from_b.at[n], (self.kept(n), self.from_b.at[n]), self.rows)
+        self.send_a(m).start()
+
+    def second(self, m):
+        n = 2 * m
+        self.send_b(n).wait_recv()
+        self.send_a(m).wait_recv()
+        add_rows(self.from_b.at[n], (self.kept(n), self.from_b.at[n], self.from_a.at[m]), self.rows)
+        pl.when(m > 0)(lambda: self.send_z(m).start())
+
+    def advance(self, now, lags=(1, 2)):
+        for lag, call in zip(lags, (self.first, self.second)):
+            m = (now - 1 - lag) // 2
+            due = jnp.logical_and((now - 1 - lag) % 2 == 0, jnp.logical_and(now > lag, m < 4))
+            pl.when(due)(lambda: call(m))
+
+    def finish(self, out_ref):
+        me = self.me
+        others = [(me.z + r) % 4 for r in range(1, 4)]
+        for z in others:
+            me.copy(self.from_z.at[z], self.from_z.at[z], self.z_send.at[0], self.z_recv.at[z], me.dp).wait_recv()
+        add_rows(out_ref, (self.from_b.at[0],) + tuple(self.from_z.at[z] for z in others), self.rows)
+
+    def drain(self):
+        for m in range(4):
+            self.send_b(2 * m).wait_send()
+            self.send_b(2 * m + 1).wait_send()
+            self.send_a(m).wait_send()
+            if m:
+                self.send_z(m).wait_send()
+
+
+def scatter_rows_scratch(rows, columns, dtype):
+    dma = pltpu.SemaphoreType.DMA
+    return [
+        pltpu.VMEM((8, rows, columns), dtype),
+        pltpu.VMEM((4, rows, columns), dtype),
+        pltpu.VMEM((4, rows, columns), dtype),
+        dma((8,)), dma((8,)), dma((4,)), dma((4,)), dma((4,)), dma((4,)),
+    ]
 
 
 def experts_kernel(
     x_ref, c_ref, g_ref, gate_ref, up_ref, down_ref,
-    moe_ref, two_ref, gu_out, down_out, xg_ref,
-    wgu, wd, ag, ggu, p, from_b, from_a, from_z, xb, cb,
-    g_send, g_recv, b_send, b_recv, a_send, a_recv, z_send, z_recv, w_send, w_recv, load_sem, tile_sem, keep_sem,
+    share_ref, two_ref, gu_out, down_out, xg_ref,
+    wgu, wd, ag, ggu, share, p, xb, cb, from_b, from_a, from_z, b_send, b_recv, a_send, a_recv, z_send, z_recv,
+    g_send, g_recv, w_send, w_recv, load_sem, tile_sem, keep_sem, share_sem,
 ):
     me = Place()
     rows, width = x_ref.shape
     hidden = wd.shape[0]
     half = hidden // 2
-    low = me.z < 2
-    depth = jnp.where(low, me.z, 3 - me.z)
-    away = jnp.where(low, 1, 0)
     dot = functools.partial(jnp.dot, preferred_element_type=jnp.float32)
     dot_t = functools.partial(lax.dot_general, dimension_numbers=(((1,), (1,)), ((), ())), preferred_element_type=jnp.float32)
     t_dot = functools.partial(lax.dot_general, dimension_numbers=(((0,), (0,)), ((), ())), preferred_element_type=jnp.float32)
     upper, lower = pl.ds(rows, rows), pl.ds(0, rows)
 
-    def z_of(m):
-        t = jnp.where(m == 0, 1 - depth, jnp.where(m == 1, 2, jnp.where(m == 2, 3, depth)))
-        return jnp.where(low, t, 3 - t)
-
-    def block(n):
-        return me.at_z(z_of(n // 2)) + (n % 2) * me.da
+    z_of, block = me.z_of, me.block
 
     def part(source, to, slot, own=False):
         return me.copy(x_ref if own else xg_ref.at[source], xg_ref.at[source], g_send.at[slot], g_recv.at[source], to)
-
-    def onward(m):
-        below = z_of(m) < me.z
-        return jnp.logical_or(jnp.logical_and(below, me.z < 3), jnp.logical_and(jnp.logical_not(below), me.z > 0)), jnp.where(below, 4, -4)
 
     def arrive(m):
         source = me.at_z(z_of(m))
         part(source, me.dp, 0).wait_recv()
-        goes, step = onward(m)
-        pl.when(goes)(lambda: part(source, me.dp + step, 4 + 3 * m).start())
-        part(source, me.dp + me.db, 6 + 3 * m).start()
-        part(source, me.dp + me.da, 5 + 3 * m).start()
+        part(source, me.dp + me.db, 3 + 2 * m).start()
+        part(source, me.dp + me.da, 4 + 2 * m).start()
 
     def arrive_a(m):
         source = me.at_z(z_of(m)) + me.da
         part(source, me.dp, 0).wait_recv()
-        part(source, me.dp + me.db, 13 + m).start()
+        part(source, me.dp + me.db, 11 + m).start()
 
     def loads(n):
         slot = n % 2
@@ -773,48 +1006,14 @@
         for c in loads(n):
             c.start()
 
-    def send_b(i, n):
-        return me.copy(p.at[i, n, upper], from_b.at[i, n], b_send.at[i, n], b_recv.at[i, n], me.dp + me.db)
-
-    def send_a(i, m):
-        return me.copy(from_b.at[i, 2 * m + 1], from_a.at[i, m], a_send.at[i, m], a_recv.at[i, m], me.dp + me.da)
-
-    def slot_z(z, up, at):
-        return jnp.where(up == 1, z, jnp.where(z == at, 4, z))
-
-    def send_z(i, m, up):
-        z = z_of(m)
-        slot = slot_z(z, up, me.z - 1)
-        return me.copy(from_b.at[i, 2 * m], from_z.at[i, slot], z_send.at[i, m], z_recv.at[i, slot], me.dp - 4 + 8 * up)
-
-    def wait_z(i, z, up):
-        slot = slot_z(z, up, me.z)
-        me.copy(from_z.at[i, slot], from_z.at[i, slot], z_send.at[i, 0], z_recv.at[i, slot], me.dp).wait_recv()
-        return from_z.at[i, slot]
-
-    def first(m):
-        for i in range(2):
-            n = 2 * m + 1
-            send_b(i, n).wait_recv()
-            add_rows(from_b.at[i, n], (p.at[i, n, lower], from_b.at[i, n]), rows)
-            send_a(i, m).start()
-
-    def second(m):
-        for i in range(2):
-            n = 2 * m
-            send_b(i, n).wait_recv()
-            send_a(i, m).wait_recv()
-            terms = (p.at[i, n, lower], from_b.at[i, n], from_a.at[i, m])
-            if m in (1, 2):
-                pl.when(depth == 0)(lambda: add_rows(from_b.at[i, n], terms, rows))
-                pl.when(depth == 1)(lambda: add_rows(from_b.at[i, n], terms + (wait_z(i, z_of(m), away),), rows))
-                send_z(i, m, away).start()
-            else:
-                add_rows(from_b.at[i, n], terms, rows)
-                if m == 0:
-                    pl.when(depth == 0)(lambda: send_z(i, 0, away).start())
-
-    own = p.at[1, 7, lower]
+    scatter = ScatterRows(
+        me, lambda n: p.at[n, upper], lambda n: p.at[n, lower], from_b, from_a, from_z, (b_send, b_recv, a_send, a_recv, z_send, z_recv)
+    )
+
+    def keep_share(n):
+        return pltpu.make_async_copy(share.at[n % 2], share_ref.at[n], share_sem.at[n % 2])
+
+    own = p.at[7, lower]
     load = pltpu.make_async_copy(x_ref, own, keep_sem.at[0])
     store = pltpu.make_async_copy(own, xg_ref.at[me.dp], keep_sem.at[1])
     load.start()
@@ -831,11 +1030,11 @@
     locals_ = [pltpu.make_async_copy(src, dst, keep_sem.at[2 + j]) for j, (src, dst) in enumerate(zip(mine, half_of(me.core)))]
     for c in locals_:
         c.start()
-    me.greet(line=True, near=True, partner=True)
-    pl.when(me.z < 3)(lambda: part(me.dp, me.dp + 4, 0, True).start())
-    pl.when(me.z > 0)(lambda: part(me.dp, me.dp - 4, 1, True).start())
+    me.greet(column=True, near=True, partner=True)
+    for m in range(1, 4):
+        part(me.dp, me.at_z(z_of(m)), m - 1, True).start()
     part(me.dp, me.dp + me.db, 3, True).start()
-    part(me.dp, me.dp + me.da, 2, True).start()
+    part(me.dp, me.dp + me.da, 4, True).start()
     shares = [
         me.copy(src, dst, w_send.at[j], w_recv.at[j], me.dp, 1 - me.core) for j, (src, dst) in enumerate(zip(mine, half_of(me.core)))
     ]
@@ -843,8 +1042,7 @@
         c.start()
     load.wait()
     store.start()
-    arrive_a(3)
-    arrive(0)
+    arrive_a(0)
     store.wait()
     for c in locals_:
         c.wait()
@@ -879,24 +1077,25 @@
 
             pl.when(n == k)(go)
 
-        at_step(0, (arrive, 1), (arrive_a, 0))
-        at_step(1, (arrive, 2))
-        at_step(2, (arrive_a, 1))
+        at_step(0, (arrive, 1))
+        at_step(1, (arrive, 2), (arrive_a, 1))
+        at_step(2, (arrive, 3))
         at_step(3, (arrive_a, 2))
+        at_step(4, (arrive_a, 3))
         pl.when(n < 7)(lambda: fetch(n + 1))
+
+        pl.when(n >= 2)(lambda: keep_share(n - 2).wait())
 
         def outer(j, _):
             at = pl.ds(pl.multiple_of(j * 2 * tile, 2 * tile), 2 * tile)
-            p[0, n, :, at] = dot(ag[n], wd[:, at]).astype(p.dtype)
-            p[1, n, :, at] = dot_t(ggu[n], wgu[at, :]).astype(p.dtype)
+            share[slot, :, at] = dot(ag[n], wd[:, at]).astype(p.dtype)
+            p[n, :, at] = dot_t(ggu[n], wgu[at, :]).astype(p.dtype)
             return 0
 
         lax.fori_loop(0, width // (2 * tile), outer, 0)
-        send_b(0, n).start()
-        send_b(1, n).start()
-        at_step(4, (first, 0))
-        at_step(6, (second, 0))
-        at_step(7, (first, 1))
+        scatter.send_b(n).start()
+        keep_share(n).start()
+        scatter.advance(n)
         return 0
 
     lax.fori_loop(0, 8, step, 0)
@@ -951,48 +1150,22 @@
         cb[slot, :, pl.ds(0, hidden)] = t_dot(c_tile, ag[...].reshape(-1, hidden)).astype(cb.dtype)
         for c in outs(i):
             c.start()
-        pl.when(i == 1)(lambda: second(1))
-        pl.when(i == 2)(lambda: first(2))
-        pl.when(i == 4)(lambda: second(2))
-        pl.when(i == 5)(lambda: first(3))
+        scatter.advance(i + 8)
         return 0
 
     lax.fori_loop(0, 8, weight_step, 0)
-    second(3)
-
-    def pass_back():
-        for i in range(2):
-            add_rows(from_b.at[i, 0], (from_b.at[i, 0], wait_z(i, z_of(0), 1 - away)), rows)
-            send_z(i, 0, 1 - away).start()
-
-    pl.when(depth == 1)(pass_back)
-    for i, out_ref in enumerate((moe_ref, two_ref)):
-        here = from_b.at[i, 6]
-        pl.when(me.z == 0)(lambda: add_rows(out_ref, (here, wait_z(i, me.z, 0)), rows))
-        pl.when(me.z == 3)(lambda: add_rows(out_ref, (here, wait_z(i, me.z, 1)), rows))
-        pl.when(depth == 1)(lambda: add_rows(out_ref, (here, wait_z(i, me.z, 0), wait_z(i, me.z, 1)), rows))
+    scatter.finish(two_ref)
 
     for i in (6, 7):
         for c in outs(i):
             c.wait()
     for c in shares:
         c.wait_send()
-    pl.when(me.z < 3)(lambda: part(me.dp, me.dp, 0).wait_send())
-    pl.when(me.z > 0)(lambda: part(me.dp, me.dp, 1).wait_send())
-    part(me.dp, me.dp, 2).wait_send()
-    part(me.dp, me.dp, 3).wait_send()
-    for m in range(4):
-        if m < 3:
-            pl.when(onward(m)[0])(lambda: part(me.dp, me.dp, 4 + 3 * m).wait_send())
-            part(me.dp, me.dp, 5 + 3 * m).wait_send()
-            part(me.dp, me.dp, 6 + 3 * m).wait_send()
-        part(me.dp, me.dp, 13 + m).wait_send()
-        for i in range(2):
-            send_b(i, 2 * m).wait_send()
-            send_b(i, 2 * m + 1).wait_send()
-            send_a(i, m).wait_send()
-            if m < 3:
-                send_z(i, m, away).wait_send()
+    for slot in range(15):
+        part(me.dp, me.dp, slot).wait_send()
+    scatter.drain()
+    keep_share(6).wait()
+    keep_share(7).wait()
 
 
 def expert_layer(x, grads, gates, gate, up, down, cid):
@@ -1004,31 +1177,27 @@
     return pl.pallas_call(
         experts_kernel,
         out_shape=[
-            jax.ShapeDtypeStruct((rows, width), jnp.float32),
+            jax.ShapeDtypeStruct((8, 2 * rows, width), dtype),
             jax.ShapeDtypeStruct((rows, width), jnp.float32),
             jax.ShapeDtypeStruct((width, 4 * half), dtype),
             jax.ShapeDtypeStruct((width, 2 * half), dtype),
             jax.ShapeDtypeStruct((16, rows, width), dtype),
         ],
         in_specs=[hbm, hbm, vmem, hbm, hbm, hbm],
-        out_specs=[vmem, vmem, hbm, hbm, hbm],
+        out_specs=[hbm, vmem, hbm, hbm, hbm],
         scratch_shapes=[
             pltpu.VMEM((width, 4 * half), dtype),
             pltpu.VMEM((2 * half, width), dtype),
             pltpu.VMEM((8, 2 * rows, 2 * half), dtype),
             pltpu.VMEM((8, 2 * rows, 4 * half), dtype),
-            pltpu.VMEM((2, 8, 2 * rows, width), dtype),
-            pltpu.VMEM((2, 8, rows, width), dtype),
-            pltpu.VMEM((2, 4, rows, width), dtype),
-            pltpu.VMEM((2, 5, rows, width), dtype),
+            pltpu.VMEM((2, 2 * rows, width), dtype),
+            pltpu.VMEM((8, 2 * rows, width), dtype),
             pltpu.VMEM((2, 2 * rows, width), dtype),
             pltpu.VMEM((2, 2 * rows, width), dtype),
-            dma((17,)), dma((16,)),
-            dma((2, 8)), dma((2, 8)),
-            dma((2, 4)), dma((2, 4)),
-            dma((2, 4)), dma((2, 5)),
+            *scatter_rows_scratch(rows, width, dtype),
+            dma((15,)), dma((16,)),
             dma((3,)), dma((3,)),
-            dma((2, 4)), dma((2, 2, 16)), dma((5,)),
+            dma((2, 4)), dma((2, 2, 16)), dma((5,)), dma((2,)),
         ],
         compiler_params=pltpu.CompilerParams(collective_id=cid, has_side_effects=True, vmem_limit_bytes=67_043_328),
         name="experts",
@@ -1339,31 +1508,18 @@
     hidden = residual + scatter_four(dot_t(mixed, w_back).astype(low).reshape(2, 2, rows, width), 5)
     inverse_two = rms_inverse(hidden)
     normed_two = (hidden * inverse_two * ffn_gain).astype(low)
-    moe, grad_two, gu_part, down_part, _ = expert_layer(normed_two, rows_grad, gates, *projections, 2)
-    output = (hidden + moe).astype(low)
+    share, grad_two, gu_part, down_part, _ = expert_layer(normed_two, rows_grad, gates, *projections, 2)
     ffn_gain_part = jnp.sum(grad_two * hidden * inverse_two, axis=0)
     grad_hidden = cotangent.astype(jnp.float32) + norm_backward(grad_two, hidden, inverse_two, ffn_gain)
-    grad_attn = gather_pair_rows(grad_hidden.astype(low), 9).reshape(-1, width)
-    grad_mixed = dot(grad_attn, w_back).astype(low).reshape(2, seq_len, group, head_dim)
-    grad_probs = jnp.einsum("bqgd,bsd->bgqs", grad_mixed, value_low, preferred_element_type=jnp.float32)
-    delta_sum = jnp.sum(grad_probs * probs, axis=-1, keepdims=True)
-    grad_scores = (probs * (grad_probs - delta_sum)).astype(low)
-    grad_query = jnp.einsum("bgqs,bsd->bqgd", grad_scores, key_low, preferred_element_type=jnp.float32)
-    grad_key = jnp.einsum("bgqs,bqgd->bsd", grad_scores, query_low, preferred_element_type=jnp.float32)
-    grad_value = jnp.einsum("bgqs,bqgd->bsd", probs_low, grad_mixed, preferred_element_type=jnp.float32)
-    grad_query_norm = rotate_back(grad_query * scale, cosine, sine_table)
-    query_gain_part = jnp.sum(grad_query_norm * query_raw * query_inverse, axis=(0, 1, 2))
-    grad_query_low = norm_backward(grad_query_norm, query_raw, query_inverse, query_gain).astype(low)
-    grad_key_norm = rotate_back(grad_key[:, :, None], cosine, sine_table)
-    key_gain_part = jnp.sum(grad_key_norm * key_raw * key_inverse, axis=(0, 1, 2))
-    grad_key_low = norm_backward(grad_key_norm, key_raw, key_inverse, key_gain).astype(low)
-    grad_proj = jnp.concatenate([v.astype(low).reshape(2 * seq_len, -1) for v in (grad_query_low, grad_key_low, grad_value)], axis=1)
-    grad_one = scatter_four(dot_t(grad_proj, w_proj).astype(low).reshape(2, 2, rows, width), 10)
-    w_parts = jnp.concatenate([t_dot(seq_normed, grad_proj), t_dot(grad_attn, mixed)], axis=1).astype(low)
-    attn_gain_part = jnp.sum(grad_one * residual * inverse_one, axis=0)
-    gains = jnp.concatenate([attn_gain_part, ffn_gain_part, query_gain_part, key_gain_part])
-    gains = jnp.pad(gains, (0, -gains.shape[0] % 1024)).reshape(-1, 128)
-    shares, totals, *grads_moe = scatter_last(w_parts.reshape(-1, rows, w_parts.shape[1]), gains, gu_part, down_part, 11)
+    gains = jnp.pad(ffn_gain_part, (width, 1024)).reshape(-1, 128)
+    raw = proj[:, : q_cols + kv_cols]
+    lows = jnp.concatenate([v.reshape(2 * seq_len, -1) for v in (query_low, key_low, value_low)], axis=1)
+    rope = jnp.stack([jnp.concatenate([v, w], axis=1) for v, w in ((cosine[:, 0], cosine[:, 0]), (sine_table[:, 0], -sine_table[:, 0]))])
+    gain = jnp.stack([query_gain, key_gain])[:, None]
+    grad_one, moe, shares, totals, *grads_moe = attention_back(
+        grad_hidden.astype(low), weights, seq_normed, raw, lows, mixed, rope, gain, residual * inverse_one, gains, gu_part, down_part, share, 9
+    )
+    output = (hidden + moe).astype(low)
     grad_w_gate, grad_w_up, grad_w_down = [v.astype(jnp.float32) for v in grads_moe]
     grad_w_down = jnp.transpose(grad_w_down, (0, 2, 1))
     shares, totals = shares.astype(jnp.float32), totals.reshape(-1)

time: 933 us -> 773 us (0.83)
  Pallas kernels: 793 us -> 697 us
  matrix products: 40.3 us -> 14 us
  other arithmetic: 51.1 us -> 31.7 us
  local copies, waits for them, and re-layouts: 38 us -> 20.5 us
    pallas_call x3 -> x2, Pallas kernels: 484 us -> 443 us  [the longest x1 262 us: attention_back(): pl.pallas_call(functools.partial(attention_back_kernel, chunks, head_dim)...]
    pallas_call x2 -> x1, Pallas kernels: 53.3 us -> 19 us  [scatter_four(): pl.pallas_call(scatter_four_kernel, out_shape=jax.ShapeDtypeStruct((rows,...]
    dot_general x8 -> x0, matrix products: 25.1 us -> none  [the longest x1 7.24 us: per_device_relay(): t_dot(seq_normed, grad_proj)]
    pallas_call x1, Pallas kernels: 256 us -> 235 us  [gather_first(): pl.pallas_call(gather_first_kernel, out_shape=[jax.ShapeDtypeStruct((16,)...]
where the time goes in v5:
time: 773 us; the launch traced here: 764 us
  Pallas kernels  697 us (90%)
  other arithmetic  31.7 us (4%)
  local copies, waits for them, and re-layouts  20.5 us (3%)
  matrix products  14 us (2%)
    pallas_call x1, Pallas kernels, attention_back(): pl.pallas_call(functools.partial(attention_back_kernel, chunks, head_dim)...  262 us
    pallas_call x1, Pallas kernels, gather_first(): pl.pallas_call(gather_first_kernel, out_shape=[jax.ShapeDtypeStruct((16,)...  235 us
    pallas_call x1, Pallas kernels, expert_layer(): pl.pallas_call(experts_kernel, out_shape=[jax.ShapeDtypeStruct((8, 2 * ro...  181 us
    pallas_call x1, Pallas kernels, scatter_four(): pl.pallas_call(scatter_four_kernel, out_shape=jax.ShapeDtypeStruct((rows,...  19 us

profile of v5, /device:TPU:0, one launch (start us, length us, event | category | flops | bytes accessed | tf_op | source)
XLA Modules:
  0.0 764.5 jit_solution(11628547516696397347)
XLA Ops:
  0.7 1.3 fusion.13
  2.5 1.2 pad_maximum_fusion.5
  9.8 1.1 pad_maximum_fusion.w_ref
  10.9 1.3 convert_multiply_fusion.2
  12.2 234.5 %gather_first.1 = (bf16[16,128,2304]{2,1,0:T(8,128)(2,1)}, bf16[16,128,2048]{2,1,0:T(8,128)(2,1)}, f32[16,8,128]{2,1,0:T(8,128)}, bf16[2,2,128,2048]{3,2,1,0:T(8...) custom-call(bf16[2,128,2304]{2,1,0:T(8,128)(2,1)} %pad_maximum_fusion.w_ref, ...), custom_call_target="tpu_custom_call" | custom-call | tf_op jit(solution)/shard_map/gather_first/pallas_call | solution.py:512
  247.6 1.3 copy.78.g_ref
  249.0 6.0 fusion
  256.4 1.1 multiply_multiply_fusion
  258.6 1.6 slice.124.raw_ref
  264.6 2.2 concatenate.56.low_ref
  269.6 1.3 copy.97
  270.8 6.0 fusion.5
  276.8 19.0 %scatter_four.1 = f32[128,2048]{1,0:T(8,128)} custom-call(bf16[2,2,128,2048]{3,2,1,0:T(8,128)(2,1)} %bitcast.108), custom_call_target="tpu_custom_call" | custom-call | tf_op jit(solution)/shard_map/scatter_four/pallas_call | solution.py:258
  295.8 1.5 multiply_reduce_fusion.3
  299.3 181.4 %experts.1 = (bf16[8,256,2048]{2,1,0:T(8,128)(2,1)}, f32[128,2048]{1,0:T(8,128)}, bf16[2048,1536]{1,0:T(8,128)(2,1)}, bf16[2048,768]{1,0:T(8,128)(2,1)}, bf16[16,128,2048]{2,1,0:T(8,128)(2,1)}) custom-call(bf16[128,2048]{1,0:T(8,128)(2,1)} %multiply_convert_fusion.x_ref, bf16[16,128,2048]{2,1,0:T(8,128)(2,1)} %get-tuple-element.33.c_ref, ...), custom_call_target="tpu_custom_call" | custom-call | tf_op jit(solution)/shard_map/experts/pallas_call | solution.py:1177
  480.8 2.0 multiply_reduce_fusion.1
  483.4 2.6 fusion.27
  486.0 261.9 %attention_back.1 = (f32[128,2048]{1,0:T(8,128)}, f32[128,2048]{1,0:T(8,128)}, bf16[2,128,2304]{2,1,0:T(8,128)(2,1)}, f32[40,128]{1,0:T(8,128)}, bf16[16,128,384...) custom-call(bf16[128,2048]{1,0:T(8,128)(2,1)} %get-tuple-element.116.ga_ref, ...), custom_call_target="tpu_custom_call" | custom-call | tf_op jit(solution)/shard_map/attention_back/pallas_call | solution.py:862
  747.9 2.6 add_convert_fusion
  750.8 1.3 fusion.17
  753.7 1.3 copy.80
  757.3 2.0 convert_element_type.72
  759.3 2.0 convert_element_type.73
  761.7 2.4 copy.81
  (109 shorter events, 24.2 us)
Async XLA Ops:
  0.6 8.7 %copy-start.13 = (bf16[2048,128]{1,0:T(8,128)(2,1)S(1)}, bf16[2048,128]{1,0:T(8,128)(2,1)}, u32[]{:S(2)}) copy-start(bf16[2048,128]{1,0:T(8,128)(2,1)} %param.22) | copy-start | bytes 1572868
  1.9 7.7 %copy-start.14 = (bf16[128,2048]{1,0:T(8,128)(2,1)S(1)}, bf16[128,2048]{1,0:T(8,128)(2,1)}, u32[]{:S(2)}) copy-start(bf16[128,2048]{1,0:T(8,128)(2,1)} %param.19) | copy-start | bytes 1572868
  2.5 8.4 %copy-start.23 = (f32[128]{0:T(128)}, f32[128]{0:T(128)S(1)}, u32[]{:S(2)}) copy-start(f32[128]{0:T(128)S(1)} %get-tuple-element.149) | copy-start | bytes 1540
  9.7 1.2 copy-start.2
  9.7 1.2 copy-start.18
  249.0 7.4 copy-start.25
  264.3 2.5 copy-start.12
  295.8 2.5 copy-start.16
  480.7 2.6 copy-start.1
  480.7 2.6 copy-start.5
  480.7 2.6 copy-start.17
  480.7 2.6 copy-start.22
  480.7 2.6 copy-start.28
  747.8 2.7 copy-start.3
  747.8 2.7 copy-start.6
  747.8 2.7 copy-start.19
  747.9 2.9 copy-start.4
  747.9 2.9 copy-start.24
  747.9 2.9 copy-start.27
  750.5 1.6 copy-start.20
  750.5 2.7 copy-start.10
  755.0 2.4 copy-start.9
  757.3 2.0 copy-start.8
  759.3 2.0 copy-start.7
  (5 other events, 4.2 us)

commit v6 on v5

--- a/solution.py
+++ b/solution.py
@@ -228,55 +228,27 @@
     lax.fori_loop(0, rows // block, body, 0)
 
 
-def scatter_four_kernel(p_ref, out_ref, from_core, from_pair, send_sem, recv_sem):
-    me = Place()
-    rows = p_ref.shape[2]
-    me.greet(chain=True, partner=True)
-
-    def beside(h, slot):
-        return me.copy(p_ref.at[h, 1 - me.core], from_core.at[slot], send_sem.at[slot], recv_sem.at[slot], me.dp, 1 - me.core)
-
-    first, second = beside(1 - me.half, 0), beside(me.half, 1)
-    first.start()
-    second.start()
-    first.wait_recv()
-    add_rows(from_core.at[0], (p_ref.at[1 - me.half, me.core], from_core.at[0]), rows)
-    across = me.copy(from_core.at[0], from_pair, send_sem.at[2], recv_sem.at[2], me.dp + me.pair)
-    across.start()
-    second.wait_recv()
-    add_rows(from_core.at[1], (p_ref.at[me.half, me.core], from_core.at[1]), rows)
-    across.wait_recv()
-    add_rows(out_ref, (from_core.at[1], from_pair), rows)
-    across.wait_send()
-    first.wait_send()
-    second.wait_send()
-
-
-def scatter_four(p, cid):
-    _, _, rows, columns = p.shape
-    vmem = pl.BlockSpec(memory_space=pltpu.VMEM)
-    return pl.pallas_call(
-        scatter_four_kernel,
-        out_shape=jax.ShapeDtypeStruct((rows, columns), jnp.float32),
-        in_specs=[vmem],
-        out_specs=vmem,
-        scratch_shapes=[
-            pltpu.VMEM((2, rows, columns), p.dtype),
-            pltpu.VMEM((rows, columns), p.dtype),
-            pltpu.SemaphoreType.DMA((3,)),
-            pltpu.SemaphoreType.DMA((3,)),
-        ],
-        compiler_params=pltpu.CompilerParams(collective_id=cid, has_side_effects=True),
-        name="scatter_four",
-    )(p)
-
-
 def run(*threads):
     threads = list(threads)
     while threads:
         for thread in list(threads):
             if next(thread, "end") == "end":
                 threads.remove(thread)
+
+
+class Threads:
+    def __init__(self, *threads):
+        self.threads = list(threads)
+
+    def step(self, times=1):
+        for _ in range(times):
+            for thread in list(self.threads):
+                if next(thread, "end") == "end":
+                    self.threads.remove(thread)
+
+    def finish(self):
+        while self.threads:
+            self.step()
 
 
 def lagged(items, first, second, lag):
@@ -474,68 +446,171 @@
     relay.wait()
 
 
-def gather_first_kernel(
-    w_ref, c_ref, g_ref, x_ref, gate_ref, up_ref, down_ref,
-    w_out, c_out, g_out, x_out, gate_out, up_out, down_out,
-    w_own, c_own, e_own, w_send, w_recv, c_send, c_recv, g_send, g_recv, x_send, x_recv, e_send, e_recv, copy_sem,
+def attention_first_kernel(
+    head_dim, start,
+    w_ref, c_ref, g_ref, x_ref, rope_ref, gain_ref, gate_ref, up_ref, down_ref,
+    w_out, c_out, g_out, seq, raw, low, mixed, sum_ref, gate_out, up_out, down_out,
+    w, c_own, e_own, part, from_core, from_pair,
+    w_send, w_recv, c_send, c_recv, g_send, g_recv, x_send, x_recv, e_send, e_recv, back_send, back_recv, copy_sem,
 ):
     me = Place()
+    rows, width = x_ref.shape
+    seq_len = 2 * rows
+    q_cols = mixed.shape[1]
+    proj_cols = q_cols + 2 * head_dim
+    group = q_cols // head_dim
     depth = gate_ref.shape[1]
-    at = pl.ds(pl.multiple_of(me.dp * depth, depth), depth)
+    dot = functools.partial(jnp.dot, preferred_element_type=jnp.float32)
+    dot_t = functools.partial(lax.dot_general, dimension_numbers=(((1,), (1,)), ((), ())), preferred_element_type=jnp.float32)
+    at_mine = pl.ds(pl.multiple_of(me.dp * depth, depth), depth)
     ends = [
-        keep_own(w_ref.at[me.half], w_own, w_out.at[me.dp], copy_sem.at[0]),
         keep_own(c_ref, c_own, c_out.at[me.dp], copy_sem.at[1]),
-        keep_own(gate_ref.at[me.dp], e_own.at[0], gate_out.at[at], copy_sem.at[2]),
-        keep_own(up_ref.at[me.dp], e_own.at[1], up_out.at[at], copy_sem.at[3]),
+        keep_own(gate_ref.at[me.dp], e_own.at[0], gate_out.at[at_mine], copy_sem.at[2]),
+        keep_own(up_ref.at[me.dp], e_own.at[1], up_out.at[at_mine], copy_sem.at[3]),
     ]
-    flat = pltpu.make_async_copy(down_ref.at[me.dp], down_out.at[:, at], copy_sem.at[4, 0])
+    flat = pltpu.make_async_copy(down_ref.at[me.dp], down_out.at[:, at_mine], copy_sem.at[4, 0])
     flat.start()
+    kept = pltpu.make_async_copy(w_ref.at[me.half], w.at[me.dp], copy_sem.at[0, 0])
+    kept.start()
     g_out[me.dp] = g_ref[me.dp]
     me.greet(everyone=True, partner=True)
-    run(
-        gather_four(me, x_ref, x_out, x_send, x_recv),
-        gather_pairs(me, w_ref, w_out, w_send, w_recv),
-        gather_line(me, c_ref, c_out, c_send, c_recv),
+    beside = Threads(
         swap_rows(me, g_ref, g_out, g_send, g_recv),
         share_experts(me, (gate_ref, up_ref, down_ref), (gate_out, up_out, down_out), e_send, e_recv),
     )
+    needed = Threads(gather_four(me, x_ref, seq, x_send, x_recv), gather_pairs(me, w_ref, w, w_send, w_recv))
+    rounds = 0
+    while needed.threads:
+        needed.step()
+        if rounds == start:
+            beside.threads.insert(0, gather_line(me, c_ref, c_out, c_send, c_recv))
+        beside.step()
+        rounds += 1
+    kept.wait()
+    store = pltpu.make_async_copy(w, w_out, copy_sem.at[0, 1])
+    store.start()
+    weights = w.reshape(16 * rows, w.shape[2])
+
+    def row_block(ref, h, core):
+        return ref.at[pl.ds(pl.multiple_of((2 * h + core) * rows, rows), rows)]
+
+    seqs = seq.reshape(4 * rows, width)
+    q_part, k_part = pl.ds(0, q_cols), pl.ds(q_cols, 2 * head_dim)
+
+    def project(j, _):
+        at = pl.ds(pl.multiple_of(j * 256, 256), 256)
+        raw[:, at] = dot(seqs[...], weights[:, at])
+        return 0
+
+    lax.fori_loop(0, q_cols // 256, project, 0)
+    keys = dot(seqs[...], weights[:, k_part])
+    raw[:, pl.ds(q_cols, head_dim)] = keys[:, :head_dim]
+    low[:, pl.ds(q_cols + head_dim, head_dim)] = keys[:, head_dim:].astype(low.dtype)
+    beside.step()
+    cosine, turn = rope_ref[0], rope_ref[1]
+
+    def turned(at, cols, which, scale):
+        values = raw[at, cols]
+        values = values * lax.rsqrt(jnp.mean(values * values, axis=-1, keepdims=True) + epsilon) * gain_ref[which]
+        return ((values * cosine - pltpu.roll(values, head_dim // 2, 1) * turn) * scale).astype(low.dtype)
+
+    k_at, v_at = pl.ds(q_cols, head_dim), pl.ds(q_cols + head_dim, head_dim)
+    for b in range(2):
+        at = pl.ds(b * seq_len, seq_len)
+        low[at, k_at] = turned(at, k_at, 1, 1.0)
+    causal = lax.broadcasted_iota(jnp.int32, (seq_len, seq_len), 0) >= lax.broadcasted_iota(jnp.int32, (seq_len, seq_len), 1)
+
+    def head(n, _):
+        at = pl.ds(pl.multiple_of(n // group * seq_len, seq_len), seq_len)
+        cols = pl.ds(pl.multiple_of(n % group * head_dim, head_dim), head_dim)
+        query = turned(at, cols, 0, head_dim ** (-0.5))
+        low[at, cols] = query
+        exp_scores = jnp.where(causal, jnp.exp(dot_t(query, low[at, k_at])), 0.0)
+        probs = exp_scores / jnp.sum(exp_scores, axis=-1, keepdims=True)
+        mixed[at, cols] = dot(probs.astype(low.dtype), low[at, v_at]).astype(mixed.dtype)
+        return 0
+
+    quarter = group // 2
+    for k in range(4):
+        lax.fori_loop(k * quarter, (k + 1) * quarter, head, 0)
+        beside.step()
+
+    def project_back(j, _):
+        at = pl.ds(pl.multiple_of(j * 256, 256), 256)
+        part[:, at] = dot_t(mixed[...], weights[at, pl.ds(proj_cols, q_cols)]).astype(part.dtype)
+        return 0
+
+    lax.fori_loop(0, width // 256, project_back, 0)
+
+    def give(h, slot):
+        return me.copy(row_block(part, h, 1 - me.core), from_core.at[slot], back_send.at[slot], back_recv.at[slot], me.dp, 1 - me.core)
+
+    give(1 - me.half, 0).start()
+    give(me.half, 1).start()
+    beside.step()
+    give(1 - me.half, 0).wait_recv()
+    add_rows(from_core.at[0], (row_block(part, 1 - me.half, me.core), from_core.at[0]), rows)
+    over = me.copy(from_core.at[0], from_pair, back_send.at[2], back_recv.at[2], me.dp + me.pair)
+    over.start()
+    give(me.half, 1).wait_recv()
+    add_rows(from_core.at[1], (row_block(part, me.half, me.core), from_core.at[1]), rows)
+    beside.step()
+    over.wait_recv()
+    add_rows(sum_ref, (from_core.at[1], from_pair), rows)
+    beside.finish()
     for end in ends:
         end()
     flat.wait()
-
-
-def gather_first(weights, rows, gates, normed, experts, cid):
+    store.wait()
+    give(0, 0).wait_send()
+    give(0, 1).wait_send()
+    over.wait_send()
+
+
+def attention_first(weights, rows, gates, normed, rope, gain, experts, cid, start=4):
     hbm, vmem = pl.BlockSpec(memory_space=pl.ANY), pl.BlockSpec(memory_space=pltpu.VMEM)
     dma = pltpu.SemaphoreType.DMA
     dtype = rows.dtype
     _, depth, hidden = experts[0].shape
+    block, width = rows.shape
+    head_dim = rope.shape[-1]
+    columns = weights.shape[2]
+    q_cols = (columns - 2 * head_dim) // 2
     return pl.pallas_call(
-        gather_first_kernel,
+        functools.partial(attention_first_kernel, head_dim, start),
         out_shape=[
             jax.ShapeDtypeStruct((16,) + weights.shape[1:], dtype),
-            jax.ShapeDtypeStruct((16,) + rows.shape, dtype),
+            jax.ShapeDtypeStruct((16, block, width), dtype),
             jax.ShapeDtypeStruct(gates.shape, gates.dtype),
-            jax.ShapeDtypeStruct((2, 2) + normed.shape, dtype),
+            jax.ShapeDtypeStruct((2, 2, block, width), dtype),
+            jax.ShapeDtypeStruct((4 * block, q_cols + head_dim), jnp.float32),
+            jax.ShapeDtypeStruct((4 * block, q_cols + 2 * head_dim), dtype),
+            jax.ShapeDtypeStruct((4 * block, q_cols), dtype),
+            jax.ShapeDtypeStruct((block, width), jnp.float32),
             jax.ShapeDtypeStruct((16 * depth, hidden), dtype),
             jax.ShapeDtypeStruct((16 * depth, hidden), dtype),
             jax.ShapeDtypeStruct((hidden, 16 * depth), dtype),
         ],
-        in_specs=[hbm, hbm, vmem, vmem, hbm, hbm, hbm],
-        out_specs=[hbm, hbm, vmem, vmem, hbm, hbm, hbm],
+        in_specs=[hbm, hbm, vmem, vmem, vmem, vmem, hbm, hbm, hbm],
+        out_specs=[hbm, hbm] + [vmem] * 6 + [hbm] * 3,
         scratch_shapes=[
-            pltpu.VMEM(weights.shape[1:], dtype),
-            pltpu.VMEM(rows.shape, dtype),
+            pltpu.VMEM((16,) + weights.shape[1:], dtype),
+            pltpu.VMEM((block, width), dtype),
             pltpu.VMEM((2, depth, hidden), dtype),
+            pltpu.VMEM((4 * block, width), dtype),
+            pltpu.VMEM((2, block, width), dtype),
+            pltpu.VMEM((block, width), dtype),
             dma((15,)), dma((16,)),
             dma((29,)), dma((16,)),
             dma((16,)), dma((16,)),
             dma((3,)), dma((3,)),
             dma((16, 3)), dma((16, 3)),
+            dma((3,)), dma((3,)),
             dma((5, 2)),
         ],
-        compiler_params=pltpu.CompilerParams(collective_id=cid, has_side_effects=True),
-        name="gather_first",
-    )(weights, rows, gates, normed, *experts)
+        compiler_params=pltpu.CompilerParams(collective_id=cid, has_side_effects=True, vmem_limit_bytes=67_043_328),
+        name="attention_first",
+    )(weights, rows, gates, normed, rope, gain, *experts)
 
 
 def scatter_pairs(me, chunks, share, make, out_ref, from_b, from_a, from_far, send_sem, recv_sem):
@@ -1483,39 +1558,21 @@
     residual = tokens.astype(jnp.float32)
     inverse_one = rms_inverse(residual)
     normed_one = (residual * inverse_one * attn_gain).astype(low)
-    weights, rows_grad, gates, seq_normed, *projections = gather_first(halves, cotangent, gates, normed_one, (w_gate, w_up, w_down), 1)
+    cosine, sine_table = rotary_tables(2 * rows, head_dim)
+    rope = jnp.stack([jnp.concatenate([v, w], axis=1) for v, w in ((cosine[:, 0], cosine[:, 0]), (sine_table[:, 0], -sine_table[:, 0]))])
+    gain = jnp.stack([query_gain, key_gain])[:, None]
+    weights, rows_grad, gates, seq_normed, raw, lows, mixed, attended, *projections = attention_first(
+        halves, cotangent, gates, normed_one, rope, gain, (w_gate, w_up, w_down), 1
+    )
     weights, gates, seq_normed = weights.reshape(-1, weights.shape[2]), gates[:, 0][:, :, None], seq_normed.reshape(-1, width)
     proj_cols = q_cols + 2 * kv_cols
-    w_proj, w_back = weights[:, :proj_cols], weights[:, proj_cols:]
-
-    seq_len = 2 * rows
-    group = q_cols // head_dim
-    scale = head_dim ** (-0.5)
-    cosine, sine_table = rotary_tables(seq_len, head_dim)
-    proj = dot(seq_normed, w_proj)
-    query_raw = proj[:, :q_cols].reshape(2, seq_len, group, head_dim)
-    key_raw = proj[:, q_cols : q_cols + kv_cols].reshape(2, seq_len, 1, head_dim)
-    value_low = proj[:, q_cols + kv_cols :].astype(low).reshape(2, seq_len, head_dim)
-    query_inverse, key_inverse = rms_inverse(query_raw), rms_inverse(key_raw)
-    query_low = (rotate(query_raw * query_inverse * query_gain, cosine, sine_table) * scale).astype(low)
-    key_low = rotate(key_raw * key_inverse * key_gain, cosine, sine_table).astype(low)[:, :, 0]
-    causal = jnp.arange(seq_len)[:, None] >= jnp.arange(seq_len)[None, :]
-    scores = jnp.einsum("bqgd,bsd->bgqs", query_low, key_low, preferred_element_type=jnp.float32)
-    exp_scores = jnp.where(causal, jnp.exp(scores), 0.0)
-    probs = exp_scores / jnp.sum(exp_scores, axis=-1, keepdims=True)
-    probs_low = probs.astype(low)
-    mixed = jnp.einsum("bgqs,bsd->bqgd", probs_low, value_low, preferred_element_type=jnp.float32).astype(low).reshape(2 * seq_len, q_cols)
-    hidden = residual + scatter_four(dot_t(mixed, w_back).astype(low).reshape(2, 2, rows, width), 5)
+    hidden = residual + attended
     inverse_two = rms_inverse(hidden)
     normed_two = (hidden * inverse_two * ffn_gain).astype(low)
     share, grad_two, gu_part, down_part, _ = expert_layer(normed_two, rows_grad, gates, *projections, 2)
     ffn_gain_part = jnp.sum(grad_two * hidden * inverse_two, axis=0)
     grad_hidden = cotangent.astype(jnp.float32) + norm_backward(grad_two, hidden, inverse_two, ffn_gain)
     gains = jnp.pad(ffn_gain_part, (width, 1024)).reshape(-1, 128)
-    raw = proj[:, : q_cols + kv_cols]
-    lows = jnp.concatenate([v.reshape(2 * seq_len, -1) for v in (query_low, key_low, value_low)], axis=1)
-    rope = jnp.stack([jnp.concatenate([v, w], axis=1) for v, w in ((cosine[:, 0], cosine[:, 0]), (sine_table[:, 0], -sine_table[:, 0]))])
-    gain = jnp.stack([query_gain, key_gain])[:, None]
     grad_one, moe, shares, totals, *grads_moe = attention_back(
         grad_hidden.astype(low), weights, seq_normed, raw, lows, mixed, rope, gain, residual * inverse_one, gains, gu_part, down_part, share, 9
     )

time: 773 us -> 765 us (0.990)
  Pallas kernels: 697 us -> 726 us
  matrix products: 14 us -> 0 us
  local copies, waits for them, and re-layouts: 20.5 us -> 11.8 us
    pallas_call x1, Pallas kernels: 181 us -> 205 us  [expert_layer(): pl.pallas_call(experts_kernel, out_shape=[jax.ShapeDtypeStruct((8, 2 * ro...]
    dot_general x4 -> x0, matrix products: 14 us -> none  [the longest x1 6 us: per_device_relay(): proj = dot(seq_normed, w_proj)]
    pallas_call x2 -> x1, Pallas kernels: 253 us -> 260 us  [attention_first(): pl.pallas_call(functools.partial(attention_first_kernel, head_dim, start)...]
where the time goes in v6:
time: 765 us; the launch traced here: 764 us
  Pallas kernels  726 us (95%)
  other arithmetic  25.7 us (3%)
  local copies, waits for them, and re-layouts  11.8 us (2%)
    pallas_call x1, Pallas kernels, attention_first(): pl.pallas_call(functools.partial(attention_first_kernel, head_dim, start)...  260 us
    pallas_call x1, Pallas kernels, attention_back(): pl.pallas_call(functools.partial(attention_back_kernel, chunks, head_dim)...  260 us
    pallas_call x1, Pallas kernels, expert_layer(): pl.pallas_call(experts_kernel, out_shape=[jax.ShapeDtypeStruct((8, 2 * ro...  205 us

profile of v6, /device:TPU:0, one launch (start us, length us, event | category | flops | bytes accessed | tf_op | source)
XLA Modules:
  0.0 764.0 jit_solution(2786765317349539801)
XLA Ops:
  0.7 1.3 fusion
  2.5 1.2 pad_maximum_fusion.5
  3.7 0.7 constant_dynamic-slice_fusion.1
  5.8 0.8 fusion.12
  6.5 0.8 fusion.13
  8.0 0.7 pad_maximum_fusion.2.rope_ref
  9.1 1.1 pad_maximum_fusion.w_ref
  10.3 1.3 convert_multiply_fusion.2
  11.6 260.3 %attention_first.1 = (bf16[16,128,2304]{2,1,0:T(8,128)(2,1)}, bf16[16,128,2048]{2,1,0:T(8,128)(2,1)}, f32[16,8,128]{2,1,0:T(8,128)}, bf16[2,2,128,2048]{3,2,1,0:...) custom-call(bf16[2,128,2304]{2,1,0:T(8,128)(2,1)} %pad_maximum_fusio, ...), custom_call_target="tpu_custom_call" | custom-call | tf_op jit(solution)/shard_map/attention_first/pallas_call | solution.py:579
  271.9 1.6 multiply_reduce_fusion.2
  274.1 0.8 slice.63
  275.0 0.9 multiply_convert_fusion.x_ref
  275.9 1.3 copy.41.g_ref
  277.3 205.0 %experts.1 = (bf16[8,256,2048]{2,1,0:T(8,128)(2,1)}, f32[128,2048]{1,0:T(8,128)}, bf16[2048,1536]{1,0:T(8,128)(2,1)}, bf16[2048,768]{1,0:T(8,128)(2,1)}, bf16[16,128,2048]{2,1,0:T(8,128)(2,1)}) custom-call(bf16[128,2048]{1,0:T(8,128)(2,1)} %multiply_convert_fusion.x_ref, bf16[16,128,2048]{2,1,0:T(8,128)(2,1)} %get-tuple-element.36.c_ref, ...), custom_call_target="tpu_custom_call" | custom-call | tf_op jit(solution)/shard_map/experts/pallas_call | solution.py:1252
  482.4 2.0 multiply_reduce_fusion
  485.0 2.6 fusion.9
  487.6 260.2 %attention_back.1 = (f32[128,2048]{1,0:T(8,128)}, f32[128,2048]{1,0:T(8,128)}, bf16[2,128,2304]{2,1,0:T(8,128)(2,1)}, f32[40,128]{1,0:T(8,128)}, bf16[16,128,384...) custom-call(bf16[128,2048]{1,0:T(8,128)(2,1)} %get-tuple-element.98.ga_ref, ...), custom_call_target="tpu_custom_call" | custom-call | tf_op jit(solution)/shard_map/attention_back/pallas_call | solution.py:937
  747.8 2.6 add_convert_fusion
  750.7 1.3 fusion.4
  753.6 1.3 copy.42
  756.2 1.0 pad_maximum_fusion.1
  757.3 2.0 convert_element_type.41
  759.3 2.0 convert_element_type.42
  761.6 2.4 copy.43
  (73 shorter events, 7.7 us)
Async XLA Ops:
  0.6 8.1 %copy-start.11 = (bf16[2048,128]{1,0:T(8,128)(2,1)S(1)}, bf16[2048,128]{1,0:T(8,128)(2,1)}, u32[]{:S(2)}) copy-start(bf16[2048,128]{1,0:T(8,128)(2,1)} %param.22) | copy-start | bytes 1572868
  2.5 7.8 %copy-start.20 = (f32[128]{0:T(128)}, f32[128]{0:T(128)S(1)}, u32[]{:S(2)}) copy-start(f32[128]{0:T(128)S(1)} %get-tuple-element.125) | copy-start | bytes 1540
  7.8 1.1 copy-start.12
  9.1 1.1 copy-start.2
  9.1 1.1 copy-start.15
  271.9 3.0 copy-start.13
  273.5 1.4 copy-start
  274.1 0.9 copy-start.18
  482.3 2.6 copy-start.1
  482.3 2.6 copy-start.5
  482.3 2.6 copy-start.14
  482.3 2.6 copy-start.19
  482.3 2.6 copy-start.23
  747.7 2.7 copy-start.3
  747.7 2.7 copy-start.6
  747.8 2.7 copy-start.16
  747.8 2.9 copy-start.4
  747.8 2.9 copy-start.21
  747.8 2.9 copy-start.22
  750.7 1.3 copy-start.17
  750.7 2.4 copy-start.10
  754.9 2.4 copy-start.9
  757.3 2.0 copy-start.8
  759.3 2.0 copy-start.7

commit v7 on v6

--- a/solution.py
+++ b/solution.py
@@ -567,7 +567,7 @@
     over.wait_send()
 
 
-def attention_first(weights, rows, gates, normed, rope, gain, experts, cid, start=4):
+def attention_first(weights, rows, gates, normed, rope, gain, experts, cid, start=14):
     hbm, vmem = pl.BlockSpec(memory_space=pl.ANY), pl.BlockSpec(memory_space=pltpu.VMEM)
     dma = pltpu.SemaphoreType.DMA
     dtype = rows.dtype
@@ -799,12 +799,12 @@
         scatter.send_b(2 * m + 1).start()
         scatter.send_b(2 * m).start()
     experts = return_experts(me, gu_ref, down_ref, (gate_out, up_out, down_out), own, held, core_send, core_recv, e_send, e_recv, copy_sem)
-    next(experts)
+    for _ in range(9):
+        next(experts)
     across.wait_recv()
     relay.start()
     across.wait_send()
     beside.wait()
-    next(experts)
     relay.wait()
     load.wait()
     for c in keeps:
@@ -817,7 +817,6 @@
         return 0
 
     lax.fori_loop(0, q_cols // 256, mix, 0)
-    next(experts)
     gains[...] = jnp.zeros_like(gains)
     turn = rope_ref[1]
     cosine = rope_ref[0]
@@ -868,7 +867,6 @@
     quarter = heads // 4
     for k in range(4):
         lax.fori_loop(k * quarter, (k + 1) * quarter, head, 0)
-        next(experts)
         scatter.first((1, 2, 3, 0)[k])
         if k:
             scatter.second((1, 2, 3, 0)[k - 1])
@@ -906,7 +904,6 @@
     add_rows(from_core.at[1], (part_at(me.half, me.core), from_core.at[1]), rows)
     next(pairs)
     scatter.second(0)
-    next(experts)
     next(pairs)
     over.wait_recv()
     add_rows(one_ref, (from_core.at[1], from_pair), rows)

time: 765 us -> 712 us (0.931)
  Pallas kernels: 726 us -> 672 us
    pallas_call x1, Pallas kernels: 205 us -> 179 us  [expert_layer(): pl.pallas_call(experts_kernel, out_shape=[jax.ShapeDtypeStruct((8, 2 * ro...]
    pallas_call x1, Pallas kernels: 260 us -> 241 us  [attention_back(): pl.pallas_call(functools.partial(attention_back_kernel, chunks, head_dim)...]
where the time goes in v7:
time: 712 us; the launch traced here: 711 us
  Pallas kernels  672 us (94%)
  other arithmetic  25.7 us (4%)
  local copies, waits for them, and re-layouts  11.8 us (2%)
    pallas_call x1, Pallas kernels, attention_first(): pl.pallas_call(functools.partial(attention_first_kernel, head_dim, start)...  253 us
    pallas_call x1, Pallas kernels, attention_back(): pl.pallas_call(functools.partial(attention_back_kernel, chunks, head_dim)...  241 us
    pallas_call x1, Pallas kernels, expert_layer(): pl.pallas_call(experts_kernel, out_shape=[jax.ShapeDtypeStruct((8, 2 * ro...  179 us

profile of v7, /device:TPU:0, one launch (start us, length us, event | category | flops | bytes accessed | tf_op | source)
XLA Modules:
  0.0 710.9 jit_solution(6814286411739387852)
XLA Ops:
  0.7 1.3 fusion
  2.5 1.2 pad_maximum_fusion.5
  3.7 0.7 constant_dynamic-slice_fusion.1
  5.8 0.8 fusion.12
  6.5 0.8 fusion.13
  8.0 0.7 pad_maximum_fusion.2.rope_ref
  9.1 1.1 pad_maximum_fusion.w_ref
  10.3 1.3 convert_multiply_fusion.2
  11.6 252.7 %attention_first.1 = (bf16[16,128,2304]{2,1,0:T(8,128)(2,1)}, bf16[16,128,2048]{2,1,0:T(8,128)(2,1)}, f32[16,8,128]{2,1,0:T(8,128)}, bf16[2,2,128,2048]{3,2,1,0:...) custom-call(bf16[2,128,2304]{2,1,0:T(8,128)(2,1)} %pad_maximum_fusio, ...), custom_call_target="tpu_custom_call" | custom-call | tf_op jit(solution)/shard_map/attention_first/pallas_call | solution.py:579
  264.4 1.6 multiply_reduce_fusion.2
  266.5 0.8 slice.63
  267.4 0.9 multiply_convert_fusion.x_ref
  268.3 1.3 copy.41.g_ref
  269.7 178.9 %experts.1 = (bf16[8,256,2048]{2,1,0:T(8,128)(2,1)}, f32[128,2048]{1,0:T(8,128)}, bf16[2048,1536]{1,0:T(8,128)(2,1)}, bf16[2048,768]{1,0:T(8,128)(2,1)}, bf16[16,128,2048]{2,1,0:T(8,128)(2,1)}) custom-call(bf16[128,2048]{1,0:T(8,128)(2,1)} %multiply_convert_fusion.x_ref, bf16[16,128,2048]{2,1,0:T(8,128)(2,1)} %get-tuple-element.36.c_ref, ...), custom_call_target="tpu_custom_call" | custom-call | tf_op jit(solution)/shard_map/experts/pallas_call | solution.py:1249
  448.7 2.0 multiply_reduce_fusion
  451.3 2.6 fusion.9
  453.9 240.8 %attention_back.1 = (f32[128,2048]{1,0:T(8,128)}, f32[128,2048]{1,0:T(8,128)}, bf16[2,128,2304]{2,1,0:T(8,128)(2,1)}, f32[40,128]{1,0:T(8,128)}, bf16[16,128,384...) custom-call(bf16[128,2048]{1,0:T(8,128)(2,1)} %get-tuple-element.98.ga_ref, ...), custom_call_target="tpu_custom_call" | custom-call | tf_op jit(solution)/shard_map/attention_back/pallas_call | solution.py:934
  694.7 2.6 add_convert_fusion
  697.6 1.3 fusion.4
  700.5 1.3 copy.42
  703.2 1.0 pad_maximum_fusion.1
  704.2 2.0 convert_element_type.41
  706.2 2.0 convert_element_type.42
  708.5 2.4 copy.43
  (73 shorter events, 7.7 us)
Async XLA Ops:
  0.6 8.1 %copy-start.11 = (bf16[2048,128]{1,0:T(8,128)(2,1)S(1)}, bf16[2048,128]{1,0:T(8,128)(2,1)}, u32[]{:S(2)}) copy-start(bf16[2048,128]{1,0:T(8,128)(2,1)} %param.22) | copy-start | bytes 1572868
  2.5 7.8 %copy-start.20 = (f32[128]{0:T(128)}, f32[128]{0:T(128)S(1)}, u32[]{:S(2)}) copy-start(f32[128]{0:T(128)S(1)} %get-tuple-element.125) | copy-start | bytes 1540
  7.8 1.1 copy-start.12
  9.1 1.1 copy-start.2
  9.1 1.1 copy-start.15
  264.3 3.0 copy-start.13
  265.9 1.4 copy-start
  266.5 0.9 copy-start.18
  448.6 2.6 copy-start.1
  448.6 2.6 copy-start.5
  448.6 2.6 copy-start.14
  448.6 2.6 copy-start.19
  448.6 2.6 copy-start.23
  694.7 2.7 copy-start.3
  694.7 2.7 copy-start.6
  694.7 2.7 copy-start.16
  694.7 2.9 copy-start.4
  694.7 2.9 copy-start.21
  694.7 2.9 copy-start.22
  697.6 1.3 copy-start.17
  697.6 2.4 copy-start.10
  701.8 2.4 copy-start.9
  704.2 2.0 copy-start.8
  706.2 2.0 copy-start.7

commit v8 on v7

--- a/solution.py
+++ b/solution.py
@@ -216,6 +216,13 @@
         pl.semaphore_wait(barrier, count)
 
 
+def each_rows(rows, body, start=None, block=16):
+    def go(i, carried):
+        return body(pl.ds(pl.multiple_of(i * block, block), block), carried)
+
+    return lax.fori_loop(0, rows // block, go, 0 if start is None else start)
+
+
 def add_rows(target, terms, rows, block=16):
     def body(i, _):
         at = pl.ds(pl.multiple_of(i * block, block), block)
@@ -333,53 +340,48 @@
 
 def gather_pairs(me, x_ref, out_ref, send_sem, recv_sem):
     mine, other = me.dp, me.dp + me.pair
-
-    def part(src, where, to, slot):
-        return me.copy(src, out_ref.at[where], send_sem.at[slot], recv_sem.at[where], to)
-
-    def relay(where, to, slot):
-        part(out_ref.at[where], where, to, slot).start()
-
-    def arrived(where):
-        part(out_ref.at[where], where, me.dp, 0).wait_recv()
-
-    part(x_ref.at[1 - me.half], mine, other, 0).start()
-    part(x_ref.at[me.half], mine, me.dp + me.far, 1).start()
-    part(x_ref.at[me.half], mine, me.dp + me.db, 2).start()
-    part(x_ref.at[me.half], mine, me.dp + me.da, 3).start()
+    chunks = send_sem.shape[1]
+    rows = x_ref.shape[1] // chunks
+
+    def part(src, where, to, slot, k):
+        at = pl.ds(k * rows, rows)
+        return me.copy(src.at[at], out_ref.at[where, at], send_sem.at[slot, k], recv_sem.at[where, k], to)
+
+    def step(where, *relays):
+        for k in range(chunks):
+            part(out_ref.at[where], where, me.dp, 0, k).wait_recv()
+            for to, slot in relays:
+                part(out_ref.at[where], where, to, slot, k).start()
+
+    far, db, da = me.dp + me.far, me.dp + me.db, me.dp + me.da
+    for k in range(chunks):
+        part(x_ref.at[1 - me.half], mine, other, 0, k).start()
+        part(x_ref.at[me.half], mine, far, 1, k).start()
+        part(x_ref.at[me.half], mine, db, 2, k).start()
+        part(x_ref.at[me.half], mine, da, 3, k).start()
     yield
-    arrived(other)
-    relay(other, me.dp + me.far, 4)
-    relay(other, me.dp + me.db, 5)
-    relay(other, me.dp + me.da, 6)
+    step(other, (far, 4), (db, 5), (da, 6))
     yield
-    arrived(mine + me.da)
-    relay(mine + me.da, me.dp + me.db, 7)
+    step(mine + me.da, (db, 7))
     yield
-    arrived(mine + me.far)
-    relay(mine + me.far, me.dp + me.db, 8)
-    relay(mine + me.far, me.dp + me.da, 9)
+    step(mine + me.far, (db, 8), (da, 9))
     yield
-    arrived(other + me.da)
-    relay(other + me.da, me.dp + me.db, 10)
+    step(other + me.da, (db, 10))
     yield
-    arrived(other + me.far)
-    relay(other + me.far, me.dp + me.db, 11)
-    relay(other + me.far, me.dp + me.da, 12)
+    step(other + me.far, (db, 11), (da, 12))
     yield
-    arrived(mine + me.far + me.da)
-    relay(mine + me.far + me.da, me.dp + me.db, 13)
+    step(mine + me.far + me.da, (db, 13))
     yield
-    arrived(other + me.far + me.da)
-    relay(other + me.far + me.da, me.dp + me.db, 14)
+    step(other + me.far + me.da, (db, 14))
     yield
     for base in (mine, other, mine + me.far, other + me.far):
-        arrived(base + me.db)
+        step(base + me.db)
         yield
-        arrived(base + me.da + me.db)
+        step(base + me.da + me.db)
         yield
     for slot in range(15):
-        part(out_ref.at[mine], mine, me.dp, slot).wait_send()
+        for k in range(chunks):
+            part(out_ref.at[mine], mine, me.dp, slot, k).wait_send()
 
 
 def swap_rows(me, x_ref, out_ref, send_sem, recv_sem):
@@ -448,8 +450,8 @@
 
 def attention_first_kernel(
     head_dim, start,
-    w_ref, c_ref, g_ref, x_ref, rope_ref, gain_ref, gate_ref, up_ref, down_ref,
-    w_out, c_out, g_out, seq, raw, low, mixed, sum_ref, gate_out, up_out, down_out,
+    w_ref, c_ref, g_ref, x_ref, rope_ref, gain_ref, tokens_ref, ffn_ref, gate_ref, up_ref, down_ref,
+    w_out, c_out, g_out, seq, raw, low, mixed, hidden_ref, normed_ref, gate_out, up_out, down_out,
     w, c_own, e_own, part, from_core, from_pair,
     w_send, w_recv, c_send, c_recv, g_send, g_recv, x_send, x_recv, e_send, e_recv, back_send, back_recv, copy_sem,
 ):
@@ -556,7 +558,14 @@
     add_rows(from_core.at[1], (row_block(part, me.half, me.core), from_core.at[1]), rows)
     beside.step()
     over.wait_recv()
-    add_rows(sum_ref, (from_core.at[1], from_pair), rows)
+
+    def close(at, _):
+        hidden = tokens_ref[at, :].astype(jnp.float32) + (from_core[1, at, :].astype(jnp.float32) + from_pair[at, :].astype(jnp.float32))
+        hidden_ref[at, :] = hidden
+        normed_ref[at, :] = (hidden * rms_inverse(hidden) * ffn_ref[...]).astype(normed_ref.dtype)
+        return 0
+
+    each_rows(rows, close)
     beside.finish()
     for end in ends:
         end()
@@ -567,7 +576,7 @@
     over.wait_send()
 
 
-def attention_first(weights, rows, gates, normed, rope, gain, experts, cid, start=14):
+def attention_first(weights, rows, gates, normed, rope, gain, tokens, ffn_gain, experts, cid, start=14):
     hbm, vmem = pl.BlockSpec(memory_space=pl.ANY), pl.BlockSpec(memory_space=pltpu.VMEM)
     dma = pltpu.SemaphoreType.DMA
     dtype = rows.dtype
@@ -587,12 +596,13 @@
             jax.ShapeDtypeStruct((4 * block, q_cols + 2 * head_dim), dtype),
             jax.ShapeDtypeStruct((4 * block, q_cols), dtype),
             jax.ShapeDtypeStruct((block, width), jnp.float32),
+            jax.ShapeDtypeStruct((block, width), dtype),
             jax.ShapeDtypeStruct((16 * depth, hidden), dtype),
             jax.ShapeDtypeStruct((16 * depth, hidden), dtype),
             jax.ShapeDtypeStruct((hidden, 16 * depth), dtype),
         ],
-        in_specs=[hbm, hbm, vmem, vmem, vmem, vmem, hbm, hbm, hbm],
-        out_specs=[hbm, hbm] + [vmem] * 6 + [hbm] * 3,
+        in_specs=[hbm, hbm] + [vmem] * 6 + [hbm] * 3,
+        out_specs=[hbm, hbm] + [vmem] * 7 + [hbm] * 3,
         scratch_shapes=[
             pltpu.VMEM((16,) + weights.shape[1:], dtype),
             pltpu.VMEM((block, width), dtype),
@@ -600,7 +610,7 @@
             pltpu.VMEM((4 * block, width), dtype),
             pltpu.VMEM((2, block, width), dtype),
             pltpu.VMEM((block, width), dtype),
-            dma((15,)), dma((16,)),
+            dma((15, 2)), dma((16, 2)),
             dma((29,)), dma((16,)),
             dma((16,)), dma((16,)),
             dma((3,)), dma((3,)),
@@ -610,7 +620,7 @@
         ],
         compiler_params=pltpu.CompilerParams(collective_id=cid, has_side_effects=True, vmem_limit_bytes=67_043_328),
         name="attention_first",
-    )(weights, rows, gates, normed, rope, gain, *experts)
+    )(weights, rows, gates, normed, rope, gain, tokens, ffn_gain, *experts)
 
 
 def scatter_pairs(me, chunks, share, make, out_ref, from_b, from_a, from_far, send_sem, recv_sem):
@@ -757,16 +767,16 @@
 
 def attention_back_kernel(
     chunks, head_dim,
-    ga_ref, w_ref, seq_ref, raw_ref, low_ref, mixed_ref, rope_ref, gain_ref, unit_ref, x_ref, gu_ref, down_ref, share_ref,
-    one_ref, moe_ref, out_ref, sum_ref, gate_out, up_out, down_out,
-    w, ga, gmix, gproj, part, kept, dk, dv, gains, from_core, from_pair,
+    tokens_ref, grad_ref, hidden_ref, two_ref, norms_ref, w_ref, seq_ref, raw_ref, low_ref, mixed_ref, rope_ref, gain_ref, gu_ref, down_ref, share_ref,
+    output_ref, grad_tokens_ref, query_out, key_out, value_out, back_out, sum_ref, gate_out, up_out, down_out,
+    grad_hidden, out_ref, w, ga, gmix, gproj, part, kept, dk, dv, gains, from_core, from_pair,
     pair_b, pair_a, pair_far, total, own, held,
     from_b, from_a, from_z, b_send, b_recv, a_send, a_recv, z_send, z_recv,
     four_send, four_recv, back_send, back_recv, pair_send, pair_recv, sum_send, sum_recv, core_send, core_recv, e_send, e_recv,
     copy_sem, load_sem,
 ):
     me = Place()
-    rows, width = ga_ref.shape
+    rows, width = tokens_ref.shape
     seq_len = 2 * rows
     q_cols = mixed_ref.shape[1]
     proj_cols = q_cols + 2 * head_dim
@@ -785,12 +795,25 @@
         return ga.at[pl.ds(pl.multiple_of((2 * h + core) * rows, rows), rows)]
 
     mine, theirs = ga_at(me.half, me.core), ga_at(1 - me.half, me.core)
-    across = me.copy(ga_ref, mine, four_send.at[0], four_recv.at[0], me.dp + me.pair)
-    beside = me.copy(ga_ref, mine, four_send.at[1], four_recv.at[1], me.dp, 1 - me.core)
+    attn_gain, ffn_gain = norms_ref[0], norms_ref[1]
+
+    def norm_back(grad, values, gain):
+        inverse = rms_inverse(values)
+        return norm_backward(grad, values, inverse, gain), grad * values * inverse
+
+    def open_rows(at, total):
+        grad, term = norm_back(two_ref[at, :], hidden_ref[at, :], ffn_gain)
+        grad = grad_ref[at, :].astype(jnp.float32) + grad
+        grad_hidden[at, :] = grad
+        mine[at, :] = grad.astype(ga.dtype)
+        return total + term
+
+    ffn_part = jnp.sum(each_rows(rows, open_rows, jnp.zeros((16, width), jnp.float32)), axis=0, keepdims=True)
+    across = me.copy(mine, mine, four_send.at[0], four_recv.at[0], me.dp + me.pair)
+    beside = me.copy(mine, mine, four_send.at[1], four_recv.at[1], me.dp, 1 - me.core)
     relay = me.copy(theirs, theirs, four_send.at[2], four_recv.at[2], me.dp, 1 - me.core)
     across.start()
     beside.start()
-    mine[...] = ga_ref[...]
     scatter = ScatterRows(
         me, lambda n: share_ref.at[n, pl.ds(rows, rows)], lambda n: kept.at[n], from_b, from_a, from_z,
         (b_send, b_recv, a_send, a_recv, z_send, z_recv),
@@ -906,23 +929,41 @@
     scatter.second(0)
     next(pairs)
     over.wait_recv()
-    add_rows(one_ref, (from_core.at[1], from_pair), rows)
-    sum_ref[...] = x_ref[...]
-    attn = jnp.sum(one_ref[...] * unit_ref[...], axis=0, keepdims=True)
+
+    def close_rows(at, total):
+        grad = from_core[1, at, :].astype(jnp.float32) + from_pair[at, :].astype(jnp.float32)
+        back_part, term = norm_back(grad, tokens_ref[at, :].astype(jnp.float32), attn_gain)
+        grad_tokens_ref[at, :] = (grad_hidden[at, :] + back_part).astype(grad_tokens_ref.dtype)
+        return total + term
+
+    attn_part = jnp.sum(each_rows(rows, close_rows, jnp.zeros((16, width), jnp.float32)), axis=0, keepdims=True)
+    sum_ref[...] = jnp.zeros_like(sum_ref)
     for j in range(width // 128):
-        sum_ref[pl.ds(j, 1), :] = attn[:, j * 128 : (j + 1) * 128]
+        sum_ref[pl.ds(j, 1), :] = attn_part[:, j * 128 : (j + 1) * 128]
+        sum_ref[pl.ds(width // 128 + j, 1), :] = ffn_part[:, j * 128 : (j + 1) * 128]
     for j in range(2):
         sum_ref[pl.ds(2 * width // 128 + j, 1), :] = gains[j]
-    scatter.finish(moe_ref)
+    scatter.finish(output_ref, hidden_ref)
     run(pairs, experts, sum_all(me, sum_ref, total, sum_send, sum_recv))
+
+    def widen_rows(at, _):
+        start = 0
+        for target in (query_out, key_out, value_out, back_out):
+            size = target.shape[1] // 2
+            for h in range(2):
+                target[at, h * size : (h + 1) * size] = out_ref[h, at, start : start + size].astype(jnp.float32)
+            start += size
+        return 0
+
+    each_rows(rows, widen_rows)
     scatter.drain()
     give(0, 0).wait_send()
     give(0, 1).wait_send()
     over.wait_send()
 
 
-def attention_back(grad_attn, weights, seq_normed, raw, low, mixed, rope, gain, unit, sums, gu, down, share, cid, chunks=2):
-    rows, width = grad_attn.shape
+def attention_back(tokens, cotangent, hidden, grad_two, norms, weights, seq_normed, raw, low, mixed, rope, gain, gu, down, share, cid, chunks=4):
+    rows, width = tokens.shape
     head_dim = rope.shape[-1]
     columns = weights.shape[1]
     half = down.shape[1] // 2
@@ -930,14 +971,19 @@
     dma = pltpu.SemaphoreType.DMA
     dtype = weights.dtype
     proj_cols = raw.shape[1] + head_dim
-    whole = jax.ShapeDtypeStruct((rows, width), jnp.float32)
+    q_cols = mixed.shape[1]
+    whole = jax.ShapeDtypeStruct((rows, width), dtype)
+    grads = [jax.ShapeDtypeStruct((rows, 2 * size), jnp.float32) for size in (q_cols, head_dim, head_dim, q_cols)]
+    sums = jax.ShapeDtypeStruct((-(-(2 * width + 2 * head_dim) // 1024) * 8, 128), jnp.float32)
     return pl.pallas_call(
         functools.partial(attention_back_kernel, chunks, head_dim),
-        out_shape=[whole, whole, jax.ShapeDtypeStruct((2, rows, columns), dtype), jax.ShapeDtypeStruct(sums.shape, sums.dtype)]
+        out_shape=[whole, whole, *grads, sums]
         + [jax.ShapeDtypeStruct((16, rows, half), dtype)] * 3,
-        in_specs=[vmem, hbm] + [vmem] * 8 + [hbm] * 3,
-        out_specs=[vmem] * 4 + [hbm] * 3,
+        in_specs=[vmem] * 5 + [hbm] + [vmem] * 6 + [hbm] * 3,
+        out_specs=[vmem] * 7 + [hbm] * 3,
         scratch_shapes=[
+            pltpu.VMEM((rows, width), jnp.float32),
+            pltpu.VMEM((2, rows, columns), dtype),
             pltpu.VMEM(weights.shape, dtype),
             pltpu.VMEM((4 * rows, width), dtype),
             pltpu.VMEM(mixed.shape, dtype),
@@ -966,7 +1012,7 @@
         ],
         compiler_params=pltpu.CompilerParams(collective_id=cid, has_side_effects=True, vmem_limit_bytes=67_043_328),
         name="attention_back",
-    )(grad_attn, weights, seq_normed, raw, low, mixed, rope, gain, unit, sums, gu, down, share)
+    )(tokens, cotangent, hidden, grad_two, norms, weights, seq_normed, raw, low, mixed, rope, gain, gu, down, share)
 
 
 class ScatterRows:
@@ -1007,12 +1053,12 @@
             due = jnp.logical_and((now - 1 - lag) % 2 == 0, jnp.logical_and(now > lag, m < 4))
             pl.when(due)(lambda: call(m))
 
-    def finish(self, out_ref):
+    def finish(self, out_ref, *more):
         me = self.me
         others = [(me.z + r) % 4 for r in range(1, 4)]
         for z in others:
             me.copy(self.from_z.at[z], self.from_z.at[z], self.z_send.at[0], self.z_recv.at[z], me.dp).wait_recv()
-        add_rows(out_ref, (self.from_b.at[0],) + tuple(self.from_z.at[z] for z in others), self.rows)
+        add_rows(out_ref, (self.from_b.at[0],) + tuple(self.from_z.at[z] for z in others) + more, self.rows)
 
     def drain(self):
         for m in range(4):
@@ -1558,29 +1604,19 @@
     cosine, sine_table = rotary_tables(2 * rows, head_dim)
     rope = jnp.stack([jnp.concatenate([v, w], axis=1) for v, w in ((cosine[:, 0], cosine[:, 0]), (sine_table[:, 0], -sine_table[:, 0]))])
     gain = jnp.stack([query_gain, key_gain])[:, None]
-    weights, rows_grad, gates, seq_normed, raw, lows, mixed, attended, *projections = attention_first(
-        halves, cotangent, gates, normed_one, rope, gain, (w_gate, w_up, w_down), 1
+    weights, rows_grad, gates, seq_normed, raw, lows, mixed, hidden, normed_two, *projections = attention_first(
+        halves, cotangent, gates, normed_one, rope, gain, tokens, ffn_gain[None], (w_gate, w_up, w_down), 1
     )
     weights, gates, seq_normed = weights.reshape(-1, weights.shape[2]), gates[:, 0][:, :, None], seq_normed.reshape(-1, width)
     proj_cols = q_cols + 2 * kv_cols
-    hidden = residual + attended
-    inverse_two = rms_inverse(hidden)
-    normed_two = (hidden * inverse_two * ffn_gain).astype(low)
     share, grad_two, gu_part, down_part, _ = expert_layer(normed_two, rows_grad, gates, *projections, 2)
-    ffn_gain_part = jnp.sum(grad_two * hidden * inverse_two, axis=0)
-    grad_hidden = cotangent.astype(jnp.float32) + norm_backward(grad_two, hidden, inverse_two, ffn_gain)
-    gains = jnp.pad(ffn_gain_part, (width, 1024)).reshape(-1, 128)
-    grad_one, moe, shares, totals, *grads_moe = attention_back(
-        grad_hidden.astype(low), weights, seq_normed, raw, lows, mixed, rope, gain, residual * inverse_one, gains, gu_part, down_part, share, 9
-    )
-    output = (hidden + moe).astype(low)
-    grad_w_gate, grad_w_up, grad_w_down = [v.astype(jnp.float32) for v in grads_moe]
+    norms = jnp.stack([attn_gain, ffn_gain])[:, None]
+    output, grad_tokens, *grads, totals, grad_gate, grad_up, grad_down = attention_back(
+        tokens, cotangent, hidden, grad_two, norms, weights, seq_normed, raw, lows, mixed, rope, gain, gu_part, down_part, share, 9
+    )
+    grad_w_gate, grad_w_up, grad_w_down = [v.astype(jnp.float32) for v in (grad_gate, grad_up, grad_down)]
     grad_w_down = jnp.transpose(grad_w_down, (0, 2, 1))
-    shares, totals = shares.astype(jnp.float32), totals.reshape(-1)
-    stops = (0, q_cols, q_cols + kv_cols, proj_cols, proj_cols + q_cols)
-    grads = [jnp.concatenate([shares[0, :, a:b], shares[1, :, a:b]], axis=1) for a, b in zip(stops, stops[1:])]
-    grad_tokens = (grad_hidden + norm_backward(grad_one, residual, inverse_one, attn_gain)).astype(low)
-    totals = jnp.split(totals, (width, 2 * width, 2 * width + head_dim, 2 * width + 2 * head_dim))[:4]
+    totals = jnp.split(totals.reshape(-1), (width, 2 * width, 2 * width + head_dim, 2 * width + 2 * head_dim))[:4]
     return (output, grad_tokens, grads[0], grads[1], grads[2], jnp.transpose(grads[3]), grad_w_gate, grad_w_up, grad_w_down, *totals)
 
 

time: 712 us -> 700 us (0.983)
  other arithmetic: 25.7 us -> 12.3 us
    pallas_call x1, Pallas kernels: 179 us -> 191 us  [expert_layer(): pl.pallas_call(experts_kernel, out_shape=[jax.ShapeDtypeStruct((8, 2 * ro...]
    pallas_call x1, Pallas kernels: 253 us -> 243 us  [attention_first(): pl.pallas_call(functools.partial(attention_first_kernel, head_dim, start)...]
where the time goes in v8:
time: 700 us
  Pallas kernels  673 us (96%)
  local copies, waits for them, and re-layouts  13.6 us (2%)
  other arithmetic  12.3 us (2%)
    pallas_call x1, Pallas kernels, attention_first(): pl.pallas_call(functools.partial(attention_first_kernel, head_dim, start)...  243 us
    pallas_call x1, Pallas kernels, attention_back(): pl.pallas_call(functools.partial(attention_back_kernel, chunks, head_dim)...  240 us
    pallas_call x1, Pallas kernels, expert_layer(): pl.pallas_call(experts_kernel, out_shape=[jax.ShapeDtypeStruct((8, 2 * ro...  191 us

profile of v8, /device:TPU:0, one launch (start us, length us, event | category | flops | bytes accessed | tf_op | source)
XLA Modules:
  0.0 700.0 jit_solution(9509272068398752990)
XLA Ops:
  0.7 1.3 copy.40
  2.3 1.1 pad_maximum_fusion.w_ref
  4.1 0.7 pad_maximum_fusion.1.rope_ref
  4.8 0.6 broadcast_in_dim.38.g_ref
  5.5 0.6 pad_maximum_fusion.3
  6.3 1.0 fusion.2.x_ref
  7.2 243.0 %attention_first.1 = (bf16[16,128,2304]{2,1,0:T(8,128)(2,1)}, bf16[16,128,2048]{2,1,0:T(8,128)(2,1)}, f32[16,8,128]{2,1,0:T(8,128)}, bf16[2,2,128,2048]{3,2,1,0:...) custom-call(bf16[2,128,2304]{2,1,0:T(8,128)(2,1)} %pad_maximum_fusio, ...), custom_call_target="tpu_custom_call" | custom-call | tf_op jit(solution)/shard_map/attention_first/pallas_call | solution.py:588
  250.3 0.8 slice.39
  251.1 1.3 copy.41.g_ref
  252.5 190.6 %experts.1 = (bf16[8,256,2048]{2,1,0:T(8,128)(2,1)}, f32[128,2048]{1,0:T(8,128)}, bf16[2048,1536]{1,0:T(8,128)(2,1)}, bf16[2048,768]{1,0:T(8,128)(2,1)}, bf16[16,128,2048]{2,1,0:T(8,128)(2,1)}) custom-call(bf16[128,2048]{1,0:T(8,128)(2,1)} %get-tuple-element.40.x_ref, bf16[16,128,2048]{2,1,0:T(8,128)(2,1)} %get-tuple-element.41.c_ref, ...), custom_call_target="tpu_custom_call" | custom-call | tf_op jit(solution)/shard_map/experts/pallas_call | solution.py:1295
  443.0 0.7 pad_maximum_fusion.2
  443.8 0.6 broadcast_in_dim.42.norms_ref
  444.4 239.6 %attention_back.1 = (bf16[128,2048]{1,0:T(8,128)(2,1)}, bf16[128,2048]{1,0:T(8,128)(2,1)}, f32[128,2048]{1,0:T(8,128)}, f32[128,256]{1,0:T(8,128)}, f32[128,256]...) custom-call(bf16[128,2048]{1,0:T(8,128)(2,1)} %tokens_ref.3, ...), custom_call_target="tpu_custom_call" | custom-call | tf_op jit(solution)/shard_map/attention_back/pallas_call | solution.py:978
  684.0 1.7 convert_bitcast_fusion
  685.8 2.4 copy.43
  688.2 3.5 convert_element_type.15
  691.7 2.0 convert_element_type.16
  693.7 1.3 copy.42
  695.0 0.6 slice_bitcast_fusion
  696.1 0.8 copy.49
  696.9 0.8 copy.50
  697.7 1.0 copy.51
  698.7 0.7 copy.52
  699.4 0.7 copy.53
  (48 shorter events, 1.6 us)
Async XLA Ops:
  0.6 1.4 copy-start.4
  0.7 1.4 copy-start.9
  0.7 1.4 copy-start.10
  2.2 2.6 copy-start.13
  2.2 2.6 copy-start.14
  2.3 3.2 copy-start.15
  2.3 3.2 copy-start.16
  2.3 3.8 copy-start
  3.4 2.8 copy-start.11
  688.2 3.5 copy-start.1
  691.7 2.0 copy-start.3
  693.7 1.3 copy-start.12
  693.7 2.4 copy-start.6
  693.7 3.2 copy-start.5
  695.0 2.7 copy-start.2
  696.9 1.8 copy-start.8
  696.9 2.4 copy-start.7
